TPU v7x, 32 devices: a whole 2x2x4 slice. The times are simulated.
32 devices in a mesh: member: 4 (over y, x), tile: 8 (over z, core).
Axes of the slice: x: 2, y: 2, z: 4, core: 2. Of those that a mesh axis runs over, the one named last changes fastest.
Arguments:
- northward_speed_field: float32 [16, 16, 64, 256], P('member', None, 'tile'), may hold values from -6 to 6
- level_depth_extent: float32 [16, 16, 64, 256], P('member', None, 'tile'), may hold values from 0.2 to 5
- potential_warmth_anomaly: float32 [16, 16, 64, 256], P('member', None, 'tile'), may hold values from -6 to 6
- ocean_region_label: int32 [64, 256], P('tile'), may hold values from 0 to 9
- zone_for_parallel: int32 [256], replicated, may hold values from 0 to 15, never falling along the last dimension, each value on 1 to 32 neighbouring positions
Outputs:
- mean_psi: float32 [10, 16, 256], P(None, None, ('member', 'tile'))
- mean_heat: float32 [10, 256], P(None, ('member', 'tile'))
- covariance: float32 [16, 16, 16], replicated
Inputs may be any that keep to these rules, and one draw needn't show every extreme that they name: `zone_for_parallel`: never falls along latitude; every band holds 1 to 32 latitudes.
All inputs are finite; a program needn't handle non-finite values.
Results may differ from a plain program's by a relative error of at most 0.00011.
Values sent between devices are 32-bit elements; how exact they have to be, the bound alone decides.
No kernel may reach another device: no remote copies, remote signals or barrier semaphores. Data moves between devices by JAX's collectives and lax.ppermute only.
A program may use at most 128 MiB of HBM per device.

v0:
```python
import math

import jax
import jax.numpy as jnp
from jax import lax
from jax.sharding import PartitionSpec as P

BASINS = 10
NBANDS = 16


def metric_factor(lats):
    index = jnp.arange(lats, dtype=jnp.float32)
    return jnp.cos((-80.0 + 160.0 * (index + 0.5) / lats) * (math.pi / 180.0))


def local(
    northward_speed_field,
    level_depth_extent,
    potential_warmth_anomaly,
    ocean_region_label,
    zone_for_parallel,
):
    greatest_bound_value = lax.Precision.HIGHEST
    members_here, layers, columns, lats = northward_speed_field.shape
    tiles = lax.axis_size("tile")
    groups = lax.axis_size("member")
    owned = lats // (groups * tiles)
    northward_volume_carriage = northward_speed_field * level_depth_extent * metric_factor(lats)
    region_indicator_matrix = (
        ocean_region_label[None, :, :] == jnp.arange(BASINS, dtype=jnp.int32)[:, None, None]
    ).astype(jnp.float32)
    transport = jnp.einsum(
        "mkxl,bxl->mbkl",
        northward_volume_carriage,
        region_indicator_matrix,
        precision=greatest_bound_value,
    ) / math.sqrt(columns * tiles)
    thermal_energy_integral = jnp.einsum(
        "tzux,pux->tpx",
        northward_volume_carriage * potential_warmth_anomaly,
        region_indicator_matrix,
        precision=greatest_bound_value,
    ) / math.sqrt(columns * tiles * layers)
    partial_value = jnp.concatenate(
        [transport.reshape(members_here, BASINS * layers, lats), thermal_energy_integral], axis=1
    )
    regrouped = lax.all_to_all(partial_value, "member", split_axis=2, concat_axis=0, tiled=True)
    summed = lax.psum_scatter(regrouped, "tile", scatter_dimension=2, tiled=True)
    members = summed.shape[0]
    streams = jnp.cumsum(
        summed[:, : BASINS * layers].reshape(members, BASINS, layers, owned), axis=2
    )
    heat_all = summed[:, BASINS * layers :]
    mean_psi = jnp.mean(streams, axis=0)
    mean_heat = jnp.mean(heat_all, axis=0)
    anomaly = (streams - mean_psi).reshape(members, BASINS * layers, owned)
    start = (lax.axis_index("member") * tiles + lax.axis_index("tile")) * owned
    bands_here = lax.dynamic_slice_in_dim(zone_for_parallel, start, owned)
    band_hot = (bands_here[:, None] == jnp.arange(NBANDS, dtype=jnp.int32)[None, :]).astype(
        jnp.float32
    )
    products = jnp.einsum("mfl,nfl->lmn", anomaly, anomaly, precision=greatest_bound_value)
    norm = float((members - 1) * BASINS * layers * (lats // NBANDS))
    local_cov = jnp.einsum("lmn,lc->cmn", products, band_hot, precision=greatest_bound_value) / norm
    covariance = lax.psum(local_cov, ("member", "tile"))
    return (mean_psi, mean_heat, covariance)


def solution(mesh):
    in_specs = (
        P("member", None, "tile", None),
        P("member", None, "tile", None),
        P("member", None, "tile", None),
        P("tile", None),
        P(),
    )
    out_specs = (P(None, None, ("member", "tile")), P(None, ("member", "tile")), P())
    return jax.shard_map(local, mesh=mesh, in_specs=in_specs, out_specs=out_specs, check_vma=False)
```

profile of v0, /device:TPU:0, one launch (start us, length us, event | category | flops | bytes accessed | tf_op | source)
XLA Modules:
  0.0 138.6 jit_solution(16982006335386744213)
XLA Ops:
  7.2 0.0 copy-start.1
  7.2 0.0 reduce-scatter.2.cloned.1.call-start
  7.3 1.5 %multiply_reduce_fusion = (f32[4,8,256]{2,1,0:T(8,128)S(1)}, f32[4,16,8,256]{3,2,1,0:T(8,128)S(1)}) fusion(f32[4,16,8,256]{3,2,1,0:T(8,128)} %param.7, f32[256]{0:T(256)S(1)} %multiply_cosine_fusion, f32[4,16,8,256]{3,2,1,0:T(8,128)} %param.5, f32[4,16,8,256]{3,2,1,0:T(8,128)} %param.6), kind=kLoop, calls=%fused_computation.7 | loop fusion | flops 516096 | bytes 2130944 | tf_op jit(solution)/shard_map/tzux,pux->tpx/reduce_sum | solution.py:39
  8.7 4.4 %copy.34 = f32[4,16,8,256]{1,2,0,3:T(8,128)} copy(f32[4,16,8,256]{3,2,1,0:T(8,128)S(1)} %get-tuple-element.16) | data formatting | bytes 1048576 | tf_op jit(solution)/shard_map/mul | solution.py:29
  13.1 0.0 copy-done.1
  13.1 0.1 copy.33
  13.2 9.7 %multiply_bitcast_fusion = f32[4,10,16,256]{2,1,0,3:T(8,128)} fusion(f32[4,16,8,256]{1,2,0,3:T(8,128)} %copy.34, s32[8,256]{0,1:T(8,128)S(1)} %copy.33), kind=kOutput, calls=%fused_computation | convolution fusion | flops 15912960 | bytes 1187840 | tf_op jit(solution)/shard_map/mkxl,bxl->mbkl/dot_general | solution.py:33
  22.9 5.3 %copy.35 = f32[4,10,16,256]{3,2,1,0:T(8,128)S(1)} copy(f32[4,10,16,256]{2,1,0,3:T(8,128)} %multiply_bitcast_fusion) | data formatting | bytes 1310720 | tf_op jit(solution)/shard_map/div | solution.py:33
  28.2 0.2 copy.36
  28.4 1.1 fusion
  29.5 0.2 copy.37
  29.7 0.1 pad_maximum_fusion
  29.8 0.0 copy-start.2
  29.8 0.4 copy.38
  30.2 19.1 %all_to_all.18 = f32[4,170,256]{1,0,2:T(4,128)S(1)} all-to-all(f32[4,170,256]{1,0,2:T(4,128)S(1)} %copy.38), channel_id=1, replica_groups=mesh['member'=4,'tile'=8] {'member'}, dimensions={2} | all-to-all | bytes 1392640 | tf_op jit(solution)/shard_map/all_to_all | solution.py:48
  49.3 0.2 copy.39
  49.5 1.1 copy.40
  50.6 0.0 reduce-scatter.2.cloned.1.call-update
  50.6 0.0 copy-done.2
  50.6 0.1 dynamic_slice.3
  50.7 32.4 %reduce-scatter.2.cloned.1.call-done = f32[16,170,8]{1,2,0:T(8,128)} async-done(((f32[16,170,64]{1,2,0:T(8,128)}), f32[16,170,8]{1,2,0:T(8,128)}) %reduce-scatter.2.cloned.1.call-update) | async-done | bytes 87056 | tf_op jit(solution)/shard_map/reduce_scatter | solution.py:49
  83.1 1.2 reshape.33
  84.3 2.3 %copy.41 = f32[16,10,16,8]{3,1,2,0:T(8,128)} copy(f32[16,10,16,8]{2,1,3,0:T(8,128)S(1)} %reshape.33) | data formatting | bytes 163840 | tf_op jit(solution)/shard_map/reshape | solution.py:52
  86.6 1.8 %fusion.11 = f32[16,10,16,8]{3,1,2,0:T(8,128)S(1)} fusion(f32[16,10,16,8]{3,1,2,0:T(8,128)} %copy.41), kind=kOutput, calls=%fused_computation.22 | output fusion | flops 307200 | bytes 163840 | tf_op jit(solution)/shard_map/jit(cumsum)/reduce_window_sum | solution.py:51
  88.4 0.0 copy-start
  88.4 1.1 copy.42
  89.5 0.2 reduce_sum.28
  89.7 0.1 copy.43
  89.8 0.7 copy.47
  90.5 0.1 div.54
  90.6 0.3 reduce_window_sum.14
  90.9 0.3 fusion.5
  91.2 0.3 convolution_multiply_fusion.1
  91.5 38.9 %psum.7 = f32[16,16,16]{2,0,1:T(8,128)S(1)} all-reduce(f32[16,16,16]{2,0,1:T(8,128)S(1)} %convolution_multiply_fusion.1), channel_id=1, replica_groups=mesh['member'=4,'tile'=8] {'member','tile'}, use_global_device_ids=true, to_apply=%region_5.6 | all-reduce | flops 4096 | bytes 32768 | tf_op jit(solution)/shard_map/psum | solution.py:66
  130.4 0.7 copy.48
  131.1 0.0 copy-done
  131.1 0.1 slice_reduce_fusion
  131.2 0.6 broadcast_multiply_fusion.1
  (3 shorter events, 0.1 us)
Async XLA Ops:
  7.2 5.9 %copy-start.1 = (s32[8,256]{1,0:T(8,128)S(1)}, s32[8,256]{1,0:T(8,128)}, u32[]{:S(2)}) copy-start(s32[8,256]{1,0:T(8,128)} %param.8) | copy-start | bytes 24580
  7.2 75.9 %reduce-scatter.2.cloned.1.call-start = ((), (), s32[]{:S(2)}) async-start(), calls=%async_computation.2 | async-start | bytes 1179648 | tf_op jit(solution)/shard_map/reduce_scatter | solution.py:49
  29.8 20.9 %copy-start.2 = (s32[256]{0:T(256)S(1)}, s32[256]{0:T(256)}, u32[]{:S(2)}) copy-start(s32[256]{0:T(256)} %param.9) | copy-start | bytes 3076
  88.4 42.7 %copy-start = (f32[16,170,8]{1,2,0:T(8,128)S(1)}, f32[16,170,8]{1,2,0:T(8,128)}, u32[]{:S(2)}) copy-start(f32[16,170,8]{1,2,0:T(8,128)} %reduce-scatter.2.cloned.1.call-done) | copy-start | bytes 261124
Sparse Core Ops, SparseCore 0:
  50.7 32.3 reduce-scatter.1
where the time goes:
time: 140 us; the launch traced here: 139 us
  blocking collectives  58 us (41%)
  waiting for transfers between devices  32.4 us (23%)
  local copies, waits for them, and re-layouts  18.4 us (13%)
  between operations  14.2 us (10%)
  matrix products  11.3 us (8%)
  other arithmetic  4.26 us (3%)
    psum x1, blocking collectives, local(): covariance = lax.psum(local_cov, ('member', 'tile'))  38.9 us
    reduce_scatter x1, waiting for transfers between devices, local(): lax.psum_scatter(regrouped, 'tile', scatter_dimension=2, tiled=True)  32.4 us
    all_to_all x1, blocking collectives, local(): lax.all_to_all(partial_value, 'member', split_axis=2, concat_axis=0, tile...  19.1 us
    dot_general x1, matrix products, local(): jnp.einsum('mkxl,bxl->mbkl', northward_volume_carriage, region_indicator_...  9.66 us
    div x1, local copies, waits for them, and re-layouts, local(): jnp.einsum('mkxl,bxl->mbkl', northward_volume_carriage, region_indicator_...  5.26 us
    mul x1, local copies, waits for them, and re-layouts, local(): northward_speed_field * level_depth_extent * metric_factor(lats)  4.36 us
    reshape x2, local copies, waits for them, and re-layouts, local(): summed[:, :BASINS * layers].reshape(members, BASINS, layers, owned)  3.48 us
  transfers between devices with their start and end apart: 1, of which 1 were waited for; matrix products, arithmetic and copies ran while one was open for 0% of the time, Pallas kernels for 0%

commit v1 on v0

v1 whole, which is shorter than its diff:
```python
import functools
import math

import jax
import jax.numpy as jnp
from jax import lax
from jax.experimental import pallas as pl
from jax.experimental.pallas import tpu as pltpu
from jax.sharding import PartitionSpec as P

BASINS = 10
NBANDS = 16
LANES = 128
SUB = 8
HEAT_LANES = 16
HIGHEST = lax.Precision.HIGHEST


def metric_factor(lats):
    index = jnp.arange(lats, dtype=jnp.float32)
    return jnp.cos((-80.0 + 160.0 * (index + 0.5) / lats) * (math.pi / 180.0))


def iota(shape, dim):
    return lax.broadcasted_iota(jnp.int32, shape, dim)


def log2(n):
    assert n & (n - 1) == 0
    return n.bit_length() - 1


def split_features(layers, members_here):
    feats = BASINS * layers
    rest = feats - LANES
    assert 0 < rest and rest * members_here == LANES and LANES % layers == 0
    return feats, rest


def partial_kernel(v_ref, h_ref, w_ref, region_ref, spacing_ref, keep_ref, send_ref, heat_ref,
                   *, members_here, layers, columns, groups, tiles):
    feats, rest = split_features(layers, members_here)
    core = lax.axis_index("tile") % 2
    lb = pl.program_id(0)
    halves = layers // SUB
    lshift = log2(layers)
    slots = members_here + 1
    pieces = LANES // SUB
    rows = iota((feats, 2 * LANES), 0)
    cols = iota((feats, 2 * LANES), 1)

    def running(m):
        feature = jnp.where(cols < LANES, cols, cols - m * rest)
        valid = (cols < LANES) | ((feature >= LANES) & (feature < feats))
        same = (rows >> lshift) == (feature >> lshift)
        return jnp.where(valid & same & (rows <= feature), 1.0, 0.0)

    hrows = iota((BASINS * SUB, LANES), 0)
    hcols = iota((BASINS * SUB, LANES), 1)
    heat_table = jnp.where((hrows >> log2(SUB)) == (hcols & (HEAT_LANES - 1)), 1.0, 0.0)
    heat_lane = iota((SUB, LANES), 1) >> log2(HEAT_LANES)

    def put(place, slot, even, odd):
        keep_ref[place, slot] = jnp.where(core == 0, even, odd)
        send_ref[place, slot] = jnp.where(core == 0, odd, even)

    @pl.when(lb == 0)
    def _():
        heat_ref[...] = jnp.zeros_like(heat_ref)

    dims = (((0,), (0,)), ((), ()))
    spacing = spacing_ref[...]
    region = [jnp.broadcast_to(region_ref[x : x + 1, :], (SUB, LANES)) for x in range(columns)]
    warm = [None] * columns
    extra = None
    packed = []
    for m in range(members_here):
        acc = [[None] * halves for _ in range(BASINS)]
        for x in range(columns):
            flux = []
            for k in range(halves):
                at = pl.ds(((m * layers) + k * SUB) * columns + x, SUB, stride=columns)
                one = v_ref[at, :] * h_ref[at, :] * spacing
                heat = one * w_ref[at, :]
                warm[x] = heat if warm[x] is None else warm[x] + heat
                flux.append(one)
            for b in range(BASINS):
                hit = region[x] == b
                for k in range(halves):
                    part = jnp.where(hit, flux[k], 0.0)
                    acc[b][k] = part if acc[b][k] is None else acc[b][k] + part
        stacked = jnp.concatenate([acc[b][k] for b in range(BASINS) for k in range(halves)], 0)
        stream = lax.dot_general(
            stacked, running(m), dims, precision=HIGHEST, preferred_element_type=jnp.float32
        )
        packed.append(stream[:, :LANES])
        extra = stream[:, LANES:] if extra is None else extra + stream[:, LANES:]
    packed.append(extra)
    basin_heat = []
    for b in range(BASINS):
        total = None
        for x in range(columns):
            part = jnp.where(region[x] == b, warm[x], 0.0)
            total = part if total is None else total + part
        basin_heat.append(total)
    heat = lax.dot_general(
        jnp.concatenate(basin_heat, 0), heat_table, dims,
        precision=HIGHEST, preferred_element_type=jnp.float32,
    )
    for row in range(0, pieces, 2):
        tile = row % tiles
        group = lb * (pieces // tiles) + row // tiles
        even = slice(row * SUB, (row + 1) * SUB)
        odd = slice((row + 1) * SUB, (row + 2) * SUB)
        for s in range(slots):
            put(tile // 2, group * slots + s, packed[s][even], packed[s][odd])
        heat_ref[tile] += jnp.where(heat_lane == group, heat[even], 0.0)
        heat_ref[tile + 1] += jnp.where(heat_lane == group, heat[odd], 0.0)

    @pl.when(lb == pl.num_programs(0) - 1)
    def _():
        for tile in range(0, tiles, 2):
            put(tile // 2, groups * slots, heat_ref[tile], heat_ref[tile + 1])


def gather_kernel(*refs, members_here, layers, groups, tiles):
    zone_ref = refs[0]
    parts = refs[1 : 1 + groups]
    psi_ref, heat_ref, cov_ref, all_ref, mean_ref = refs[1 + groups :]
    feats, rest = split_features(layers, members_here)
    slots = members_here + 1
    members = members_here * groups
    mine = lax.axis_index("member")
    tile = lax.axis_index("tile")
    for r in range(groups):
        all_ref[mine ^ r] = parts[r][...]
    wide = members * SUB
    lane = iota((SUB, LANES), 1)
    sshift, jmask = log2(SUB), SUB - 1
    same_lat = (iota((wide, wide), 0) & jmask) == (iota((wide, wide), 1) & jmask)
    pick = jnp.where(iota((members, wide), 0) == (iota((members, wide), 1) >> sshift), 1.0, 0.0)
    qrow = iota((NBANDS * members, wide), 0)
    qcol = iota((NBANDS * members, wide), 1)
    same_member = (qrow & (members - 1)) == (qcol >> sshift)
    qband = qrow >> log2(members)
    lat_lane = iota((1, wide), 1) & jmask
    last = (((1,), (1,)), ((), ()))
    dot = functools.partial(
        lax.dot_general, precision=HIGHEST, preferred_element_type=jnp.float32
    )
    total = None
    for g in range(groups):
        heads, tails = [], []
        for q in range(groups):
            tail = all_ref[q, g * slots + members_here]
            for m in range(members_here):
                heads.append(all_ref[q, g * slots + m])
                moved = tail if m == 0 else pltpu.roll(tail, LANES - m * rest, 1)
                tails.append(jnp.where(lane < rest, moved, 0.0))
        head_mean = sum(heads) * (1.0 / members)
        tail_mean = sum(tails) * (1.0 / members)
        mean_ref[g, 0] = head_mean
        mean_ref[g, 1] = tail_mean
        head = jnp.concatenate([a - head_mean for a in heads], 0)
        tail = jnp.concatenate([a - tail_mean for a in tails], 0)
        gram = dot(head, head, last) + dot(tail, tail, last)
        gram = jnp.where(same_lat, gram, 0.0)
        summed = dot(pick, gram, (((1,), (0,)), ((), ())))
        zone = jnp.zeros((1, wide), jnp.int32)
        for j in range(SUB):
            zone = jnp.where(lat_lane == j, zone_ref[(g * tiles + tile) * SUB + j], zone)
        chosen = jnp.where(same_member & (qband == zone), 1.0, 0.0)
        share = dot(summed, chosen, last)
        total = share if total is None else total + share
    cov_ref[...] = total
    for b in range(BASINS):
        half, at = divmod(b * layers, LANES)
        psi_ref[b] = mean_ref[mine, half][:, at : at + layers]
    warm = sum(all_ref[q, groups * slots] for q in range(groups))
    out = jnp.zeros((SUB, BASINS), jnp.float32)
    for g in range(groups):
        out = jnp.where(mine == g, warm[:, g * HEAT_LANES : g * HEAT_LANES + BASINS], out)
    heat_ref[...] = out * (1.0 / (members * math.sqrt(layers)))


def unpack_kernel(*refs, members, scale):
    out_ref = refs[-1]
    total = refs[0][...]
    for ref in refs[1:-1]:
        total = total + ref[...]
    total = total * scale
    for c in range(NBANDS):
        out_ref[c] = total[:, c * members : (c + 1) * members]


def exchange(value, axis, bit):
    size = lax.axis_size(axis)
    return lax.ppermute(value, axis, [(i, i ^ bit) for i in range(size)])


VMEM = pl.BlockSpec(memory_space=pltpu.MemorySpace.VMEM)
SMEM = pl.BlockSpec(memory_space=pltpu.MemorySpace.SMEM)


def local(
    northward_speed_field,
    level_depth_extent,
    potential_warmth_anomaly,
    ocean_region_label,
    zone_for_parallel,
):
    members_here, layers, columns, lats = northward_speed_field.shape
    tiles = lax.axis_size("tile")
    groups = lax.axis_size("member")
    members = members_here * groups
    slots = groups * (members_here + 1) + 1
    assert lats == groups * tiles * SUB and (LANES // SUB) % tiles == 0 and groups * HEAT_LANES <= LANES
    spacing = (metric_factor(lats) / math.sqrt(columns * tiles)).reshape(1, lats)
    flat = (members_here * layers * columns, lats)
    piece = jax.ShapeDtypeStruct((tiles // 2, slots, SUB, LANES), jnp.float32)
    keep, send = pl.pallas_call(
        functools.partial(
            partial_kernel, members_here=members_here, layers=layers, columns=columns,
            groups=groups, tiles=tiles,
        ),
        out_shape=(piece, piece),
        grid=(lats // LANES,),
        in_specs=[
            pl.BlockSpec((flat[0], LANES), lambda i: (0, i)),
            pl.BlockSpec((flat[0], LANES), lambda i: (0, i)),
            pl.BlockSpec((flat[0], LANES), lambda i: (0, i)),
            pl.BlockSpec((columns, LANES), lambda i: (0, i)),
            pl.BlockSpec((1, LANES), lambda i: (0, i)),
        ],
        out_specs=(
            pl.BlockSpec(piece.shape, lambda i: (0, 0, 0, 0)),
            pl.BlockSpec(piece.shape, lambda i: (0, 0, 0, 0)),
        ),
        scratch_shapes=[pltpu.VMEM((tiles, SUB, LANES), jnp.float32)],
        name="partial",
    )(
        northward_speed_field.reshape(flat),
        level_depth_extent.reshape(flat),
        potential_warmth_anomaly.reshape(flat),
        ocean_region_label,
        spacing,
    )
    tile = lax.axis_index("tile")
    got = exchange(send, "tile", 1)
    bit = 2
    while bit < tiles:
        shape = (keep.shape[0] // 2, 2) + keep.shape[1:]
        keep, got = keep.reshape(shape), got.reshape(shape)
        mine = (tile // bit) % 2
        send = lax.dynamic_index_in_dim(keep, 1 - mine, 1, False) + lax.dynamic_index_in_dim(
            got, 1 - mine, 1, False
        )
        keep = lax.dynamic_index_in_dim(keep, mine, 1, False) + lax.dynamic_index_in_dim(
            got, mine, 1, False
        )
        got = exchange(send, "tile", bit)
        bit *= 2
    owned = (keep + got).reshape(slots, SUB, LANES)
    parts = [owned] + [exchange(owned, "member", r) for r in range(1, groups)]
    psi, heat, share = pl.pallas_call(
        functools.partial(
            gather_kernel, members_here=members_here, layers=layers, groups=groups, tiles=tiles
        ),
        out_shape=(
            jax.ShapeDtypeStruct((BASINS, SUB, layers), jnp.float32),
            jax.ShapeDtypeStruct((SUB, BASINS), jnp.float32),
            jax.ShapeDtypeStruct((members, NBANDS * members), jnp.float32),
        ),
        in_specs=[SMEM] + [VMEM] * groups,
        out_specs=(VMEM, VMEM, VMEM),
        scratch_shapes=[
            pltpu.VMEM((groups, slots, SUB, LANES), jnp.float32),
            pltpu.VMEM((groups, 2, SUB, LANES), jnp.float32),
        ],
        name="gather",
    )(zone_for_parallel, *parts)
    bit = 1
    while 2 * bit < tiles:
        share = share + exchange(share, "tile", bit)
        bit *= 2
    norm = float((members - 1) * BASINS * layers * (lats // NBANDS))
    covariance = pl.pallas_call(
        functools.partial(unpack_kernel, members=members, scale=1.0 / norm),
        out_shape=jax.ShapeDtypeStruct((NBANDS, members, members), jnp.float32),
        in_specs=[VMEM] * 2,
        out_specs=VMEM,
        name="unpack",
    )(share, exchange(share, "tile", bit))
    return (jnp.transpose(psi, (0, 2, 1)), jnp.transpose(heat, (1, 0)), covariance)


def solution(mesh):
    in_specs = (
        P("member", None, "tile", None),
        P("member", None, "tile", None),
        P("member", None, "tile", None),
        P("tile", None),
        P(),
    )
    out_specs = (P(None, None, ("member", "tile")), P(None, ("member", "tile")), P())
    return jax.shard_map(local, mesh=mesh, in_specs=in_specs, out_specs=out_specs, check_vma=False)
```

time: 140 us -> 48.2 us (0.34)
  blocking collectives: 58 us -> 0 us
  local copies, waits for them, and re-layouts: 18.4 us -> 1.39 us
  between operations: 14.2 us -> 0.67 us
  starting transfers between devices: 0.04 us -> 12.4 us
  matrix products: 11.3 us -> 0 us
  waiting for transfers between devices: 32.4 us -> 21.2 us
  Pallas kernels: 0 us -> 9.79 us
  other arithmetic: 4.26 us -> 2.33 us
    psum x1 -> x0, blocking collectives: 38.9 us -> none  [local(): covariance = lax.psum(local_cov, ('member', 'tile'))]
    reduce_scatter x1 -> x0, waiting for transfers between devices: 32.4 us -> none  [local(): lax.psum_scatter(regrouped, 'tile', scatter_dimension=2, tiled=True)]
    ppermute x0 -> x9, waiting for transfers between devices: none -> 21.2 us  [exchange(): return lax.ppermute(value, axis, [(i, i ^ bit) for i in range(size)])]
    all_to_all x1 -> x0, blocking collectives: 19.1 us -> none  [local(): lax.all_to_all(partial_value, 'member', split_axis=2, concat_axis=0, tile...]
    ppermute x0 -> x9, starting transfers between devices: none -> 12.4 us  [exchange(): return lax.ppermute(value, axis, [(i, i ^ bit) for i in range(size)])]
    dot_general x4 -> x0, matrix products: 11.3 us -> none  [the longest x1 9.66 us: local(): jnp.einsum('mkxl,bxl->mbkl', northward_volume_carriage, region_indicator_...]
    pallas_call x0 -> x3, Pallas kernels: none -> 9.79 us  [the longest x1 4.35 us: local(): pl.pallas_call(functools.partial(gather_kernel, members_here=members_here...]
    div x4 -> x0, local copies, waits for them, and re-layouts: 5.67 us -> none  [the longest x1 5.26 us: local(): jnp.einsum('mkxl,bxl->mbkl', northward_volume_carriage, region_indicator_...]
  transfers between devices with their start and end apart: 1 -> 9, of which waited for: 1 -> 9; matrix products, arithmetic and copies ran while one was open for 0% -> 0% of each run, Pallas kernels for 0% -> 0%
where the time goes in v1:
time: 48.2 us; the launch traced here: 47.9 us
  waiting for transfers between devices  21.2 us (44%)
  starting transfers between devices  12.4 us (26%)
  Pallas kernels  9.79 us (20%)
  other arithmetic  2.33 us (5%)
  local copies, waits for them, and re-layouts  1.39 us (3%)
  between operations  0.67 us (1%)
    ppermute x9, waiting for transfers between devices, exchange(): return lax.ppermute(value, axis, [(i, i ^ bit) for i in range(size)])  21.2 us
    ppermute x9, starting transfers between devices, exchange(): return lax.ppermute(value, axis, [(i, i ^ bit) for i in range(size)])  12.4 us
    pallas_call x1, Pallas kernels, local(): pl.pallas_call(functools.partial(gather_kernel, members_here=members_here...  4.35 us
    pallas_call x1, Pallas kernels, local(): pl.pallas_call(functools.partial(partial_kernel, members_here=members_her...  3.95 us
    pallas_call x1, Pallas kernels, local(): pl.pallas_call(functools.partial(unpack_kernel, members=members, scale=1....  1.49 us
    unnamed x14, local copies, waits for them, and re-layouts  1.39 us
  transfers between devices with their start and end apart: 9, of which 9 were waited for; matrix products, arithmetic and copies ran while one was open for 0% of the time, Pallas kernels for 0%

profile of v1, /device:TPU:0, one launch (start us, length us, event | category | flops | bytes accessed | tf_op | source)
XLA Modules:
  0.0 47.9 jit_solution(15149743053650863967)
XLA Ops:
  0.6 0.6 %cosine_multiply_fusion.spacing_ref = f32[1,256]{1,0:T(1,128)} fusion(), kind=kLoop, calls=%fused_computation.7 | loop fusion | flops 1280 | bytes 1024 | tf_op jit(solution)/shard_map/div | solution.py:218
  1.3 4.0 %partial.1 = (f32[4,21,8,128]{3,2,1,0:T(8,128)}, f32[4,21,8,128]{3,2,1,0:T(8,128)}) custom-call(f32[512,256]{1,0:T(8,128)} %bitcast.25, f32[512,256]{1,0:T(8,128)} %bitcast.26, f32[512,256]{1,0:T(8,128)} %bitcast.27, s32[8,256]{1,0:T(8,128)} %region_ref.1, f32[1,256]{1,0:T(1,128)} %cosine_multiply_fusion.spacing_ref), custom_call_target="tpu_custom_call" | custom-call | tf_op jit(solution)/shard_map/partial/pallas_call | solution.py:221
  5.2 0.0 copy-start
  5.2 0.5 %collective-permute-start = (f32[4,21,8,128]{3,2,1,0:T(8,128)}, f32[4,21,8,128]{3,2,1,0:T(8,128)S(1)}, u32[]{:S(2)}, u32[]{:S(2)}) collective-permute-start(f32[4,21,8,128]{3,2,1,0:T(8,128)} %get-tuple-element.9), channel_id=1, source_target_pairs={{0,1},{1,0},{2,3},{3,2},{4,5},{5,4},{6,7},{7,6},{8,9},{9,8},{10,11... | collective-permute-start | bytes 1032200 | tf_op jit(solution)/shard_map/ppermute | solution.py:198
  5.7 1.5 %collective-permute-done = f32[4,21,8,128]{3,2,1,0:T(8,128)S(1)} collective-permute-done((f32[4,21,8,128]{3,2,1,0:T(8,128)}, f32[4,21,8,128]{3,2,1,0:T(8,128)S(1)}, u32[]{:S(2)}, u32[]{:S(2)}) %collective-permute-start) | collective-permute-done | bytes 344096 | tf_op jit(solution)/shard_map/ppermute | solution.py:198
  7.2 0.9 %fusion = f32[2,21,8,128]{3,2,1,0:T(8,128)S(1)} fusion(f32[2,2,21,8,128]{4,3,2,1,0:T(8,128)S(1)} %bitcast.30, s32[]{:T(128)S(6)} %select_n.42, f32[2,2,21,8,128]{4,3,2,1,0:T(8,128)} %bitcast.28), kind=kLoop, calls=%fused_computation.1 | loop fusion | flops 43008 | bytes 516100 | tf_op jit(solution)/shard_map/add | solution.py:255
  8.1 3.0 %collective-permute-start.1 = (f32[2,21,8,128]{3,2,1,0:T(8,128)S(1)}, f32[2,21,8,128]{3,2,1,0:T(8,128)S(1)}, u32[]{:S(2)}, u32[]{:S(2)}) collective-permute-start(f32[2,21,8,128]{3,2,1,0:T(8,128)S(1)} %fusion), channel_id=1, source_target_pairs={{0,2},{1,3},{2,0},{3,1},{4,6},{5,7},{6,4},{7,5},{8,10},{9,11},{10,... | collective-permute-start | bytes 516104 | tf_op jit(solution)/shard_map/ppermute | solution.py:198
  11.1 0.0 copy-done
  11.2 4.7 %collective-permute-done.1 = f32[2,21,8,128]{3,2,1,0:T(8,128)S(1)} collective-permute-done((f32[2,21,8,128]{3,2,1,0:T(8,128)S(1)}, f32[2,21,8,128]{3,2,1,0:T(8,128)S(1)}, u32[]{:S(2)}, u32[]{:S(2)}) %collective-permute-start.1) | collective-permute-done | bytes 172064 | tf_op jit(solution)/shard_map/ppermute | solution.py:198
  15.8 2.8 %collective-permute-start.2 = (f32[1,21,8,128]{3,2,1,0:T(8,128)S(1)}, f32[1,21,8,128]{3,2,1,0:T(8,128)S(1)}, u32[]{:S(2)}, u32[]{:S(2)}) collective-permute-start(f32[1,21,8,128]{3,2,1,0:T(8,128)S(1)} %bitcast_add_fusion.1), channel_id=1, source_target_pairs={{0,4},{1,5},{2,6},{3,7},{4,0},{5,1},{6,2},{7,3},{8,12},{9,13},{10,... | collective-permute-start | bytes 258056 | tf_op jit(solution)/shard_map/ppermute | solution.py:198
  18.6 4.0 %collective-permute-done.2 = f32[1,21,8,128]{3,2,1,0:T(8,128)S(1)} collective-permute-done((f32[1,21,8,128]{3,2,1,0:T(8,128)S(1)}, f32[1,21,8,128]{3,2,1,0:T(8,128)S(1)}, u32[]{:S(2)}, u32[]{:S(2)}) %collective-permute-start.2) | collective-permute-done | bytes 86048 | tf_op jit(solution)/shard_map/ppermute | solution.py:198
  22.6 0.0 copy-start.1
  22.7 2.5 %collective-permute-start.5 = (f32[21,8,128]{2,1,0:T(8,128)S(1)}, f32[21,8,128]{2,1,0:T(8,128)S(1)}, u32[]{:S(2)}, u32[]{:S(2)}) collective-permute-start(f32[21,8,128]{2,1,0:T(8,128)S(1)} %fusion.2.refs_1_), channel_id=1, source_target_pairs={{0,24},{8,16},{16,8},{24,0},{1,25},{9,17},{17,9},{25,1},{2,26},{10... | collective-permute-start | bytes 258056 | tf_op jit(solution)/shard_map/ppermute | solution.py:198
  25.1 0.5 %collective-permute-start.4 = (f32[21,8,128]{2,1,0:T(8,128)S(1)}, f32[21,8,128]{2,1,0:T(8,128)S(1)}, u32[]{:S(2)}, u32[]{:S(2)}) collective-permute-start(f32[21,8,128]{2,1,0:T(8,128)S(1)} %fusion.2.refs_1_), channel_id=1, source_target_pairs={{0,16},{8,24},{16,0},{24,8},{1,17},{9,25},{17,1},{25,9},{2,18},{10... | collective-permute-start | bytes 258056 | tf_op jit(solution)/shard_map/ppermute | solution.py:198
  25.7 0.6 %collective-permute-start.3 = (f32[21,8,128]{2,1,0:T(8,128)S(1)}, f32[21,8,128]{2,1,0:T(8,128)S(1)}, u32[]{:S(2)}, u32[]{:S(2)}) collective-permute-start(f32[21,8,128]{2,1,0:T(8,128)S(1)} %fusion.2.refs_1_), channel_id=1, source_target_pairs={{0,8},{8,0},{16,24},{24,16},{1,9},{9,1},{17,25},{25,17},{2,10},{10... | collective-permute-start | bytes 258056 | tf_op jit(solution)/shard_map/ppermute | solution.py:198
  26.2 1.9 %collective-permute-done.5.refs_4_ = f32[21,8,128]{2,1,0:T(8,128)S(1)} collective-permute-done((f32[21,8,128]{2,1,0:T(8,128)S(1)}, f32[21,8,128]{2,1,0:T(8,128)S(1)}, u32[]{:S(2)}, u32[]{:S(2)}) %collective-permute-start.5) | collective-permute-done | bytes 86048 | tf_op jit(solution)/shard_map/ppermute | solution.py:198
  28.1 0.0 copy-start.2
  28.1 1.5 %collective-permute-done.4.refs_3_ = f32[21,8,128]{2,1,0:T(8,128)S(1)} collective-permute-done((f32[21,8,128]{2,1,0:T(8,128)S(1)}, f32[21,8,128]{2,1,0:T(8,128)S(1)}, u32[]{:S(2)}, u32[]{:S(2)}) %collective-permute-start.4) | collective-permute-done | bytes 86048 | tf_op jit(solution)/shard_map/ppermute | solution.py:198
  29.6 0.0 copy-start.3
  29.6 0.5 %collective-permute-done.3.refs_2_ = f32[21,8,128]{2,1,0:T(8,128)S(1)} collective-permute-done((f32[21,8,128]{2,1,0:T(8,128)S(1)}, f32[21,8,128]{2,1,0:T(8,128)S(1)}, u32[]{:S(2)}, u32[]{:S(2)}) %collective-permute-start.3) | collective-permute-done | bytes 86048 | tf_op jit(solution)/shard_map/ppermute | solution.py:198
  30.1 0.0 copy-done.1
  30.1 0.0 copy-done.2
  30.1 0.1 copy-done.3
  30.3 0.0 copy-start.4
  30.3 0.6 %copy-done.4 = f32[21,8,128]{2,1,0:T(8,128)} copy-done((f32[21,8,128]{2,1,0:T(8,128)}, f32[21,8,128]{2,1,0:T(8,128)S(1)}, u32[]{:S(2)}) %copy-start.4) | copy-done | bytes 86040
  30.9 4.4 %gather.1 = (f32[10,8,16]{2,1,0:T(8,128)}, f32[8,10]{1,0:T(8,128)}, f32[16,256]{1,0:T(8,128)}) custom-call(s32[256]{0:T(256)} %refs_0_.1, f32[21,8,128]{2,1,0:T(8,128)} %copy-done.1, f32[21,8,128]{2,1,0:T(8,128)} %copy-done.4, f32[21,8,128]{2,1,0:T(8,128)} %copy-done.3, f32[21,8,128]{2,1,0:T(8,128)} %copy-done.2), custom_call_target="tpu_custom_call" | custom-call | tf_op jit(solution)/shard_map/gather/pallas_call | solution.py:265
  35.3 0.0 collective-permute-start.6
  35.3 1.4 %collective-permute-done.6 = f32[16,256]{1,0:T(8,128)S(1)} collective-permute-done((f32[16,256]{1,0:T(8,128)}, f32[16,256]{1,0:T(8,128)S(1)}, u32[]{:S(2)}, u32[]{:S(2)}) %collective-permute-start.6) | collective-permute-done | bytes 16416 | tf_op jit(solution)/shard_map/ppermute | solution.py:198
  36.7 0.7 %add.100 = f32[16,256]{1,0:T(8,128)S(1)} add(f32[16,256]{1,0:T(8,128)} %get-tuple-element.12, f32[16,256]{1,0:T(8,128)S(1)} %collective-permute-done.6) | non-fusion elementwise | flops 4096 | bytes 49152 | tf_op jit(solution)/shard_map/add | solution.py:284
  37.4 0.6 %collective-permute-start.7 = (f32[16,256]{1,0:T(8,128)S(1)}, f32[16,256]{1,0:T(8,128)S(1)}, u32[]{:S(2)}, u32[]{:S(2)}) collective-permute-start(f32[16,256]{1,0:T(8,128)S(1)} %add.100), channel_id=1, source_target_pairs={{0,2},{1,3},{2,0},{3,1},{4,6},{5,7},{6,4},{7,5},{8,10},{9,11},{10,... | collective-permute-start | bytes 49160 | tf_op jit(solution)/shard_map/ppermute | solution.py:198
  38.0 3.1 %collective-permute-done.7 = f32[16,256]{1,0:T(8,128)S(1)} collective-permute-done((f32[16,256]{1,0:T(8,128)S(1)}, f32[16,256]{1,0:T(8,128)S(1)}, u32[]{:S(2)}, u32[]{:S(2)}) %collective-permute-start.7) | collective-permute-done | bytes 16416 | tf_op jit(solution)/shard_map/ppermute | solution.py:198
  41.1 0.0 copy-start.5
  41.1 1.9 %collective-permute-start.8 = (f32[16,256]{1,0:T(8,128)S(1)}, f32[16,256]{1,0:T(8,128)S(1)}, u32[]{:S(2)}, u32[]{:S(2)}) collective-permute-start(f32[16,256]{1,0:T(8,128)S(1)} %add.101.refs_0_), channel_id=1, source_target_pairs={{0,4},{1,5},{2,6},{3,7},{4,0},{5,1},{6,2},{7,3},{8,12},{9,13},{10,... | collective-permute-start | bytes 49160 | tf_op jit(solution)/shard_map/ppermute | solution.py:198
  43.1 2.7 %collective-permute-done.8.refs_1_ = f32[16,256]{1,0:T(8,128)S(1)} collective-permute-done((f32[16,256]{1,0:T(8,128)S(1)}, f32[16,256]{1,0:T(8,128)S(1)}, u32[]{:S(2)}, u32[]{:S(2)}) %collective-permute-start.8) | collective-permute-done | bytes 16416 | tf_op jit(solution)/shard_map/ppermute | solution.py:198
  45.8 0.0 copy-done.5
  45.8 0.0 copy-start.6
  45.8 0.6 %copy-done.6 = f32[16,256]{1,0:T(8,128)} copy-done((f32[16,256]{1,0:T(8,128)}, f32[16,256]{1,0:T(8,128)S(1)}, u32[]{:S(2)}) %copy-start.6) | copy-done | bytes 16408
  46.4 1.5 %unpack.1 = f32[16,16,16]{2,1,0:T(8,128)} custom-call(f32[16,256]{1,0:T(8,128)} %copy-done.5, f32[16,256]{1,0:T(8,128)} %copy-done.6), custom_call_target="tpu_custom_call" | custom-call | tf_op jit(solution)/shard_map/unpack/pallas_call | solution.py:287
  (4 shorter events, 0.0 us)
Async XLA Ops:
  5.2 5.9 %copy-start = (f32[4,21,8,128]{3,2,1,0:T(8,128)S(1)}, f32[4,21,8,128]{3,2,1,0:T(8,128)}, u32[]{:S(2)}) copy-start(f32[4,21,8,128]{3,2,1,0:T(8,128)} %get-tuple-element.8) | copy-start | bytes 1032196
  5.2 2.0 %collective-permute-start = (f32[4,21,8,128]{3,2,1,0:T(8,128)}, f32[4,21,8,128]{3,2,1,0:T(8,128)S(1)}, u32[]{:S(2)}, u32[]{:S(2)}) collective-permute-start(f32[4,21,8,128]{3,2,1,0:T(8,128)} %get-tuple-element.9), channel_id=1, source_target_pairs={{0,1},{1,0},{2,3},{3,2},{4,5},{5,4},{6,7},{7,6},{8,9},{9,8},{10,11... | collective-permute-start | bytes 1032200 | tf_op jit(solution)/shard_map/ppermute | solution.py:198
  8.1 7.7 %collective-permute-start.1 = (f32[2,21,8,128]{3,2,1,0:T(8,128)S(1)}, f32[2,21,8,128]{3,2,1,0:T(8,128)S(1)}, u32[]{:S(2)}, u32[]{:S(2)}) collective-permute-start(f32[2,21,8,128]{3,2,1,0:T(8,128)S(1)} %fusion), channel_id=1, source_target_pairs={{0,2},{1,3},{2,0},{3,1},{4,6},{5,7},{6,4},{7,5},{8,10},{9,11},{10,... | collective-permute-start | bytes 516104 | tf_op jit(solution)/shard_map/ppermute | solution.py:198
  15.8 6.8 %collective-permute-start.2 = (f32[1,21,8,128]{3,2,1,0:T(8,128)S(1)}, f32[1,21,8,128]{3,2,1,0:T(8,128)S(1)}, u32[]{:S(2)}, u32[]{:S(2)}) collective-permute-start(f32[1,21,8,128]{3,2,1,0:T(8,128)S(1)} %bitcast_add_fusion.1), channel_id=1, source_target_pairs={{0,4},{1,5},{2,6},{3,7},{4,0},{5,1},{6,2},{7,3},{8,12},{9,13},{10,... | collective-permute-start | bytes 258056 | tf_op jit(solution)/shard_map/ppermute | solution.py:198
  22.6 7.5 %copy-start.1 = (f32[21,8,128]{2,1,0:T(8,128)}, f32[21,8,128]{2,1,0:T(8,128)S(1)}, u32[]{:S(2)}) copy-start(f32[21,8,128]{2,1,0:T(8,128)S(1)} %fusion.2.refs_1_) | copy-start | bytes 258052
  22.7 5.4 %collective-permute-start.5 = (f32[21,8,128]{2,1,0:T(8,128)S(1)}, f32[21,8,128]{2,1,0:T(8,128)S(1)}, u32[]{:S(2)}, u32[]{:S(2)}) collective-permute-start(f32[21,8,128]{2,1,0:T(8,128)S(1)} %fusion.2.refs_1_), channel_id=1, source_target_pairs={{0,24},{8,16},{16,8},{24,0},{1,25},{9,17},{17,9},{25,1},{2,26},{10... | collective-permute-start | bytes 258056 | tf_op jit(solution)/shard_map/ppermute | solution.py:198
  25.1 4.5 %collective-permute-start.4 = (f32[21,8,128]{2,1,0:T(8,128)S(1)}, f32[21,8,128]{2,1,0:T(8,128)S(1)}, u32[]{:S(2)}, u32[]{:S(2)}) collective-permute-start(f32[21,8,128]{2,1,0:T(8,128)S(1)} %fusion.2.refs_1_), channel_id=1, source_target_pairs={{0,16},{8,24},{16,0},{24,8},{1,17},{9,25},{17,1},{25,9},{2,18},{10... | collective-permute-start | bytes 258056 | tf_op jit(solution)/shard_map/ppermute | solution.py:198
  25.7 4.5 %collective-permute-start.3 = (f32[21,8,128]{2,1,0:T(8,128)S(1)}, f32[21,8,128]{2,1,0:T(8,128)S(1)}, u32[]{:S(2)}, u32[]{:S(2)}) collective-permute-start(f32[21,8,128]{2,1,0:T(8,128)S(1)} %fusion.2.refs_1_), channel_id=1, source_target_pairs={{0,8},{8,0},{16,24},{24,16},{1,9},{9,1},{17,25},{25,17},{2,10},{10... | collective-permute-start | bytes 258056 | tf_op jit(solution)/shard_map/ppermute | solution.py:198
  28.1 2.0 %copy-start.2 = (f32[21,8,128]{2,1,0:T(8,128)}, f32[21,8,128]{2,1,0:T(8,128)S(1)}, u32[]{:S(2)}) copy-start(f32[21,8,128]{2,1,0:T(8,128)S(1)} %collective-permute-done.5.refs_4_) | copy-start | bytes 258052
  29.6 0.6 %copy-start.3 = (f32[21,8,128]{2,1,0:T(8,128)}, f32[21,8,128]{2,1,0:T(8,128)S(1)}, u32[]{:S(2)}) copy-start(f32[21,8,128]{2,1,0:T(8,128)S(1)} %collective-permute-done.4.refs_3_) | copy-start | bytes 258052
  30.3 0.6 %copy-start.4 = (f32[21,8,128]{2,1,0:T(8,128)}, f32[21,8,128]{2,1,0:T(8,128)S(1)}, u32[]{:S(2)}) copy-start(f32[21,8,128]{2,1,0:T(8,128)S(1)} %collective-permute-done.3.refs_2_) | copy-start | bytes 258052
  35.3 1.4 %collective-permute-start.6 = (f32[16,256]{1,0:T(8,128)}, f32[16,256]{1,0:T(8,128)S(1)}, u32[]{:S(2)}, u32[]{:S(2)}) collective-permute-start(f32[16,256]{1,0:T(8,128)} %get-tuple-element.12), channel_id=1, source_target_pairs={{0,1},{1,0},{2,3},{3,2},{4,5},{5,4},{6,7},{7,6},{8,9},{9,8},{10,11... | collective-permute-start | bytes 49160 | tf_op jit(solution)/shard_map/ppermute | solution.py:198
  37.4 3.7 %collective-permute-start.7 = (f32[16,256]{1,0:T(8,128)S(1)}, f32[16,256]{1,0:T(8,128)S(1)}, u32[]{:S(2)}, u32[]{:S(2)}) collective-permute-start(f32[16,256]{1,0:T(8,128)S(1)} %add.100), channel_id=1, source_target_pairs={{0,2},{1,3},{2,0},{3,1},{4,6},{5,7},{6,4},{7,5},{8,10},{9,11},{10,... | collective-permute-start | bytes 49160 | tf_op jit(solution)/shard_map/ppermute | solution.py:198
  41.1 4.6 %copy-start.5 = (f32[16,256]{1,0:T(8,128)}, f32[16,256]{1,0:T(8,128)S(1)}, u32[]{:S(2)}) copy-start(f32[16,256]{1,0:T(8,128)S(1)} %add.101.refs_0_) | copy-start | bytes 49156
  41.1 4.6 %collective-permute-start.8 = (f32[16,256]{1,0:T(8,128)S(1)}, f32[16,256]{1,0:T(8,128)S(1)}, u32[]{:S(2)}, u32[]{:S(2)}) collective-permute-start(f32[16,256]{1,0:T(8,128)S(1)} %add.101.refs_0_), channel_id=1, source_target_pairs={{0,4},{1,5},{2,6},{3,7},{4,0},{5,1},{6,2},{7,3},{8,12},{9,13},{10,... | collective-permute-start | bytes 49160 | tf_op jit(solution)/shard_map/ppermute | solution.py:198
  45.8 0.6 %copy-start.6 = (f32[16,256]{1,0:T(8,128)}, f32[16,256]{1,0:T(8,128)S(1)}, u32[]{:S(2)}) copy-start(f32[16,256]{1,0:T(8,128)S(1)} %collective-permute-done.8.refs_1_) | copy-start | bytes 49156

commit v2 on v0

v2 whole, which is shorter than its diff:
```python
import functools
import math

import jax
import jax.numpy as jnp
from jax import lax
from jax.experimental import pallas as pl
from jax.experimental.pallas import tpu as pltpu
from jax.sharding import PartitionSpec as P

BASINS = 10
NBANDS = 16
LANES = 128
SUB = 8
HEAT_LANES = 16
HIGHEST = lax.Precision.HIGHEST


def metric_factor(lats):
    index = jnp.arange(lats, dtype=jnp.float32)
    return jnp.cos((-80.0 + 160.0 * (index + 0.5) / lats) * (math.pi / 180.0))


def iota(shape, dim):
    return lax.broadcasted_iota(jnp.int32, shape, dim)


def log2(n):
    assert n & (n - 1) == 0
    return n.bit_length() - 1


def split_features(layers, members_here):
    feats = BASINS * layers
    rest = feats - LANES
    assert 0 < rest and rest * members_here == LANES and LANES % layers == 0
    return feats, rest


def exact_parts(x):
    parts = []
    for _ in range(3):
        parts.append(x.astype(jnp.bfloat16))
        x = x - parts[-1].astype(jnp.float32)
    return parts


def partial_kernel(v_ref, h_ref, w_ref, region_ref, spacing_ref, keep0_ref, send0_ref,
                   keep1_ref, send1_ref, buf, small, sems, small_sem,
                   *, half, members_here, layers, columns, groups, tiles):
    feats, rest = split_features(layers, members_here)
    core = lax.axis_index("tile") % 2
    halves = layers // SUB
    lshift = log2(layers)
    slots = members_here + 1
    pieces = LANES // SUB
    blocks = 2 * half
    inputs = (v_ref, h_ref, w_ref)
    per = layers * blocks * columns

    def fetch(m, a):
        part = pl.ds(m * per, per)
        return pltpu.make_async_copy(inputs[a].at[part], buf.at[a, part], sems.at[m, a])

    labels = pltpu.make_async_copy(region_ref, small, small_sem)
    labels.start()
    for m in range(members_here):
        for a in range(3):
            fetch(m, a).start()
    rows = iota((feats, feats), 0)
    cols = iota((feats, feats), 1)
    running = ((rows >> lshift) == (cols >> lshift)) & (cols <= rows)
    running = jnp.where(running, 1.0, 0.0).astype(jnp.bfloat16)
    rows = iota((LANES, BASINS * SUB), 0)
    cols = iota((LANES, BASINS * SUB), 1)
    gather = jnp.where((rows & (HEAT_LANES - 1)) == (cols >> log2(SUB)), 1.0, 0.0)
    gather = gather.astype(jnp.bfloat16)
    heat_group = iota((LANES, LANES), 0) >> log2(HEAT_LANES)
    heat_lat = iota((LANES, LANES), 1)

    def select(table, x):
        return jnp.dot(
            jnp.concatenate([table] * 3, 1), jnp.concatenate(exact_parts(x), 0),
            preferred_element_type=jnp.float32,
        )

    def put(late, place, slot, even, odd):
        keep_ref, send_ref = (keep1_ref, send1_ref) if late else (keep0_ref, send0_ref)
        keep_ref[place, slot] = jnp.where(core == 0, even, odd)
        send_ref[place, slot] = jnp.where(core == 0, odd, even)

    def put_block(lb, s, value):
        for row in range(0, pieces, 2):
            group, tile = divmod(lb * pieces + row, tiles)
            late = group >= groups // 2
            slot = (group - late * (groups // 2)) * slots + s
            even = value[row * SUB : (row + 1) * SUB]
            put(late, tile // 2, slot, even, value[(row + 1) * SUB : (row + 2) * SUB])

    warm = [[None] * columns for _ in range(blocks)]
    extra = [[] for _ in range(blocks)]
    labels.wait()
    region, spacing = small[...], spacing_ref[...]

    def label(lb, x):
        line = region[x : x + 1, lb * LANES : (lb + 1) * LANES]
        return jnp.broadcast_to(line, (SUB, LANES))

    for m in range(members_here):
        for a in range(3):
            fetch(m, a).wait()
        for lb in range(blocks):
            scale = spacing[:, lb * LANES : (lb + 1) * LANES]
            acc = [[None] * halves for _ in range(BASINS)]
            for x in range(columns):
                flux = []
                for k in range(halves):
                    start = m * per + (k * SUB * blocks + lb) * columns + x
                    at = pl.ds(start, SUB, stride=blocks * columns)
                    one = buf[0, at, :] * buf[1, at, :] * scale
                    heat = one * buf[2, at, :]
                    warm[lb][x] = heat if warm[lb][x] is None else warm[lb][x] + heat
                    flux.append(one)
                here = label(lb, x)
                for b in range(BASINS):
                    hit = here == b
                    for k in range(halves):
                        part = jnp.where(hit, flux[k], 0.0)
                        acc[b][k] = part if acc[b][k] is None else acc[b][k] + part
            stacked = jnp.concatenate([acc[b][k] for b in range(BASINS) for k in range(halves)], 0)
            stream = select(running, stacked)
            put_block(lb, m, stream[:LANES].T)
            extra[lb].append(stream[LANES:])
    span = tiles * SUB
    heat = None
    for lb in range(blocks):
        put_block(lb, members_here, jnp.concatenate(extra[lb], 0).T)
        basin_heat = []
        for b in range(BASINS):
            total = None
            for x in range(columns):
                part = jnp.where(label(lb, x) == b, warm[lb][x], 0.0)
                total = part if total is None else total + part
            basin_heat.append(total)
        block = select(gather, jnp.concatenate(basin_heat, 0))
        for p in range(LANES // span):
            moved = block if p == 0 else pltpu.roll(block, LANES - p * span, 1)
            mine = (heat_group == lb * (LANES // span) + p) & (heat_lat < span)
            part = jnp.where(mine, moved, 0.0)
            heat = part if heat is None else heat + part
    heat = heat.T
    for t in range(0, tiles, 2):
        even = heat[t * SUB : (t + 1) * SUB]
        put(True, t // 2, slots * (groups // 2), even, heat[(t + 1) * SUB : (t + 2) * SUB])


def bands_kernel(zone_ref, order_ref, out_ref, *, members, groups, tiles):
    tile = lax.axis_index("tile")
    wide = members * SUB
    sshift = log2(SUB)
    row = iota((NBANDS * members, wide), 0)
    col = iota((NBANDS * members, wide), 1)
    same_member = (row & (members - 1)) == (col >> sshift)
    band = row >> log2(members)
    lat_lane = iota((1, wide), 1) & (SUB - 1)
    for g in range(groups):
        zone = jnp.zeros((1, wide), jnp.int32)
        for j in range(SUB):
            zone = jnp.where(lat_lane == j, zone_ref[(g * tiles + tile) * SUB + j], zone)
        hit = jnp.where(same_member & (band == zone), 1.0, 0.0)
        out_ref[g] = hit.astype(jnp.bfloat16)


def share_kernel(*refs, members_here, layers, groups):
    bands_ref = refs[0]
    parts = refs[1 : 1 + groups]
    cov_ref, all_ref = refs[1 + groups :]
    feats, rest = split_features(layers, members_here)
    slots = members_here + 1
    members = members_here * groups
    mine = lax.axis_index("member")
    for r in range(groups):
        all_ref[mine ^ r] = parts[r][: groups * slots]
    wide = members * SUB
    lane = iota((SUB, LANES), 1)
    jmask = SUB - 1
    same_lat = (iota((SUB, wide), 0)) == (iota((SUB, wide), 1) & jmask)
    last = (((1,), (1,)), ((), ()))
    total = None
    for g in range(groups):
        heads, tails = [], []
        for q in range(groups):
            tail = all_ref[q, g * slots + members_here]
            for m in range(members_here):
                heads.append(all_ref[q, g * slots + m])
                moved = tail if m == 0 else pltpu.roll(tail, LANES - m * rest, 1)
                tails.append(jnp.where(lane < rest, moved, 0.0))
        head_mean = sum(heads) * (1.0 / members)
        tail_mean = sum(tails) * (1.0 / members)
        head = jnp.concatenate([a - head_mean for a in heads], 0)
        tail = jnp.concatenate([a - tail_mean for a in tails], 0)
        both = jnp.concatenate([head, tail], 1)
        gram = lax.dot_general(
            both, both, last, precision=HIGHEST, preferred_element_type=jnp.float32
        )
        summed = jnp.concatenate(
            [
                jnp.sum(
                    jnp.where(same_lat, gram[n * SUB : (n + 1) * SUB], 0.0), axis=0, keepdims=True
                )
                for n in range(members)
            ],
            0,
        )
        share = lax.dot_general(
            jnp.concatenate(exact_parts(summed), 0), bands_ref[g], last,
            preferred_element_type=jnp.float32,
        )
        total = share if total is None else total + share
    cov_ref[...] = total[:members] + (total[members : 2 * members] + total[2 * members :])


def means_kernel(*refs, members_here, layers, groups):
    parts = refs[:groups]
    psi_ref, heat_ref = refs[groups:]
    feats, rest = split_features(layers, members_here)
    slots = members_here + 1
    members = members_here * groups
    mine = lax.axis_index("member")
    at = mine * slots

    def total(slot):
        return sum(ref[slot] for ref in parts)

    head = sum(total(at + m) for m in range(members_here)) * (1.0 / members)
    packed = total(at + members_here)
    tail = packed
    for m in range(1, members_here):
        tail = tail + pltpu.roll(packed, LANES - m * rest, 1)
    tail = tail * (1.0 / members)
    for b in range(BASINS):
        part, lane = divmod(b * layers, LANES)
        psi_ref[b] = (tail if part else head)[:, lane : lane + layers]
    warm = total(groups * slots)
    out = jnp.zeros((SUB, BASINS), jnp.float32)
    for g in range(groups):
        out = jnp.where(mine == g, warm[:, g * HEAT_LANES : g * HEAT_LANES + BASINS], out)
    heat_ref[...] = out * (1.0 / (members * math.sqrt(layers)))


def unpack_kernel(*refs, members, scale):
    out_ref = refs[-1]
    total = refs[0][...]
    for ref in refs[1:-1]:
        total = total + ref[...]
    total = total * scale
    for c in range(NBANDS):
        out_ref[c] = total[:, c * members : (c + 1) * members]


def exchange(value, axis, bit):
    size = lax.axis_size(axis)
    return lax.ppermute(value, axis, [(i, i ^ bit) for i in range(size)])


def halve(keep, got, tile, bit):
    shape = (keep.shape[0] // 2, 2) + keep.shape[1:]
    keep, got = keep.reshape(shape), got.reshape(shape)
    mine = (tile // bit) % 2
    send, keep = (
        lax.dynamic_index_in_dim(keep, side, 1, False)
        + lax.dynamic_index_in_dim(got, side, 1, False)
        for side in (1 - mine, mine)
    )
    return keep, exchange(send, "tile", bit)


ANY = pl.BlockSpec(memory_space=pl.ANY)
VMEM = pl.BlockSpec(memory_space=pltpu.MemorySpace.VMEM)
PARAMS = pltpu.CompilerParams(vmem_limit_bytes=16 * 1024 * 1024)
SMEM = pl.BlockSpec(memory_space=pltpu.MemorySpace.SMEM)


def local(
    northward_speed_field,
    level_depth_extent,
    potential_warmth_anomaly,
    ocean_region_label,
    zone_for_parallel,
):
    members_here, layers, columns, lats = northward_speed_field.shape
    tiles = lax.axis_size("tile")
    groups = lax.axis_size("member")
    members = members_here * groups
    per_block = LANES // SUB // tiles
    half = lats // LANES // 2
    count = groups // 2
    slots = members_here + 1
    assert lats == groups * tiles * SUB and groups * HEAT_LANES <= LANES
    assert half >= 1 and half * per_block == count and lats == 2 * half * LANES
    spacing = (metric_factor(lats) / math.sqrt(columns * tiles)).reshape(1, lats)
    rows = members_here * layers * columns
    sizes = dict(
        half=half, members_here=members_here, layers=layers, columns=columns,
        groups=groups, tiles=tiles,
    )
    inputs = (northward_speed_field, level_depth_extent, potential_warmth_anomaly)
    blocked = [
        pltpu.with_memory_space_constraint(
            x.reshape(rows // columns, columns, 2 * half, LANES)
            .transpose(0, 2, 1, 3)
            .reshape(2 * half * rows, LANES),
            pltpu.MemorySpace.HBM,
        )
        for x in (northward_speed_field, level_depth_extent, potential_warmth_anomaly)
    ]
    labels = pltpu.with_memory_space_constraint(ocean_region_label, pltpu.MemorySpace.HBM)
    early = pltpu.VMEM((tiles // 2, count * slots, SUB, LANES), jnp.float32)
    late = pltpu.VMEM((tiles // 2, count * slots + 1, SUB, LANES), jnp.float32)
    keep0, send0, keep1, send1 = pl.pallas_call(
        functools.partial(partial_kernel, **sizes),
        out_shape=(early, early, late, late),
        in_specs=[ANY] * 4 + [VMEM],
        out_specs=(VMEM,) * 4,
        scratch_shapes=[
            pltpu.VMEM((3, 2 * half * rows, LANES), jnp.float32),
            pltpu.VMEM((columns, lats), jnp.int32),
            pltpu.SemaphoreType.DMA((members_here, 3)),
            pltpu.SemaphoreType.DMA(()),
        ],
        compiler_params=PARAMS,
        name="partial",
    )(*blocked, labels, spacing)
    got0 = exchange(send0, "tile", 1)
    got1 = exchange(send1, "tile", 1)
    bands = pl.pallas_call(
        functools.partial(bands_kernel, members=members, groups=groups, tiles=tiles),
        out_shape=pltpu.VMEM((groups, NBANDS * members, members * SUB), jnp.bfloat16),
        in_specs=[SMEM, ANY],
        out_specs=VMEM,
        compiler_params=PARAMS,
        name="bands",
    )(zone_for_parallel, got0)
    tile = lax.axis_index("tile")
    chunks = [(keep0, got0), (keep1, got1)]
    bit = 2
    while bit < tiles:
        chunks = [halve(keep, got, tile, bit) for keep, got in chunks]
        bit *= 2
    owned = jnp.concatenate([(keep + got)[0] for keep, got in chunks], 0)
    parts = [owned] + [exchange(owned, "member", r) for r in range(1, groups)]
    known = dict(members_here=members_here, layers=layers, groups=groups)
    share = pl.pallas_call(
        functools.partial(share_kernel, **known),
        out_shape=pltpu.VMEM((members, NBANDS * members), jnp.float32),
        in_specs=[VMEM] * (1 + groups),
        out_specs=VMEM,
        scratch_shapes=[pltpu.VMEM((groups, groups * slots, SUB, LANES), jnp.float32)],
        compiler_params=PARAMS,
        name="share",
    )(bands, *parts)
    psi, heat = pl.pallas_call(
        functools.partial(means_kernel, **known),
        out_shape=(
            jax.ShapeDtypeStruct((BASINS, SUB, layers), jnp.float32),
            jax.ShapeDtypeStruct((SUB, BASINS), jnp.float32),
        ),
        in_specs=[VMEM] * groups,
        out_specs=(VMEM, VMEM),
        compiler_params=PARAMS,
        name="means",
    )(*parts)
    bit = 1
    while 2 * bit < tiles:
        share = share + exchange(share, "tile", bit)
        bit *= 2
    norm = float((members - 1) * BASINS * layers * (lats // NBANDS))
    covariance = pl.pallas_call(
        functools.partial(unpack_kernel, members=members, scale=1.0 / norm),
        out_shape=jax.ShapeDtypeStruct((NBANDS, members, members), jnp.float32),
        in_specs=[VMEM] * 2,
        out_specs=VMEM,
        compiler_params=PARAMS,
        name="unpack",
    )(share, exchange(share, "tile", bit))
    return (jnp.transpose(psi, (0, 2, 1)), jnp.transpose(heat, (1, 0)), covariance)


def solution(mesh):
    in_specs = (
        P("member", None, "tile", None),
        P("member", None, "tile", None),
        P("member", None, "tile", None),
        P("tile", None),
        P(),
    )
    out_specs = (P(None, None, ("member", "tile")), P(None, ("member", "tile")), P())
    return jax.shard_map(local, mesh=mesh, in_specs=in_specs, out_specs=out_specs, check_vma=False)
```

time: 140 us -> 38.8 us (0.28)
  blocking collectives: 58 us -> 0 us
  local copies, waits for them, and re-layouts: 18.4 us -> 0.01 us
  waiting for transfers between devices: 32.4 us -> 15 us
  starting transfers between devices: 0.04 us -> 15.9 us
  between operations: 14.2 us -> 0.71 us
  matrix products: 11.3 us -> 0 us
  Pallas kernels: 0 us -> 6.82 us
  other arithmetic: 4.26 us -> 0.17 us
    psum x1 -> x0, blocking collectives: 38.9 us -> none  [local(): covariance = lax.psum(local_cov, ('member', 'tile'))]
    reduce_scatter x1 -> x0, waiting for transfers between devices: 32.4 us -> none  [local(): lax.psum_scatter(regrouped, 'tile', scatter_dimension=2, tiled=True)]
    all_to_all x1 -> x0, blocking collectives: 19.1 us -> none  [local(): lax.all_to_all(partial_value, 'member', split_axis=2, concat_axis=0, tile...]
    ppermute x0 -> x12, starting transfers between devices: none -> 15.9 us  [exchange(): return lax.ppermute(value, axis, [(i, i ^ bit) for i in range(size)])]
    ppermute x0 -> x12, waiting for transfers between devices: none -> 15 us  [exchange(): return lax.ppermute(value, axis, [(i, i ^ bit) for i in range(size)])]
    dot_general x4 -> x0, matrix products: 11.3 us -> none  [the longest x1 9.66 us: local(): jnp.einsum('mkxl,bxl->mbkl', northward_volume_carriage, region_indicator_...]
    pallas_call x0 -> x5, Pallas kernels: none -> 6.82 us  [the longest x1 3.48 us: local(): pl.pallas_call(functools.partial(partial_kernel, **sizes), out_shape=(ear...]
    div x4 -> x0, local copies, waits for them, and re-layouts: 5.67 us -> none  [the longest x1 5.26 us: local(): jnp.einsum('mkxl,bxl->mbkl', northward_volume_carriage, region_indicator_...]
  transfers between devices with their start and end apart: 1 -> 12, of which waited for: 1 -> 10; matrix products, arithmetic and copies ran while one was open for 0% -> 0% of each run, Pallas kernels for 0% -> 4%
where the time goes in v2:
time: 38.8 us; the launch traced here: 38.6 us
  starting transfers between devices  15.9 us (41%)
  waiting for transfers between devices  15 us (39%)
  Pallas kernels  6.82 us (18%)
  between operations  0.71 us (2%)
    ppermute x12, starting transfers between devices, exchange(): return lax.ppermute(value, axis, [(i, i ^ bit) for i in range(size)])  15.9 us
    ppermute x12, waiting for transfers between devices, exchange(): return lax.ppermute(value, axis, [(i, i ^ bit) for i in range(size)])  15 us
    pallas_call x1, Pallas kernels, local(): pl.pallas_call(functools.partial(partial_kernel, **sizes), out_shape=(ear...  3.48 us
    pallas_call x1, Pallas kernels, local(): pl.pallas_call(functools.partial(share_kernel, **known), out_shape=pltpu....  1.06 us
    pallas_call x1, Pallas kernels, local(): pl.pallas_call(functools.partial(means_kernel, **known), out_shape=(jax.S...  0.87 us
  transfers between devices with their start and end apart: 12, of which 10 were waited for; matrix products, arithmetic and copies ran while one was open for 0% of the time, Pallas kernels for 4%

profile of v2, /device:TPU:0, one launch (start us, length us, event | category | flops | bytes accessed | tf_op | source)
XLA Modules:
  0.0 38.6 jit_solution(9903604574988575770)
XLA Ops:
  0.6 0.1 cosine_multiply_fusion.spacing_ref
  0.7 3.5 %partial.1 = (f32[4,10,8,128]{3,2,1,0:T(8,128)S(1)}, f32[4,10,8,128]{3,2,1,0:T(8,128)S(1)}, f32[4,11,8,128]{3,2,1,0:T(8,128)S(1)}, f32[4,11,8,128]{3,2,1,0:T(8,128)S(1)}) custom-call(f32[1024,128]{1,0:T(8,128)} %bitcast.63, f32[1024,128]{1,0:T(8,128)} %bitcast.64, f32[1024,128]{1,0:T(8,128)} %bitcast.65, s32[8,256]{1,0:T(8,128)} %region_ref.1, ...), custom_call_target="tpu_custom_call" | custom-call | tf_op jit(solution)/shard_map/partial/pallas_call | solution.py:320
  4.2 0.6 %collective-permute-start = (f32[4,10,8,128]{3,2,1,0:T(8,128)S(1)}, f32[4,10,8,128]{3,2,1,0:T(8,128)S(1)}, u32[]{:S(2)}, u32[]{:S(2)}) collective-permute-start(f32[4,10,8,128]{3,2,1,0:T(8,128)S(1)} %get-tuple-element.10), channel_id=1, source_target_pairs={{0,1},{1,0},{2,3},{3,2},{4,5},{5,4},{6,7},{7,6},{8,9},{9,8},{10,11... | collective-permute-start | bytes 491528 | tf_op jit(solution)/shard_map/ppermute | solution.py:263
  4.7 0.1 collective-permute-start.3
  4.8 0.9 %collective-permute-done.order_ref = f32[4,10,8,128]{3,2,1,0:T(8,128)S(1)} collective-permute-done((f32[4,10,8,128]{3,2,1,0:T(8,128)S(1)}, f32[4,10,8,128]{3,2,1,0:T(8,128)S(1)}, u32[]{:S(2)}, u32[]{:S(2)}) %collective-permute-start) | collective-permute-done | bytes 163872 | tf_op jit(solution)/shard_map/ppermute | solution.py:263
  5.8 3.0 %collective-permute-start.1 = (f32[2,10,8,128]{3,2,1,0:T(8,128)S(1)}, f32[2,10,8,128]{3,2,1,0:T(8,128)S(1)}, u32[]{:S(2)}, u32[]{:S(2)}) collective-permute-start(f32[2,10,8,128]{3,2,1,0:T(8,128)S(1)} %fusion.1), channel_id=1, source_target_pairs={{0,2},{1,3},{2,0},{3,1},{4,6},{5,7},{6,4},{7,5},{8,10},{9,11},{10,... | collective-permute-start | bytes 245768 | tf_op jit(solution)/shard_map/ppermute | solution.py:263
  8.8 0.0 collective-permute-done.3
  8.8 0.2 collective-permute-start.4
  9.0 2.7 %collective-permute-done.1 = f32[2,10,8,128]{3,2,1,0:T(8,128)S(1)} collective-permute-done((f32[2,10,8,128]{3,2,1,0:T(8,128)S(1)}, f32[2,10,8,128]{3,2,1,0:T(8,128)S(1)}, u32[]{:S(2)}, u32[]{:S(2)}) %collective-permute-start.1) | collective-permute-done | bytes 81952 | tf_op jit(solution)/shard_map/ppermute | solution.py:263
  11.7 2.9 %collective-permute-start.2 = (f32[1,10,8,128]{3,2,1,0:T(8,128)S(1)}, f32[1,10,8,128]{3,2,1,0:T(8,128)S(1)}, u32[]{:S(2)}, u32[]{:S(2)}) collective-permute-start(f32[1,10,8,128]{3,2,1,0:T(8,128)S(1)} %bitcast_add_fusion.4), channel_id=1, source_target_pairs={{0,4},{1,5},{2,6},{3,7},{4,0},{5,1},{6,2},{7,3},{8,12},{9,13},{10,... | collective-permute-start | bytes 122888 | tf_op jit(solution)/shard_map/ppermute | solution.py:263
  14.6 0.0 collective-permute-done.4
  14.6 1.8 %collective-permute-start.5 = (f32[1,11,8,128]{3,2,1,0:T(8,128)S(1)}, f32[1,11,8,128]{3,2,1,0:T(8,128)S(1)}, u32[]{:S(2)}, u32[]{:S(2)}) collective-permute-start(f32[1,11,8,128]{3,2,1,0:T(8,128)S(1)} %bitcast_add_fusion.2), channel_id=1, source_target_pairs={{0,4},{1,5},{2,6},{3,7},{4,0},{5,1},{6,2},{7,3},{8,12},{9,13},{10,... | collective-permute-start | bytes 135176 | tf_op jit(solution)/shard_map/ppermute | solution.py:263
  16.4 0.2 collective-permute-done.2
  16.6 3.0 %collective-permute-done.5 = f32[1,11,8,128]{3,2,1,0:T(8,128)S(1)} collective-permute-done((f32[1,11,8,128]{3,2,1,0:T(8,128)S(1)}, f32[1,11,8,128]{3,2,1,0:T(8,128)S(1)}, u32[]{:S(2)}, u32[]{:S(2)}) %collective-permute-start.5) | collective-permute-done | bytes 45088 | tf_op jit(solution)/shard_map/ppermute | solution.py:263
  19.7 0.0 copy-start
  19.7 2.5 %collective-permute-start.8 = (f32[21,8,128]{2,1,0:T(8,128)S(1)}, f32[21,8,128]{2,1,0:T(8,128)S(1)}, u32[]{:S(2)}, u32[]{:S(2)}) collective-permute-start(f32[21,8,128]{2,1,0:T(8,128)S(1)} %pad_maximum_fusion.refs_0_.refs_1_), channel_id=1, source_target_pairs={{0,24},{8,16},{16,8},{24,0},{1,25},{9,17},{17,9},{25,1},{2,26},{10... | collective-permute-start | bytes 258056 | tf_op jit(solution)/shard_map/ppermute | solution.py:263
  22.2 0.5 %collective-permute-start.7 = (f32[21,8,128]{2,1,0:T(8,128)S(1)}, f32[21,8,128]{2,1,0:T(8,128)S(1)}, u32[]{:S(2)}, u32[]{:S(2)}) collective-permute-start(f32[21,8,128]{2,1,0:T(8,128)S(1)} %pad_maximum_fusion.refs_0_.refs_1_), channel_id=1, source_target_pairs={{0,16},{8,24},{16,0},{24,8},{1,17},{9,25},{17,1},{25,9},{2,18},{10... | collective-permute-start | bytes 258056 | tf_op jit(solution)/shard_map/ppermute | solution.py:263
  22.7 0.5 %collective-permute-start.6 = (f32[21,8,128]{2,1,0:T(8,128)S(1)}, f32[21,8,128]{2,1,0:T(8,128)S(1)}, u32[]{:S(2)}, u32[]{:S(2)}) collective-permute-start(f32[21,8,128]{2,1,0:T(8,128)S(1)} %pad_maximum_fusion.refs_0_.refs_1_), channel_id=1, source_target_pairs={{0,8},{8,0},{16,24},{24,16},{1,9},{9,1},{17,25},{25,17},{2,10},{10... | collective-permute-start | bytes 258056 | tf_op jit(solution)/shard_map/ppermute | solution.py:263
  23.2 0.0 copy-done
  23.3 0.7 %bands.1.refs_0_ = bf16[4,256,128]{2,1,0:T(8,128)(2,1)S(1)} custom-call(s32[256]{0:T(256)S(1)} %copy-done, f32[4,10,8,128]{3,2,1,0:T(8,128)S(1)} %collective-permute-done.order_ref), custom_call_target="tpu_custom_call" | custom-call | tf_op jit(solution)/shard_map/bands/pallas_call | solution.py:336
  23.9 1.2 %collective-permute-done.8.refs_3_.refs_4_ = f32[21,8,128]{2,1,0:T(8,128)S(1)} collective-permute-done((f32[21,8,128]{2,1,0:T(8,128)S(1)}, f32[21,8,128]{2,1,0:T(8,128)S(1)}, u32[]{:S(2)}, u32[]{:S(2)}) %collective-permute-start.8) | collective-permute-done | bytes 86048 | tf_op jit(solution)/shard_map/ppermute | solution.py:263
  25.1 1.5 %collective-permute-done.7.refs_2_.refs_3_ = f32[21,8,128]{2,1,0:T(8,128)S(1)} collective-permute-done((f32[21,8,128]{2,1,0:T(8,128)S(1)}, f32[21,8,128]{2,1,0:T(8,128)S(1)}, u32[]{:S(2)}, u32[]{:S(2)}) %collective-permute-start.7) | collective-permute-done | bytes 86048 | tf_op jit(solution)/shard_map/ppermute | solution.py:263
  26.7 0.5 %collective-permute-done.6.refs_1_.refs_2_ = f32[21,8,128]{2,1,0:T(8,128)S(1)} collective-permute-done((f32[21,8,128]{2,1,0:T(8,128)S(1)}, f32[21,8,128]{2,1,0:T(8,128)S(1)}, u32[]{:S(2)}, u32[]{:S(2)}) %collective-permute-start.6) | collective-permute-done | bytes 86048 | tf_op jit(solution)/shard_map/ppermute | solution.py:263
  27.2 1.1 %share.1 = f32[16,256]{1,0:T(8,128)S(1)} custom-call(bf16[4,256,128]{2,1,0:T(8,128)(2,1)S(1)} %bands.1.refs_0_, f32[21,8,128]{2,1,0:T(8,128)S(1)} %pad_maximum_fusion.refs_0_.refs_1_, f32[21,8,128]{2,1,0:T(8,128)S(1)} %collective-permute-done.6.refs_1_.refs_2_, f32[21,8,128]{2,1,0:T(8,128)S(1)} %collective-permute-done.7.refs_2_.refs_3_, ...), custom_call_target="tpu_custom_call" | custom-call | tf_op jit(solution)/shard_map/share/pallas_call | solution.py:353
  28.3 0.0 collective-permute-start.9
  28.3 1.2 %collective-permute-done.9 = f32[16,256]{1,0:T(8,128)S(1)} collective-permute-done((f32[16,256]{1,0:T(8,128)S(1)}, f32[16,256]{1,0:T(8,128)S(1)}, u32[]{:S(2)}, u32[]{:S(2)}) %collective-permute-start.9) | collective-permute-done | bytes 16416 | tf_op jit(solution)/shard_map/ppermute | solution.py:263
  29.5 2.1 %collective-permute-start.10 = (f32[16,256]{1,0:T(8,128)S(1)}, f32[16,256]{1,0:T(8,128)S(1)}, u32[]{:S(2)}, u32[]{:S(2)}) collective-permute-start(f32[16,256]{1,0:T(8,128)S(1)} %add.141), channel_id=1, source_target_pairs={{0,2},{1,3},{2,0},{3,1},{4,6},{5,7},{6,4},{7,5},{8,10},{9,11},{10,... | collective-permute-start | bytes 49160 | tf_op jit(solution)/shard_map/ppermute | solution.py:263
  31.5 1.7 %collective-permute-done.10 = f32[16,256]{1,0:T(8,128)S(1)} collective-permute-done((f32[16,256]{1,0:T(8,128)S(1)}, f32[16,256]{1,0:T(8,128)S(1)}, u32[]{:S(2)}, u32[]{:S(2)}) %collective-permute-start.10) | collective-permute-done | bytes 16416 | tf_op jit(solution)/shard_map/ppermute | solution.py:263
  33.2 1.8 %collective-permute-start.11 = (f32[16,256]{1,0:T(8,128)S(1)}, f32[16,256]{1,0:T(8,128)S(1)}, u32[]{:S(2)}, u32[]{:S(2)}) collective-permute-start(f32[16,256]{1,0:T(8,128)S(1)} %add.142.refs_0_), channel_id=1, source_target_pairs={{0,4},{1,5},{2,6},{3,7},{4,0},{5,1},{6,2},{7,3},{8,12},{9,13},{10,... | collective-permute-start | bytes 49160 | tf_op jit(solution)/shard_map/ppermute | solution.py:263
  35.0 0.9 %means.1 = (f32[10,8,16]{2,1,0:T(8,128)}, f32[8,10]{1,0:T(8,128)}) custom-call(f32[21,8,128]{2,1,0:T(8,128)S(1)} %pad_maximum_fusion.refs_0_.refs_1_, f32[21,8,128]{2,1,0:T(8,128)S(1)} %collective-permute-done.6.refs_1_.refs_2_, f32[21,8,128]{2,1,0:T(8,128)S(1)} %collective-permute-done.7.refs_2_.refs_3_, ...), custom_call_target="tpu_custom_call" | custom-call | tf_op jit(solution)/shard_map/means/pallas_call | solution.py:362
  35.9 2.0 %collective-permute-done.11.refs_1_ = f32[16,256]{1,0:T(8,128)S(1)} collective-permute-done((f32[16,256]{1,0:T(8,128)S(1)}, f32[16,256]{1,0:T(8,128)S(1)}, u32[]{:S(2)}, u32[]{:S(2)}) %collective-permute-start.11) | collective-permute-done | bytes 16416 | tf_op jit(solution)/shard_map/ppermute | solution.py:263
  37.9 0.8 %unpack.1 = f32[16,16,16]{2,1,0:T(8,128)} custom-call(f32[16,256]{1,0:T(8,128)S(1)} %add.142.refs_0_, f32[16,256]{1,0:T(8,128)S(1)} %collective-permute-done.11.refs_1_), custom_call_target="tpu_custom_call" | custom-call | tf_op jit(solution)/shard_map/unpack/pallas_call | solution.py:378
  (11 shorter events, 0.1 us)
Async XLA Ops:
  4.2 1.6 %collective-permute-start = (f32[4,10,8,128]{3,2,1,0:T(8,128)S(1)}, f32[4,10,8,128]{3,2,1,0:T(8,128)S(1)}, u32[]{:S(2)}, u32[]{:S(2)}) collective-permute-start(f32[4,10,8,128]{3,2,1,0:T(8,128)S(1)} %get-tuple-element.10), channel_id=1, source_target_pairs={{0,1},{1,0},{2,3},{3,2},{4,5},{5,4},{6,7},{7,6},{8,9},{9,8},{10,11... | collective-permute-start | bytes 491528 | tf_op jit(solution)/shard_map/ppermute | solution.py:263
  4.7 4.1 %collective-permute-start.3 = (f32[4,11,8,128]{3,2,1,0:T(8,128)S(1)}, f32[4,11,8,128]{3,2,1,0:T(8,128)S(1)}, u32[]{:S(2)}, u32[]{:S(2)}) collective-permute-start(f32[4,11,8,128]{3,2,1,0:T(8,128)S(1)} %get-tuple-element.12), channel_id=1, source_target_pairs={{0,1},{1,0},{2,3},{3,2},{4,5},{5,4},{6,7},{7,6},{8,9},{9,8},{10,11... | collective-permute-start | bytes 540680 | tf_op jit(solution)/shard_map/ppermute | solution.py:263
  5.8 5.9 %collective-permute-start.1 = (f32[2,10,8,128]{3,2,1,0:T(8,128)S(1)}, f32[2,10,8,128]{3,2,1,0:T(8,128)S(1)}, u32[]{:S(2)}, u32[]{:S(2)}) collective-permute-start(f32[2,10,8,128]{3,2,1,0:T(8,128)S(1)} %fusion.1), channel_id=1, source_target_pairs={{0,2},{1,3},{2,0},{3,1},{4,6},{5,7},{6,4},{7,5},{8,10},{9,11},{10,... | collective-permute-start | bytes 245768 | tf_op jit(solution)/shard_map/ppermute | solution.py:263
  8.8 5.8 %collective-permute-start.4 = (f32[2,11,8,128]{3,2,1,0:T(8,128)S(1)}, f32[2,11,8,128]{3,2,1,0:T(8,128)S(1)}, u32[]{:S(2)}, u32[]{:S(2)}) collective-permute-start(f32[2,11,8,128]{3,2,1,0:T(8,128)S(1)} %fusion), channel_id=1, source_target_pairs={{0,2},{1,3},{2,0},{3,1},{4,6},{5,7},{6,4},{7,5},{8,10},{9,11},{10,... | collective-permute-start | bytes 270344 | tf_op jit(solution)/shard_map/ppermute | solution.py:263
  11.7 4.9 %collective-permute-start.2 = (f32[1,10,8,128]{3,2,1,0:T(8,128)S(1)}, f32[1,10,8,128]{3,2,1,0:T(8,128)S(1)}, u32[]{:S(2)}, u32[]{:S(2)}) collective-permute-start(f32[1,10,8,128]{3,2,1,0:T(8,128)S(1)} %bitcast_add_fusion.4), channel_id=1, source_target_pairs={{0,4},{1,5},{2,6},{3,7},{4,0},{5,1},{6,2},{7,3},{8,12},{9,13},{10,... | collective-permute-start | bytes 122888 | tf_op jit(solution)/shard_map/ppermute | solution.py:263
  14.6 5.0 %collective-permute-start.5 = (f32[1,11,8,128]{3,2,1,0:T(8,128)S(1)}, f32[1,11,8,128]{3,2,1,0:T(8,128)S(1)}, u32[]{:S(2)}, u32[]{:S(2)}) collective-permute-start(f32[1,11,8,128]{3,2,1,0:T(8,128)S(1)} %bitcast_add_fusion.2), channel_id=1, source_target_pairs={{0,4},{1,5},{2,6},{3,7},{4,0},{5,1},{6,2},{7,3},{8,12},{9,13},{10,... | collective-permute-start | bytes 135176 | tf_op jit(solution)/shard_map/ppermute | solution.py:263
  19.7 3.6 %copy-start = (s32[256]{0:T(256)S(1)}, s32[256]{0:T(256)}, u32[]{:S(2)}) copy-start(s32[256]{0:T(256)} %zone_ref.1) | copy-start | bytes 3076
  19.7 5.4 %collective-permute-start.8 = (f32[21,8,128]{2,1,0:T(8,128)S(1)}, f32[21,8,128]{2,1,0:T(8,128)S(1)}, u32[]{:S(2)}, u32[]{:S(2)}) collective-permute-start(f32[21,8,128]{2,1,0:T(8,128)S(1)} %pad_maximum_fusion.refs_0_.refs_1_), channel_id=1, source_target_pairs={{0,24},{8,16},{16,8},{24,0},{1,25},{9,17},{17,9},{25,1},{2,26},{10... | collective-permute-start | bytes 258056 | tf_op jit(solution)/shard_map/ppermute | solution.py:263
  22.2 4.5 %collective-permute-start.7 = (f32[21,8,128]{2,1,0:T(8,128)S(1)}, f32[21,8,128]{2,1,0:T(8,128)S(1)}, u32[]{:S(2)}, u32[]{:S(2)}) collective-permute-start(f32[21,8,128]{2,1,0:T(8,128)S(1)} %pad_maximum_fusion.refs_0_.refs_1_), channel_id=1, source_target_pairs={{0,16},{8,24},{16,0},{24,8},{1,17},{9,25},{17,1},{25,9},{2,18},{10... | collective-permute-start | bytes 258056 | tf_op jit(solution)/shard_map/ppermute | solution.py:263
  22.7 4.5 %collective-permute-start.6 = (f32[21,8,128]{2,1,0:T(8,128)S(1)}, f32[21,8,128]{2,1,0:T(8,128)S(1)}, u32[]{:S(2)}, u32[]{:S(2)}) collective-permute-start(f32[21,8,128]{2,1,0:T(8,128)S(1)} %pad_maximum_fusion.refs_0_.refs_1_), channel_id=1, source_target_pairs={{0,8},{8,0},{16,24},{24,16},{1,9},{9,1},{17,25},{25,17},{2,10},{10... | collective-permute-start | bytes 258056 | tf_op jit(solution)/shard_map/ppermute | solution.py:263
  28.3 1.2 %collective-permute-start.9 = (f32[16,256]{1,0:T(8,128)S(1)}, f32[16,256]{1,0:T(8,128)S(1)}, u32[]{:S(2)}, u32[]{:S(2)}) collective-permute-start(f32[16,256]{1,0:T(8,128)S(1)} %share.1), channel_id=1, source_target_pairs={{0,1},{1,0},{2,3},{3,2},{4,5},{5,4},{6,7},{7,6},{8,9},{9,8},{10,11... | collective-permute-start | bytes 49160 | tf_op jit(solution)/shard_map/ppermute | solution.py:263
  29.5 3.8 %collective-permute-start.10 = (f32[16,256]{1,0:T(8,128)S(1)}, f32[16,256]{1,0:T(8,128)S(1)}, u32[]{:S(2)}, u32[]{:S(2)}) collective-permute-start(f32[16,256]{1,0:T(8,128)S(1)} %add.141), channel_id=1, source_target_pairs={{0,2},{1,3},{2,0},{3,1},{4,6},{5,7},{6,4},{7,5},{8,10},{9,11},{10,... | collective-permute-start | bytes 49160 | tf_op jit(solution)/shard_map/ppermute | solution.py:263
  33.2 4.6 %collective-permute-start.11 = (f32[16,256]{1,0:T(8,128)S(1)}, f32[16,256]{1,0:T(8,128)S(1)}, u32[]{:S(2)}, u32[]{:S(2)}) collective-permute-start(f32[16,256]{1,0:T(8,128)S(1)} %add.142.refs_0_), channel_id=1, source_target_pairs={{0,4},{1,5},{2,6},{3,7},{4,0},{5,1},{6,2},{7,3},{8,12},{9,13},{10,... | collective-permute-start | bytes 49160 | tf_op jit(solution)/shard_map/ppermute | solution.py:263

commit v3 on v2

--- a/solution.py
+++ b/solution.py
@@ -8,12 +8,12 @@
 from jax.experimental.pallas import tpu as pltpu
 from jax.sharding import PartitionSpec as P
 
+
 BASINS = 10
 NBANDS = 16
 LANES = 128
 SUB = 8
 HEAT_LANES = 16
-HIGHEST = lax.Precision.HIGHEST
 
 
 def metric_factor(lats):
@@ -45,28 +45,17 @@
     return parts
 
 
-def partial_kernel(v_ref, h_ref, w_ref, region_ref, spacing_ref, keep0_ref, send0_ref,
-                   keep1_ref, send1_ref, buf, small, sems, small_sem,
-                   *, half, members_here, layers, columns, groups, tiles):
-    feats, rest = split_features(layers, members_here)
+def basin_sums(buf, region, spacing, heat_ref, keep_ref, send_ref,
+               *, late, half, members_here, layers, columns, groups, tiles):
+    feats, _ = split_features(layers, members_here)
     core = lax.axis_index("tile") % 2
     halves = layers // SUB
     lshift = log2(layers)
     slots = members_here + 1
     pieces = LANES // SUB
     blocks = 2 * half
-    inputs = (v_ref, h_ref, w_ref)
     per = layers * blocks * columns
-
-    def fetch(m, a):
-        part = pl.ds(m * per, per)
-        return pltpu.make_async_copy(inputs[a].at[part], buf.at[a, part], sems.at[m, a])
-
-    labels = pltpu.make_async_copy(region_ref, small, small_sem)
-    labels.start()
-    for m in range(members_here):
-        for a in range(3):
-            fetch(m, a).start()
+    mine = range(half, blocks) if late else range(half)
     rows = iota((feats, feats), 0)
     cols = iota((feats, feats), 1)
     running = ((rows >> lshift) == (cols >> lshift)) & (cols <= rows)
@@ -84,32 +73,26 @@
             preferred_element_type=jnp.float32,
         )
 
-    def put(late, place, slot, even, odd):
-        keep_ref, send_ref = (keep1_ref, send1_ref) if late else (keep0_ref, send0_ref)
+    def put(place, slot, even, odd):
         keep_ref[place, slot] = jnp.where(core == 0, even, odd)
         send_ref[place, slot] = jnp.where(core == 0, odd, even)
 
     def put_block(lb, s, value):
         for row in range(0, pieces, 2):
             group, tile = divmod(lb * pieces + row, tiles)
-            late = group >= groups // 2
-            slot = (group - late * (groups // 2)) * slots + s
+            slot = (group % (groups // 2)) * slots + s
             even = value[row * SUB : (row + 1) * SUB]
-            put(late, tile // 2, slot, even, value[(row + 1) * SUB : (row + 2) * SUB])
+            put(tile // 2, slot, even, value[(row + 1) * SUB : (row + 2) * SUB])
 
     warm = [[None] * columns for _ in range(blocks)]
     extra = [[] for _ in range(blocks)]
-    labels.wait()
-    region, spacing = small[...], spacing_ref[...]
 
     def label(lb, x):
         line = region[x : x + 1, lb * LANES : (lb + 1) * LANES]
         return jnp.broadcast_to(line, (SUB, LANES))
 
     for m in range(members_here):
-        for a in range(3):
-            fetch(m, a).wait()
-        for lb in range(blocks):
+        for lb in mine:
             scale = spacing[:, lb * LANES : (lb + 1) * LANES]
             acc = [[None] * halves for _ in range(BASINS)]
             for x in range(columns):
@@ -132,8 +115,8 @@
             put_block(lb, m, stream[:LANES].T)
             extra[lb].append(stream[LANES:])
     span = tiles * SUB
-    heat = None
-    for lb in range(blocks):
+    heat = heat_ref[...] if late else None
+    for lb in mine:
         put_block(lb, members_here, jnp.concatenate(extra[lb], 0).T)
         basin_heat = []
         for b in range(BASINS):
@@ -145,13 +128,38 @@
         block = select(gather, jnp.concatenate(basin_heat, 0))
         for p in range(LANES // span):
             moved = block if p == 0 else pltpu.roll(block, LANES - p * span, 1)
-            mine = (heat_group == lb * (LANES // span) + p) & (heat_lat < span)
-            part = jnp.where(mine, moved, 0.0)
+            keep = (heat_group == lb * (LANES // span) + p) & (heat_lat < span)
+            part = jnp.where(keep, moved, 0.0)
             heat = part if heat is None else heat + part
+    if not late:
+        heat_ref[...] = heat
+        return
     heat = heat.T
     for t in range(0, tiles, 2):
         even = heat[t * SUB : (t + 1) * SUB]
-        put(True, t // 2, slots * (groups // 2), even, heat[(t + 1) * SUB : (t + 2) * SUB])
+        put(t // 2, slots * (groups // 2), even, heat[(t + 1) * SUB : (t + 2) * SUB])
+
+
+def first_kernel(v_ref, h_ref, w_ref, region_ref, spacing_ref, keep_ref, send_ref, heat_ref,
+                 data_ref, small_ref, sems, small_sem, **sizes):
+    copies = [pltpu.make_async_copy(region_ref, small_ref, small_sem)]
+    for a, ref in enumerate((v_ref, h_ref, w_ref)):
+        copies.append(pltpu.make_async_copy(ref, data_ref.at[a], sems.at[a]))
+    for copy in copies:
+        copy.start(priority=1)
+    for copy in copies:
+        copy.wait()
+    basin_sums(
+        data_ref, small_ref[...], spacing_ref[...], heat_ref, keep_ref, send_ref,
+        late=False, **sizes,
+    )
+
+
+def second_kernel(data_ref, region_ref, spacing_ref, heat_ref, keep_ref, send_ref, **sizes):
+    basin_sums(
+        data_ref, region_ref[...], spacing_ref[...], heat_ref, keep_ref, send_ref,
+        late=True, **sizes,
+    )
 
 
 def bands_kernel(zone_ref, order_ref, out_ref, *, members, groups, tiles):
@@ -175,7 +183,7 @@
     bands_ref = refs[0]
     parts = refs[1 : 1 + groups]
     cov_ref, all_ref = refs[1 + groups :]
-    feats, rest = split_features(layers, members_here)
+    _, rest = split_features(layers, members_here)
     slots = members_here + 1
     members = members_here * groups
     mine = lax.axis_index("member")
@@ -200,8 +208,11 @@
         head = jnp.concatenate([a - head_mean for a in heads], 0)
         tail = jnp.concatenate([a - tail_mean for a in tails], 0)
         both = jnp.concatenate([head, tail], 1)
+        high = both.astype(jnp.bfloat16)
+        low = (both - high.astype(jnp.float32)).astype(jnp.bfloat16)
         gram = lax.dot_general(
-            both, both, last, precision=HIGHEST, preferred_element_type=jnp.float32
+            jnp.concatenate([high, high, low], 1), jnp.concatenate([high, low, high], 1),
+            last, preferred_element_type=jnp.float32,
         )
         summed = jnp.concatenate(
             [
@@ -223,7 +234,7 @@
 def means_kernel(*refs, members_here, layers, groups):
     parts = refs[:groups]
     psi_ref, heat_ref = refs[groups:]
-    feats, rest = split_features(layers, members_here)
+    _, rest = split_features(layers, members_here)
     slots = members_here + 1
     members = members_here * groups
     mine = lax.axis_index("member")
@@ -263,16 +274,18 @@
     return lax.ppermute(value, axis, [(i, i ^ bit) for i in range(size)])
 
 
-def halve(keep, got, tile, bit):
-    shape = (keep.shape[0] // 2, 2) + keep.shape[1:]
-    keep, got = keep.reshape(shape), got.reshape(shape)
+def halve(chunks, tile, bit):
     mine = (tile // bit) % 2
-    send, keep = (
-        lax.dynamic_index_in_dim(keep, side, 1, False)
-        + lax.dynamic_index_in_dim(got, side, 1, False)
-        for side in (1 - mine, mine)
-    )
-    return keep, exchange(send, "tile", bit)
+    keeps, sends = [], []
+    for keep, got in chunks:
+        shape = (keep.shape[0] // 2, 2) + keep.shape[1:]
+        keep, got = keep.reshape(shape), got.reshape(shape)
+        for side, out in ((1 - mine, sends), (mine, keeps)):
+            out.append(
+                lax.dynamic_index_in_dim(keep, side, 1, False)
+                + lax.dynamic_index_in_dim(got, side, 1, False)
+            )
+    return [(keep, exchange(send, "tile", bit)) for keep, send in zip(keeps, sends)]
 
 
 ANY = pl.BlockSpec(memory_space=pl.ANY)
@@ -304,7 +317,6 @@
         half=half, members_here=members_here, layers=layers, columns=columns,
         groups=groups, tiles=tiles,
     )
-    inputs = (northward_speed_field, level_depth_extent, potential_warmth_anomaly)
     blocked = [
         pltpu.with_memory_space_constraint(
             x.reshape(rows // columns, columns, 2 * half, LANES)
@@ -317,21 +329,30 @@
     labels = pltpu.with_memory_space_constraint(ocean_region_label, pltpu.MemorySpace.HBM)
     early = pltpu.VMEM((tiles // 2, count * slots, SUB, LANES), jnp.float32)
     late = pltpu.VMEM((tiles // 2, count * slots + 1, SUB, LANES), jnp.float32)
-    keep0, send0, keep1, send1 = pl.pallas_call(
-        functools.partial(partial_kernel, **sizes),
-        out_shape=(early, early, late, late),
-        in_specs=[ANY] * 4 + [VMEM],
-        out_specs=(VMEM,) * 4,
-        scratch_shapes=[
+    keep0, send0, heat, data, labels = pl.pallas_call(
+        functools.partial(first_kernel, **sizes),
+        out_shape=(
+            early,
+            early,
+            pltpu.VMEM((LANES, LANES), jnp.float32),
             pltpu.VMEM((3, 2 * half * rows, LANES), jnp.float32),
             pltpu.VMEM((columns, lats), jnp.int32),
-            pltpu.SemaphoreType.DMA((members_here, 3)),
-            pltpu.SemaphoreType.DMA(()),
-        ],
-        compiler_params=PARAMS,
-        name="partial",
+        ),
+        in_specs=[ANY] * 4 + [VMEM],
+        out_specs=(VMEM,) * 5,
+        scratch_shapes=[pltpu.SemaphoreType.DMA((3,)), pltpu.SemaphoreType.DMA(())],
+        compiler_params=PARAMS,
+        name="first",
     )(*blocked, labels, spacing)
     got0 = exchange(send0, "tile", 1)
+    keep1, send1 = pl.pallas_call(
+        functools.partial(second_kernel, **sizes),
+        out_shape=(late, late),
+        in_specs=[VMEM] * 4,
+        out_specs=(VMEM, VMEM),
+        compiler_params=PARAMS,
+        name="second",
+    )(data, labels, spacing, heat)
     got1 = exchange(send1, "tile", 1)
     bands = pl.pallas_call(
         functools.partial(bands_kernel, members=members, groups=groups, tiles=tiles),
@@ -345,7 +366,7 @@
     chunks = [(keep0, got0), (keep1, got1)]
     bit = 2
     while bit < tiles:
-        chunks = [halve(keep, got, tile, bit) for keep, got in chunks]
+        chunks = halve(chunks, tile, bit)
         bit *= 2
     owned = jnp.concatenate([(keep + got)[0] for keep, got in chunks], 0)
     parts = [owned] + [exchange(owned, "member", r) for r in range(1, groups)]

time: 38.8 us -> 38.3 us (0.987)
  starting transfers between devices: 15.9 us -> 16.5 us
  waiting for transfers between devices: 15 us -> 14.4 us
  Pallas kernels: 6.82 us -> 6.25 us
    ppermute x12, waiting for transfers between devices: 15 us -> 14.4 us  [exchange(): return lax.ppermute(value, axis, [(i, i ^ bit) for i in range(size)])]
    ppermute x12, starting transfers between devices: 15.9 us -> 16.5 us  [exchange(): return lax.ppermute(value, axis, [(i, i ^ bit) for i in range(size)])]
    pallas_call x1 -> x2, Pallas kernels: 3.48 us -> 3.12 us  [the longest x1 2.25 us: local(): pl.pallas_call(functools.partial(first_kernel, **sizes), out_shape=(early...]
  transfers between devices with their start and end apart: 12 -> 12, of which waited for: 10 -> 9; matrix products, arithmetic and copies ran while one was open for 0% -> 0% of each run, Pallas kernels for 4% -> 6%
where the time goes in v3:
time: 38.3 us; the launch traced here: 38.1 us
  starting transfers between devices  16.5 us (43%)
  waiting for transfers between devices  14.4 us (38%)
  Pallas kernels  6.25 us (16%)
  between operations  0.78 us (2%)
    ppermute x12, starting transfers between devices, exchange(): return lax.ppermute(value, axis, [(i, i ^ bit) for i in range(size)])  16.5 us
    ppermute x12, waiting for transfers between devices, exchange(): return lax.ppermute(value, axis, [(i, i ^ bit) for i in range(size)])  14.4 us
    pallas_call x1, Pallas kernels, local(): pl.pallas_call(functools.partial(first_kernel, **sizes), out_shape=(early...  2.25 us
    pallas_call x1, Pallas kernels, local(): pl.pallas_call(functools.partial(second_kernel, **sizes), out_shape=(late...  0.87 us
    pallas_call x1, Pallas kernels, local(): pl.pallas_call(functools.partial(means_kernel, **known), out_shape=(jax.S...  0.87 us
    pallas_call x1, Pallas kernels, local(): pl.pallas_call(functools.partial(share_kernel, **known), out_shape=pltpu....  0.85 us
  transfers between devices with their start and end apart: 12, of which 9 were waited for; matrix products, arithmetic and copies ran while one was open for 0% of the time, Pallas kernels for 6%

profile of v3, /device:TPU:0, one launch (start us, length us, event | category | flops | bytes accessed | tf_op | source)
XLA Modules:
  0.0 38.1 jit_solution(11030183395639794041)
XLA Ops:
  0.6 0.1 cosine_multiply_fusion.spacing_ref
  0.7 2.2 %first.1 = (f32[4,10,8,128]{3,2,1,0:T(8,128)S(1)}, f32[4,10,8,128]{3,2,1,0:T(8,128)S(1)}, f32[128,128]{1,0:T(8,128)S(1)}, f32[3,1024,128]{2,1,0:T(8,128)S(1)}, s32[8,256]{1,0:T(8,128)S(1)}) custom-call(f32[1024,128]{1,0:T(8,128)} %bitcast.63, f32[1024,128]{1,0:T(8,128)} %bitcast.64, f32[1024,128]{1,0:T(8,128)} %bitcast.65, s32[8,256]{1,0:T(8,128)} %region_ref.1, ...), custom_call_target="tpu_custom_call" | custom-call | tf_op jit(solution)/shard_map/first/pallas_call | solution.py:332
  2.9 0.6 %collective-permute-start = (f32[4,10,8,128]{3,2,1,0:T(8,128)S(1)}, f32[4,10,8,128]{3,2,1,0:T(8,128)S(1)}, u32[]{:S(2)}, u32[]{:S(2)}) collective-permute-start(f32[4,10,8,128]{3,2,1,0:T(8,128)S(1)} %get-tuple-element.13), channel_id=1, source_target_pairs={{0,1},{1,0},{2,3},{3,2},{4,5},{5,4},{6,7},{7,6},{8,9},{9,8},{10,11... | collective-permute-start | bytes 491528 | tf_op jit(solution)/shard_map/ppermute | solution.py:274
  3.5 0.0 copy-start
  3.5 0.9 %second.1 = (f32[4,11,8,128]{3,2,1,0:T(8,128)S(1)}, f32[4,11,8,128]{3,2,1,0:T(8,128)S(1)}) custom-call(f32[3,1024,128]{2,1,0:T(8,128)S(1)} %get-tuple-element.14.data_ref, s32[8,256]{1,0:T(8,128)S(1)} %get-tuple-element.15.region_ref, f32[1,256]{1,0:T(1,128)S(1)} %cosine_multiply_fusion.spacing_ref, f32[128,128]{1,0:T(8,128)S(1)} %get-tuple-element.16.heat_ref), custom_call_target="tpu_custom_call" | custom-call | tf_op jit(solution)/shard_map/second/pallas_call | solution.py:348
  4.4 0.1 collective-permute-start.3
  4.5 0.0 collective-permute-done.order_ref
  4.6 3.0 %collective-permute-start.1 = (f32[2,10,8,128]{3,2,1,0:T(8,128)S(1)}, f32[2,10,8,128]{3,2,1,0:T(8,128)S(1)}, u32[]{:S(2)}, u32[]{:S(2)}) collective-permute-start(f32[2,10,8,128]{3,2,1,0:T(8,128)S(1)} %fusion.1), channel_id=1, source_target_pairs={{0,2},{1,3},{2,0},{3,1},{4,6},{5,7},{6,4},{7,5},{8,10},{9,11},{10,... | collective-permute-start | bytes 245768 | tf_op jit(solution)/shard_map/ppermute | solution.py:274
  7.6 0.0 collective-permute-done.3
  7.7 1.0 %collective-permute-start.4 = (f32[2,11,8,128]{3,2,1,0:T(8,128)S(1)}, f32[2,11,8,128]{3,2,1,0:T(8,128)S(1)}, u32[]{:S(2)}, u32[]{:S(2)}) collective-permute-start(f32[2,11,8,128]{3,2,1,0:T(8,128)S(1)} %fusion), channel_id=1, source_target_pairs={{0,2},{1,3},{2,0},{3,1},{4,6},{5,7},{6,4},{7,5},{8,10},{9,11},{10,... | collective-permute-start | bytes 270344 | tf_op jit(solution)/shard_map/ppermute | solution.py:274
  8.7 1.8 %collective-permute-done.1 = f32[2,10,8,128]{3,2,1,0:T(8,128)S(1)} collective-permute-done((f32[2,10,8,128]{3,2,1,0:T(8,128)S(1)}, f32[2,10,8,128]{3,2,1,0:T(8,128)S(1)}, u32[]{:S(2)}, u32[]{:S(2)}) %collective-permute-start.1) | collective-permute-done | bytes 81952 | tf_op jit(solution)/shard_map/ppermute | solution.py:274
  10.5 2.9 %collective-permute-start.2 = (f32[1,10,8,128]{3,2,1,0:T(8,128)S(1)}, f32[1,10,8,128]{3,2,1,0:T(8,128)S(1)}, u32[]{:S(2)}, u32[]{:S(2)}) collective-permute-start(f32[1,10,8,128]{3,2,1,0:T(8,128)S(1)} %bitcast_add_fusion.4), channel_id=1, source_target_pairs={{0,4},{1,5},{2,6},{3,7},{4,0},{5,1},{6,2},{7,3},{8,12},{9,13},{10,... | collective-permute-start | bytes 122888 | tf_op jit(solution)/shard_map/ppermute | solution.py:274
  13.4 0.0 collective-permute-done.4
  13.4 1.8 %collective-permute-start.5 = (f32[1,11,8,128]{3,2,1,0:T(8,128)S(1)}, f32[1,11,8,128]{3,2,1,0:T(8,128)S(1)}, u32[]{:S(2)}, u32[]{:S(2)}) collective-permute-start(f32[1,11,8,128]{3,2,1,0:T(8,128)S(1)} %bitcast_add_fusion.2), channel_id=1, source_target_pairs={{0,4},{1,5},{2,6},{3,7},{4,0},{5,1},{6,2},{7,3},{8,12},{9,13},{10,... | collective-permute-start | bytes 135176 | tf_op jit(solution)/shard_map/ppermute | solution.py:274
  15.3 0.1 collective-permute-done.2
  15.4 3.0 %collective-permute-done.5 = f32[1,11,8,128]{3,2,1,0:T(8,128)S(1)} collective-permute-done((f32[1,11,8,128]{3,2,1,0:T(8,128)S(1)}, f32[1,11,8,128]{3,2,1,0:T(8,128)S(1)}, u32[]{:S(2)}, u32[]{:S(2)}) %collective-permute-start.5) | collective-permute-done | bytes 45088 | tf_op jit(solution)/shard_map/ppermute | solution.py:274
  18.5 1.6 %collective-permute-start.6 = (f32[21,8,128]{2,1,0:T(8,128)S(1)}, f32[21,8,128]{2,1,0:T(8,128)S(1)}, u32[]{:S(2)}, u32[]{:S(2)}) collective-permute-start(f32[21,8,128]{2,1,0:T(8,128)S(1)} %pad_maximum_fusion.refs_0_.refs_1_), channel_id=1, source_target_pairs={{0,8},{8,0},{16,24},{24,16},{1,9},{9,1},{17,25},{25,17},{2,10},{10... | collective-permute-start | bytes 258056 | tf_op jit(solution)/shard_map/ppermute | solution.py:274
  20.0 1.5 %collective-permute-start.7 = (f32[21,8,128]{2,1,0:T(8,128)S(1)}, f32[21,8,128]{2,1,0:T(8,128)S(1)}, u32[]{:S(2)}, u32[]{:S(2)}) collective-permute-start(f32[21,8,128]{2,1,0:T(8,128)S(1)} %pad_maximum_fusion.refs_0_.refs_1_), channel_id=1, source_target_pairs={{0,16},{8,24},{16,0},{24,8},{1,17},{9,25},{17,1},{25,9},{2,18},{10... | collective-permute-start | bytes 258056 | tf_op jit(solution)/shard_map/ppermute | solution.py:274
  21.6 0.5 %collective-permute-start.8 = (f32[21,8,128]{2,1,0:T(8,128)S(1)}, f32[21,8,128]{2,1,0:T(8,128)S(1)}, u32[]{:S(2)}, u32[]{:S(2)}) collective-permute-start(f32[21,8,128]{2,1,0:T(8,128)S(1)} %pad_maximum_fusion.refs_0_.refs_1_), channel_id=1, source_target_pairs={{0,24},{8,16},{16,8},{24,0},{1,25},{9,17},{17,9},{25,1},{2,26},{10... | collective-permute-start | bytes 258056 | tf_op jit(solution)/shard_map/ppermute | solution.py:274
  22.0 0.0 copy-done
  22.0 0.7 %bands.1.refs_0_ = bf16[4,256,128]{2,1,0:T(8,128)(2,1)S(1)} custom-call(s32[256]{0:T(256)S(1)} %copy-done, f32[4,10,8,128]{3,2,1,0:T(8,128)S(1)} %collective-permute-done.order_ref), custom_call_target="tpu_custom_call" | custom-call | tf_op jit(solution)/shard_map/bands/pallas_call | solution.py:357
  22.7 0.3 collective-permute-done.6.refs_1_.refs_2_
  23.0 1.5 %collective-permute-done.7.refs_2_.refs_3_ = f32[21,8,128]{2,1,0:T(8,128)S(1)} collective-permute-done((f32[21,8,128]{2,1,0:T(8,128)S(1)}, f32[21,8,128]{2,1,0:T(8,128)S(1)}, u32[]{:S(2)}, u32[]{:S(2)}) %collective-permute-start.7) | collective-permute-done | bytes 86048 | tf_op jit(solution)/shard_map/ppermute | solution.py:274
  24.5 2.4 %collective-permute-done.8.refs_3_.refs_4_ = f32[21,8,128]{2,1,0:T(8,128)S(1)} collective-permute-done((f32[21,8,128]{2,1,0:T(8,128)S(1)}, f32[21,8,128]{2,1,0:T(8,128)S(1)}, u32[]{:S(2)}, u32[]{:S(2)}) %collective-permute-start.8) | collective-permute-done | bytes 86048 | tf_op jit(solution)/shard_map/ppermute | solution.py:274
  26.9 0.8 %share.1 = f32[16,256]{1,0:T(8,128)S(1)} custom-call(bf16[4,256,128]{2,1,0:T(8,128)(2,1)S(1)} %bands.1.refs_0_, f32[21,8,128]{2,1,0:T(8,128)S(1)} %pad_maximum_fusion.refs_0_.refs_1_, f32[21,8,128]{2,1,0:T(8,128)S(1)} %collective-permute-done.6.refs_1_.refs_2_, f32[21,8,128]{2,1,0:T(8,128)S(1)} %collective-permute-done.7.refs_2_.refs_3_, ...), custom_call_target="tpu_custom_call" | custom-call | tf_op jit(solution)/shard_map/share/pallas_call | solution.py:374
  27.8 0.0 collective-permute-start.9
  27.8 1.2 %collective-permute-done.9 = f32[16,256]{1,0:T(8,128)S(1)} collective-permute-done((f32[16,256]{1,0:T(8,128)S(1)}, f32[16,256]{1,0:T(8,128)S(1)}, u32[]{:S(2)}, u32[]{:S(2)}) %collective-permute-start.9) | collective-permute-done | bytes 16416 | tf_op jit(solution)/shard_map/ppermute | solution.py:274
  29.0 1.7 %collective-permute-start.10 = (f32[16,256]{1,0:T(8,128)S(1)}, f32[16,256]{1,0:T(8,128)S(1)}, u32[]{:S(2)}, u32[]{:S(2)}) collective-permute-start(f32[16,256]{1,0:T(8,128)S(1)} %add.143), channel_id=1, source_target_pairs={{0,2},{1,3},{2,0},{3,1},{4,6},{5,7},{6,4},{7,5},{8,10},{9,11},{10,... | collective-permute-start | bytes 49160 | tf_op jit(solution)/shard_map/ppermute | solution.py:274
  30.7 2.1 %collective-permute-done.10 = f32[16,256]{1,0:T(8,128)S(1)} collective-permute-done((f32[16,256]{1,0:T(8,128)S(1)}, f32[16,256]{1,0:T(8,128)S(1)}, u32[]{:S(2)}, u32[]{:S(2)}) %collective-permute-start.10) | collective-permute-done | bytes 16416 | tf_op jit(solution)/shard_map/ppermute | solution.py:274
  32.7 1.9 %collective-permute-start.11 = (f32[16,256]{1,0:T(8,128)S(1)}, f32[16,256]{1,0:T(8,128)S(1)}, u32[]{:S(2)}, u32[]{:S(2)}) collective-permute-start(f32[16,256]{1,0:T(8,128)S(1)} %add.144.refs_0_), channel_id=1, source_target_pairs={{0,4},{1,5},{2,6},{3,7},{4,0},{5,1},{6,2},{7,3},{8,12},{9,13},{10,... | collective-permute-start | bytes 49160 | tf_op jit(solution)/shard_map/ppermute | solution.py:274
  34.6 0.9 %means.1 = (f32[10,8,16]{2,1,0:T(8,128)}, f32[8,10]{1,0:T(8,128)}) custom-call(f32[21,8,128]{2,1,0:T(8,128)S(1)} %pad_maximum_fusion.refs_0_.refs_1_, f32[21,8,128]{2,1,0:T(8,128)S(1)} %collective-permute-done.6.refs_1_.refs_2_, f32[21,8,128]{2,1,0:T(8,128)S(1)} %collective-permute-done.7.refs_2_.refs_3_, ...), custom_call_target="tpu_custom_call" | custom-call | tf_op jit(solution)/shard_map/means/pallas_call | solution.py:383
  35.5 1.9 %collective-permute-done.11.refs_1_ = f32[16,256]{1,0:T(8,128)S(1)} collective-permute-done((f32[16,256]{1,0:T(8,128)S(1)}, f32[16,256]{1,0:T(8,128)S(1)}, u32[]{:S(2)}, u32[]{:S(2)}) %collective-permute-start.11) | collective-permute-done | bytes 16416 | tf_op jit(solution)/shard_map/ppermute | solution.py:274
  37.4 0.8 %unpack.1 = f32[16,16,16]{2,1,0:T(8,128)} custom-call(f32[16,256]{1,0:T(8,128)S(1)} %add.144.refs_0_, f32[16,256]{1,0:T(8,128)S(1)} %collective-permute-done.11.refs_1_), custom_call_target="tpu_custom_call" | custom-call | tf_op jit(solution)/shard_map/unpack/pallas_call | solution.py:399
  (11 shorter events, 0.1 us)
Async XLA Ops:
  2.9 1.6 %collective-permute-start = (f32[4,10,8,128]{3,2,1,0:T(8,128)S(1)}, f32[4,10,8,128]{3,2,1,0:T(8,128)S(1)}, u32[]{:S(2)}, u32[]{:S(2)}) collective-permute-start(f32[4,10,8,128]{3,2,1,0:T(8,128)S(1)} %get-tuple-element.13), channel_id=1, source_target_pairs={{0,1},{1,0},{2,3},{3,2},{4,5},{5,4},{6,7},{7,6},{8,9},{9,8},{10,11... | collective-permute-start | bytes 491528 | tf_op jit(solution)/shard_map/ppermute | solution.py:274
  3.5 18.5 %copy-start = (s32[256]{0:T(256)S(1)}, s32[256]{0:T(256)}, u32[]{:S(2)}) copy-start(s32[256]{0:T(256)} %zone_ref.1) | copy-start | bytes 3076
  4.4 3.2 %collective-permute-start.3 = (f32[4,11,8,128]{3,2,1,0:T(8,128)S(1)}, f32[4,11,8,128]{3,2,1,0:T(8,128)S(1)}, u32[]{:S(2)}, u32[]{:S(2)}) collective-permute-start(f32[4,11,8,128]{3,2,1,0:T(8,128)S(1)} %get-tuple-element.18), channel_id=1, source_target_pairs={{0,1},{1,0},{2,3},{3,2},{4,5},{5,4},{6,7},{7,6},{8,9},{9,8},{10,11... | collective-permute-start | bytes 540680 | tf_op jit(solution)/shard_map/ppermute | solution.py:274
  4.6 5.9 %collective-permute-start.1 = (f32[2,10,8,128]{3,2,1,0:T(8,128)S(1)}, f32[2,10,8,128]{3,2,1,0:T(8,128)S(1)}, u32[]{:S(2)}, u32[]{:S(2)}) collective-permute-start(f32[2,10,8,128]{3,2,1,0:T(8,128)S(1)} %fusion.1), channel_id=1, source_target_pairs={{0,2},{1,3},{2,0},{3,1},{4,6},{5,7},{6,4},{7,5},{8,10},{9,11},{10,... | collective-permute-start | bytes 245768 | tf_op jit(solution)/shard_map/ppermute | solution.py:274
  7.7 5.8 %collective-permute-start.4 = (f32[2,11,8,128]{3,2,1,0:T(8,128)S(1)}, f32[2,11,8,128]{3,2,1,0:T(8,128)S(1)}, u32[]{:S(2)}, u32[]{:S(2)}) collective-permute-start(f32[2,11,8,128]{3,2,1,0:T(8,128)S(1)} %fusion), channel_id=1, source_target_pairs={{0,2},{1,3},{2,0},{3,1},{4,6},{5,7},{6,4},{7,5},{8,10},{9,11},{10,... | collective-permute-start | bytes 270344 | tf_op jit(solution)/shard_map/ppermute | solution.py:274
  10.5 4.9 %collective-permute-start.2 = (f32[1,10,8,128]{3,2,1,0:T(8,128)S(1)}, f32[1,10,8,128]{3,2,1,0:T(8,128)S(1)}, u32[]{:S(2)}, u32[]{:S(2)}) collective-permute-start(f32[1,10,8,128]{3,2,1,0:T(8,128)S(1)} %bitcast_add_fusion.4), channel_id=1, source_target_pairs={{0,4},{1,5},{2,6},{3,7},{4,0},{5,1},{6,2},{7,3},{8,12},{9,13},{10,... | collective-permute-start | bytes 122888 | tf_op jit(solution)/shard_map/ppermute | solution.py:274
  13.4 5.0 %collective-permute-start.5 = (f32[1,11,8,128]{3,2,1,0:T(8,128)S(1)}, f32[1,11,8,128]{3,2,1,0:T(8,128)S(1)}, u32[]{:S(2)}, u32[]{:S(2)}) collective-permute-start(f32[1,11,8,128]{3,2,1,0:T(8,128)S(1)} %bitcast_add_fusion.2), channel_id=1, source_target_pairs={{0,4},{1,5},{2,6},{3,7},{4,0},{5,1},{6,2},{7,3},{8,12},{9,13},{10,... | collective-permute-start | bytes 135176 | tf_op jit(solution)/shard_map/ppermute | solution.py:274
  18.5 4.6 %collective-permute-start.6 = (f32[21,8,128]{2,1,0:T(8,128)S(1)}, f32[21,8,128]{2,1,0:T(8,128)S(1)}, u32[]{:S(2)}, u32[]{:S(2)}) collective-permute-start(f32[21,8,128]{2,1,0:T(8,128)S(1)} %pad_maximum_fusion.refs_0_.refs_1_), channel_id=1, source_target_pairs={{0,8},{8,0},{16,24},{24,16},{1,9},{9,1},{17,25},{25,17},{2,10},{10... | collective-permute-start | bytes 258056 | tf_op jit(solution)/shard_map/ppermute | solution.py:274
  20.0 4.5 %collective-permute-start.7 = (f32[21,8,128]{2,1,0:T(8,128)S(1)}, f32[21,8,128]{2,1,0:T(8,128)S(1)}, u32[]{:S(2)}, u32[]{:S(2)}) collective-permute-start(f32[21,8,128]{2,1,0:T(8,128)S(1)} %pad_maximum_fusion.refs_0_.refs_1_), channel_id=1, source_target_pairs={{0,16},{8,24},{16,0},{24,8},{1,17},{9,25},{17,1},{25,9},{2,18},{10... | collective-permute-start | bytes 258056 | tf_op jit(solution)/shard_map/ppermute | solution.py:274
  21.6 5.4 %collective-permute-start.8 = (f32[21,8,128]{2,1,0:T(8,128)S(1)}, f32[21,8,128]{2,1,0:T(8,128)S(1)}, u32[]{:S(2)}, u32[]{:S(2)}) collective-permute-start(f32[21,8,128]{2,1,0:T(8,128)S(1)} %pad_maximum_fusion.refs_0_.refs_1_), channel_id=1, source_target_pairs={{0,24},{8,16},{16,8},{24,0},{1,25},{9,17},{17,9},{25,1},{2,26},{10... | collective-permute-start | bytes 258056 | tf_op jit(solution)/shard_map/ppermute | solution.py:274
  27.8 1.2 %collective-permute-start.9 = (f32[16,256]{1,0:T(8,128)S(1)}, f32[16,256]{1,0:T(8,128)S(1)}, u32[]{:S(2)}, u32[]{:S(2)}) collective-permute-start(f32[16,256]{1,0:T(8,128)S(1)} %share.1), channel_id=1, source_target_pairs={{0,1},{1,0},{2,3},{3,2},{4,5},{5,4},{6,7},{7,6},{8,9},{9,8},{10,11... | collective-permute-start | bytes 49160 | tf_op jit(solution)/shard_map/ppermute | solution.py:274
  29.0 3.7 %collective-permute-start.10 = (f32[16,256]{1,0:T(8,128)S(1)}, f32[16,256]{1,0:T(8,128)S(1)}, u32[]{:S(2)}, u32[]{:S(2)}) collective-permute-start(f32[16,256]{1,0:T(8,128)S(1)} %add.143), channel_id=1, source_target_pairs={{0,2},{1,3},{2,0},{3,1},{4,6},{5,7},{6,4},{7,5},{8,10},{9,11},{10,... | collective-permute-start | bytes 49160 | tf_op jit(solution)/shard_map/ppermute | solution.py:274
  32.7 4.6 %collective-permute-start.11 = (f32[16,256]{1,0:T(8,128)S(1)}, f32[16,256]{1,0:T(8,128)S(1)}, u32[]{:S(2)}, u32[]{:S(2)}) collective-permute-start(f32[16,256]{1,0:T(8,128)S(1)} %add.144.refs_0_), channel_id=1, source_target_pairs={{0,4},{1,5},{2,6},{3,7},{4,0},{5,1},{6,2},{7,3},{8,12},{9,13},{10,... | collective-permute-start | bytes 49160 | tf_op jit(solution)/shard_map/ppermute | solution.py:274

commit v4 on v3

--- a/solution.py
+++ b/solution.py
@@ -274,6 +274,14 @@
     return lax.ppermute(value, axis, [(i, i ^ bit) for i in range(size)])
 
 
+def sum_stages(tiles):
+    stages, size = [(3, 2, 1)], 4
+    while size < tiles:
+        stages.append((size,))
+        size *= 2
+    return stages
+
+
 def halve(chunks, tile, bit):
     mine = (tile // bit) % 2
     keeps, sends = [], []
@@ -391,19 +399,21 @@
         compiler_params=PARAMS,
         name="means",
     )(*parts)
-    bit = 1
-    while 2 * bit < tiles:
-        share = share + exchange(share, "tile", bit)
-        bit *= 2
     norm = float((members - 1) * BASINS * layers * (lats // NBANDS))
+    stages = sum_stages(tiles)
+    for stage in stages[:-1]:
+        gots = [exchange(share, "tile", r) for r in stage]
+        for got in gots:
+            share = share + got
+    gots = [exchange(share, "tile", r) for r in stages[-1]]
     covariance = pl.pallas_call(
         functools.partial(unpack_kernel, members=members, scale=1.0 / norm),
         out_shape=jax.ShapeDtypeStruct((NBANDS, members, members), jnp.float32),
-        in_specs=[VMEM] * 2,
+        in_specs=[VMEM] * (1 + len(gots)),
         out_specs=VMEM,
         compiler_params=PARAMS,
         name="unpack",
-    )(share, exchange(share, "tile", bit))
+    )(share, *gots)
     return (jnp.transpose(psi, (0, 2, 1)), jnp.transpose(heat, (1, 0)), covariance)
 
 

time: 38.3 us -> 38.2 us (level)
  waiting for transfers between devices: 14.4 us -> 13.7 us
  starting transfers between devices: 16.5 us -> 17.2 us
    ppermute x12 -> x13, waiting for transfers between devices: 14.4 us -> 13.7 us  [exchange(): return lax.ppermute(value, axis, [(i, i ^ bit) for i in range(size)])]
    ppermute x12 -> x13, starting transfers between devices: 16.5 us -> 17.2 us  [exchange(): return lax.ppermute(value, axis, [(i, i ^ bit) for i in range(size)])]
  transfers between devices with their start and end apart: 12 -> 13, of which waited for: 9 -> 9; matrix products, arithmetic and copies ran while one was open for 0% -> 0% of each run, Pallas kernels for 6% -> 6%
where the time goes in v4:
time: 38.2 us; the launch traced here: 38.1 us
  starting transfers between devices  17.2 us (45%)
  waiting for transfers between devices  13.7 us (36%)
  Pallas kernels  6.25 us (16%)
  between operations  0.78 us (2%)
    ppermute x13, starting transfers between devices, exchange(): return lax.ppermute(value, axis, [(i, i ^ bit) for i in range(size)])  17.2 us
    ppermute x13, waiting for transfers between devices, exchange(): return lax.ppermute(value, axis, [(i, i ^ bit) for i in range(size)])  13.7 us
    pallas_call x1, Pallas kernels, local(): pl.pallas_call(functools.partial(first_kernel, **sizes), out_shape=(early...  2.25 us
    pallas_call x1, Pallas kernels, local(): pl.pallas_call(functools.partial(second_kernel, **sizes), out_shape=(late...  0.87 us
    pallas_call x1, Pallas kernels, local(): pl.pallas_call(functools.partial(means_kernel, **known), out_shape=(jax.S...  0.87 us
    pallas_call x1, Pallas kernels, local(): pl.pallas_call(functools.partial(share_kernel, **known), out_shape=pltpu....  0.85 us
  transfers between devices with their start and end apart: 13, of which 9 were waited for; matrix products, arithmetic and copies ran while one was open for 0% of the time, Pallas kernels for 6%

profile of v4, /device:TPU:0, one launch (start us, length us, event | category | flops | bytes accessed | tf_op | source)
XLA Modules:
  0.0 38.1 jit_solution(14380013511569451664)
XLA Ops:
  0.6 0.1 cosine_multiply_fusion.spacing_ref
  0.7 2.2 %first.1 = (f32[4,10,8,128]{3,2,1,0:T(8,128)S(1)}, f32[4,10,8,128]{3,2,1,0:T(8,128)S(1)}, f32[128,128]{1,0:T(8,128)S(1)}, f32[3,1024,128]{2,1,0:T(8,128)S(1)}, s32[8,256]{1,0:T(8,128)S(1)}) custom-call(f32[1024,128]{1,0:T(8,128)} %bitcast.63, f32[1024,128]{1,0:T(8,128)} %bitcast.64, f32[1024,128]{1,0:T(8,128)} %bitcast.65, s32[8,256]{1,0:T(8,128)} %region_ref.1, ...), custom_call_target="tpu_custom_call" | custom-call | tf_op jit(solution)/shard_map/first/pallas_call | solution.py:340
  2.9 0.6 %collective-permute-start = (f32[4,10,8,128]{3,2,1,0:T(8,128)S(1)}, f32[4,10,8,128]{3,2,1,0:T(8,128)S(1)}, u32[]{:S(2)}, u32[]{:S(2)}) collective-permute-start(f32[4,10,8,128]{3,2,1,0:T(8,128)S(1)} %get-tuple-element.13), channel_id=1, source_target_pairs={{0,1},{1,0},{2,3},{3,2},{4,5},{5,4},{6,7},{7,6},{8,9},{9,8},{10,11... | collective-permute-start | bytes 491528 | tf_op jit(solution)/shard_map/ppermute | solution.py:274
  3.5 0.0 copy-start
  3.5 0.9 %second.1 = (f32[4,11,8,128]{3,2,1,0:T(8,128)S(1)}, f32[4,11,8,128]{3,2,1,0:T(8,128)S(1)}) custom-call(f32[3,1024,128]{2,1,0:T(8,128)S(1)} %get-tuple-element.14.data_ref, s32[8,256]{1,0:T(8,128)S(1)} %get-tuple-element.15.region_ref, f32[1,256]{1,0:T(1,128)S(1)} %cosine_multiply_fusion.spacing_ref, f32[128,128]{1,0:T(8,128)S(1)} %get-tuple-element.16.heat_ref), custom_call_target="tpu_custom_call" | custom-call | tf_op jit(solution)/shard_map/second/pallas_call | solution.py:356
  4.4 0.1 collective-permute-start.3
  4.5 0.0 collective-permute-done.order_ref
  4.6 3.0 %collective-permute-start.1 = (f32[2,10,8,128]{3,2,1,0:T(8,128)S(1)}, f32[2,10,8,128]{3,2,1,0:T(8,128)S(1)}, u32[]{:S(2)}, u32[]{:S(2)}) collective-permute-start(f32[2,10,8,128]{3,2,1,0:T(8,128)S(1)} %fusion.1), channel_id=1, source_target_pairs={{0,2},{1,3},{2,0},{3,1},{4,6},{5,7},{6,4},{7,5},{8,10},{9,11},{10,... | collective-permute-start | bytes 245768 | tf_op jit(solution)/shard_map/ppermute | solution.py:274
  7.6 0.0 collective-permute-done.3
  7.7 1.0 %collective-permute-start.4 = (f32[2,11,8,128]{3,2,1,0:T(8,128)S(1)}, f32[2,11,8,128]{3,2,1,0:T(8,128)S(1)}, u32[]{:S(2)}, u32[]{:S(2)}) collective-permute-start(f32[2,11,8,128]{3,2,1,0:T(8,128)S(1)} %fusion), channel_id=1, source_target_pairs={{0,2},{1,3},{2,0},{3,1},{4,6},{5,7},{6,4},{7,5},{8,10},{9,11},{10,... | collective-permute-start | bytes 270344 | tf_op jit(solution)/shard_map/ppermute | solution.py:274
  8.7 1.8 %collective-permute-done.1 = f32[2,10,8,128]{3,2,1,0:T(8,128)S(1)} collective-permute-done((f32[2,10,8,128]{3,2,1,0:T(8,128)S(1)}, f32[2,10,8,128]{3,2,1,0:T(8,128)S(1)}, u32[]{:S(2)}, u32[]{:S(2)}) %collective-permute-start.1) | collective-permute-done | bytes 81952 | tf_op jit(solution)/shard_map/ppermute | solution.py:274
  10.5 2.9 %collective-permute-start.2 = (f32[1,10,8,128]{3,2,1,0:T(8,128)S(1)}, f32[1,10,8,128]{3,2,1,0:T(8,128)S(1)}, u32[]{:S(2)}, u32[]{:S(2)}) collective-permute-start(f32[1,10,8,128]{3,2,1,0:T(8,128)S(1)} %bitcast_add_fusion.4), channel_id=1, source_target_pairs={{0,4},{1,5},{2,6},{3,7},{4,0},{5,1},{6,2},{7,3},{8,12},{9,13},{10,... | collective-permute-start | bytes 122888 | tf_op jit(solution)/shard_map/ppermute | solution.py:274
  13.4 0.0 collective-permute-done.4
  13.4 1.8 %collective-permute-start.5 = (f32[1,11,8,128]{3,2,1,0:T(8,128)S(1)}, f32[1,11,8,128]{3,2,1,0:T(8,128)S(1)}, u32[]{:S(2)}, u32[]{:S(2)}) collective-permute-start(f32[1,11,8,128]{3,2,1,0:T(8,128)S(1)} %bitcast_add_fusion.2), channel_id=1, source_target_pairs={{0,4},{1,5},{2,6},{3,7},{4,0},{5,1},{6,2},{7,3},{8,12},{9,13},{10,... | collective-permute-start | bytes 135176 | tf_op jit(solution)/shard_map/ppermute | solution.py:274
  15.3 0.1 collective-permute-done.2
  15.4 3.0 %collective-permute-done.5 = f32[1,11,8,128]{3,2,1,0:T(8,128)S(1)} collective-permute-done((f32[1,11,8,128]{3,2,1,0:T(8,128)S(1)}, f32[1,11,8,128]{3,2,1,0:T(8,128)S(1)}, u32[]{:S(2)}, u32[]{:S(2)}) %collective-permute-start.5) | collective-permute-done | bytes 45088 | tf_op jit(solution)/shard_map/ppermute | solution.py:274
  18.5 1.6 %collective-permute-start.6 = (f32[21,8,128]{2,1,0:T(8,128)S(1)}, f32[21,8,128]{2,1,0:T(8,128)S(1)}, u32[]{:S(2)}, u32[]{:S(2)}) collective-permute-start(f32[21,8,128]{2,1,0:T(8,128)S(1)} %pad_maximum_fusion.refs_0_.refs_1_), channel_id=1, source_target_pairs={{0,8},{8,0},{16,24},{24,16},{1,9},{9,1},{17,25},{25,17},{2,10},{10... | collective-permute-start | bytes 258056 | tf_op jit(solution)/shard_map/ppermute | solution.py:274
  20.0 1.5 %collective-permute-start.7 = (f32[21,8,128]{2,1,0:T(8,128)S(1)}, f32[21,8,128]{2,1,0:T(8,128)S(1)}, u32[]{:S(2)}, u32[]{:S(2)}) collective-permute-start(f32[21,8,128]{2,1,0:T(8,128)S(1)} %pad_maximum_fusion.refs_0_.refs_1_), channel_id=1, source_target_pairs={{0,16},{8,24},{16,0},{24,8},{1,17},{9,25},{17,1},{25,9},{2,18},{10... | collective-permute-start | bytes 258056 | tf_op jit(solution)/shard_map/ppermute | solution.py:274
  21.6 0.5 %collective-permute-start.8 = (f32[21,8,128]{2,1,0:T(8,128)S(1)}, f32[21,8,128]{2,1,0:T(8,128)S(1)}, u32[]{:S(2)}, u32[]{:S(2)}) collective-permute-start(f32[21,8,128]{2,1,0:T(8,128)S(1)} %pad_maximum_fusion.refs_0_.refs_1_), channel_id=1, source_target_pairs={{0,24},{8,16},{16,8},{24,0},{1,25},{9,17},{17,9},{25,1},{2,26},{10... | collective-permute-start | bytes 258056 | tf_op jit(solution)/shard_map/ppermute | solution.py:274
  22.0 0.0 copy-done
  22.0 0.7 %bands.1.refs_0_ = bf16[4,256,128]{2,1,0:T(8,128)(2,1)S(1)} custom-call(s32[256]{0:T(256)S(1)} %copy-done, f32[4,10,8,128]{3,2,1,0:T(8,128)S(1)} %collective-permute-done.order_ref), custom_call_target="tpu_custom_call" | custom-call | tf_op jit(solution)/shard_map/bands/pallas_call | solution.py:365
  22.7 0.3 collective-permute-done.6.refs_1_.refs_2_
  23.0 1.5 %collective-permute-done.7.refs_2_.refs_3_ = f32[21,8,128]{2,1,0:T(8,128)S(1)} collective-permute-done((f32[21,8,128]{2,1,0:T(8,128)S(1)}, f32[21,8,128]{2,1,0:T(8,128)S(1)}, u32[]{:S(2)}, u32[]{:S(2)}) %collective-permute-start.7) | collective-permute-done | bytes 86048 | tf_op jit(solution)/shard_map/ppermute | solution.py:274
  24.5 2.4 %collective-permute-done.8.refs_3_.refs_4_ = f32[21,8,128]{2,1,0:T(8,128)S(1)} collective-permute-done((f32[21,8,128]{2,1,0:T(8,128)S(1)}, f32[21,8,128]{2,1,0:T(8,128)S(1)}, u32[]{:S(2)}, u32[]{:S(2)}) %collective-permute-start.8) | collective-permute-done | bytes 86048 | tf_op jit(solution)/shard_map/ppermute | solution.py:274
  26.9 0.8 %share.1 = f32[16,256]{1,0:T(8,128)S(1)} custom-call(bf16[4,256,128]{2,1,0:T(8,128)(2,1)S(1)} %bands.1.refs_0_, f32[21,8,128]{2,1,0:T(8,128)S(1)} %pad_maximum_fusion.refs_0_.refs_1_, f32[21,8,128]{2,1,0:T(8,128)S(1)} %collective-permute-done.6.refs_1_.refs_2_, f32[21,8,128]{2,1,0:T(8,128)S(1)} %collective-permute-done.7.refs_2_.refs_3_, ...), custom_call_target="tpu_custom_call" | custom-call | tf_op jit(solution)/shard_map/share/pallas_call | solution.py:382
  27.8 1.7 %collective-permute-start.10 = (f32[16,256]{1,0:T(8,128)S(1)}, f32[16,256]{1,0:T(8,128)S(1)}, u32[]{:S(2)}, u32[]{:S(2)}) collective-permute-start(f32[16,256]{1,0:T(8,128)S(1)} %share.1), channel_id=1, source_target_pairs={{0,2},{1,3},{2,0},{3,1},{4,6},{5,7},{6,4},{7,5},{8,10},{9,11},{10,... | collective-permute-start | bytes 49160 | tf_op jit(solution)/shard_map/ppermute | solution.py:274
  29.5 0.0 collective-permute-start.11
  29.5 0.5 %collective-permute-start.9 = (f32[16,256]{1,0:T(8,128)S(1)}, f32[16,256]{1,0:T(8,128)S(1)}, u32[]{:S(2)}, u32[]{:S(2)}) collective-permute-start(f32[16,256]{1,0:T(8,128)S(1)} %share.1), channel_id=1, source_target_pairs={{0,3},{1,2},{2,1},{3,0},{4,7},{5,6},{6,5},{7,4},{8,11},{9,10},{10,... | collective-permute-start | bytes 49160 | tf_op jit(solution)/shard_map/ppermute | solution.py:274
  29.9 1.6 %collective-permute-done.10 = f32[16,256]{1,0:T(8,128)S(1)} collective-permute-done((f32[16,256]{1,0:T(8,128)S(1)}, f32[16,256]{1,0:T(8,128)S(1)}, u32[]{:S(2)}, u32[]{:S(2)}) %collective-permute-start.10) | collective-permute-done | bytes 16416 | tf_op jit(solution)/shard_map/ppermute | solution.py:274
  31.5 0.0 collective-permute-done.11
  31.5 1.1 %collective-permute-done.9 = f32[16,256]{1,0:T(8,128)S(1)} collective-permute-done((f32[16,256]{1,0:T(8,128)S(1)}, f32[16,256]{1,0:T(8,128)S(1)}, u32[]{:S(2)}, u32[]{:S(2)}) %collective-permute-start.9) | collective-permute-done | bytes 16416 | tf_op jit(solution)/shard_map/ppermute | solution.py:274
  32.6 2.0 %collective-permute-start.12 = (f32[16,256]{1,0:T(8,128)S(1)}, f32[16,256]{1,0:T(8,128)S(1)}, u32[]{:S(2)}, u32[]{:S(2)}) collective-permute-start(f32[16,256]{1,0:T(8,128)S(1)} %add_add_fusion.refs_0_), channel_id=1, source_target_pairs={{0,4},{1,5},{2,6},{3,7},{4,0},{5,1},{6,2},{7,3},{8,12},{9,13},{10,... | collective-permute-start | bytes 49160 | tf_op jit(solution)/shard_map/ppermute | solution.py:274
  34.7 0.9 %means.1 = (f32[10,8,16]{2,1,0:T(8,128)}, f32[8,10]{1,0:T(8,128)}) custom-call(f32[21,8,128]{2,1,0:T(8,128)S(1)} %pad_maximum_fusion.refs_0_.refs_1_, f32[21,8,128]{2,1,0:T(8,128)S(1)} %collective-permute-done.6.refs_1_.refs_2_, f32[21,8,128]{2,1,0:T(8,128)S(1)} %collective-permute-done.7.refs_2_.refs_3_, ...), custom_call_target="tpu_custom_call" | custom-call | tf_op jit(solution)/shard_map/means/pallas_call | solution.py:391
  35.5 1.8 %collective-permute-done.12.refs_1_ = f32[16,256]{1,0:T(8,128)S(1)} collective-permute-done((f32[16,256]{1,0:T(8,128)S(1)}, f32[16,256]{1,0:T(8,128)S(1)}, u32[]{:S(2)}, u32[]{:S(2)}) %collective-permute-start.12) | collective-permute-done | bytes 16416 | tf_op jit(solution)/shard_map/ppermute | solution.py:274
  37.3 0.8 %unpack.1 = f32[16,16,16]{2,1,0:T(8,128)} custom-call(f32[16,256]{1,0:T(8,128)S(1)} %add_add_fusion.refs_0_, f32[16,256]{1,0:T(8,128)S(1)} %collective-permute-done.12.refs_1_), custom_call_target="tpu_custom_call" | custom-call | tf_op jit(solution)/shard_map/unpack/pallas_call | solution.py:409
  (10 shorter events, 0.1 us)
Async XLA Ops:
  2.9 1.6 %collective-permute-start = (f32[4,10,8,128]{3,2,1,0:T(8,128)S(1)}, f32[4,10,8,128]{3,2,1,0:T(8,128)S(1)}, u32[]{:S(2)}, u32[]{:S(2)}) collective-permute-start(f32[4,10,8,128]{3,2,1,0:T(8,128)S(1)} %get-tuple-element.13), channel_id=1, source_target_pairs={{0,1},{1,0},{2,3},{3,2},{4,5},{5,4},{6,7},{7,6},{8,9},{9,8},{10,11... | collective-permute-start | bytes 491528 | tf_op jit(solution)/shard_map/ppermute | solution.py:274
  3.5 18.5 %copy-start = (s32[256]{0:T(256)S(1)}, s32[256]{0:T(256)}, u32[]{:S(2)}) copy-start(s32[256]{0:T(256)} %zone_ref.1) | copy-start | bytes 3076
  4.4 3.2 %collective-permute-start.3 = (f32[4,11,8,128]{3,2,1,0:T(8,128)S(1)}, f32[4,11,8,128]{3,2,1,0:T(8,128)S(1)}, u32[]{:S(2)}, u32[]{:S(2)}) collective-permute-start(f32[4,11,8,128]{3,2,1,0:T(8,128)S(1)} %get-tuple-element.18), channel_id=1, source_target_pairs={{0,1},{1,0},{2,3},{3,2},{4,5},{5,4},{6,7},{7,6},{8,9},{9,8},{10,11... | collective-permute-start | bytes 540680 | tf_op jit(solution)/shard_map/ppermute | solution.py:274
  4.6 5.9 %collective-permute-start.1 = (f32[2,10,8,128]{3,2,1,0:T(8,128)S(1)}, f32[2,10,8,128]{3,2,1,0:T(8,128)S(1)}, u32[]{:S(2)}, u32[]{:S(2)}) collective-permute-start(f32[2,10,8,128]{3,2,1,0:T(8,128)S(1)} %fusion.1), channel_id=1, source_target_pairs={{0,2},{1,3},{2,0},{3,1},{4,6},{5,7},{6,4},{7,5},{8,10},{9,11},{10,... | collective-permute-start | bytes 245768 | tf_op jit(solution)/shard_map/ppermute | solution.py:274
  7.7 5.8 %collective-permute-start.4 = (f32[2,11,8,128]{3,2,1,0:T(8,128)S(1)}, f32[2,11,8,128]{3,2,1,0:T(8,128)S(1)}, u32[]{:S(2)}, u32[]{:S(2)}) collective-permute-start(f32[2,11,8,128]{3,2,1,0:T(8,128)S(1)} %fusion), channel_id=1, source_target_pairs={{0,2},{1,3},{2,0},{3,1},{4,6},{5,7},{6,4},{7,5},{8,10},{9,11},{10,... | collective-permute-start | bytes 270344 | tf_op jit(solution)/shard_map/ppermute | solution.py:274
  10.5 4.9 %collective-permute-start.2 = (f32[1,10,8,128]{3,2,1,0:T(8,128)S(1)}, f32[1,10,8,128]{3,2,1,0:T(8,128)S(1)}, u32[]{:S(2)}, u32[]{:S(2)}) collective-permute-start(f32[1,10,8,128]{3,2,1,0:T(8,128)S(1)} %bitcast_add_fusion.4), channel_id=1, source_target_pairs={{0,4},{1,5},{2,6},{3,7},{4,0},{5,1},{6,2},{7,3},{8,12},{9,13},{10,... | collective-permute-start | bytes 122888 | tf_op jit(solution)/shard_map/ppermute | solution.py:274
  13.4 5.0 %collective-permute-start.5 = (f32[1,11,8,128]{3,2,1,0:T(8,128)S(1)}, f32[1,11,8,128]{3,2,1,0:T(8,128)S(1)}, u32[]{:S(2)}, u32[]{:S(2)}) collective-permute-start(f32[1,11,8,128]{3,2,1,0:T(8,128)S(1)} %bitcast_add_fusion.2), channel_id=1, source_target_pairs={{0,4},{1,5},{2,6},{3,7},{4,0},{5,1},{6,2},{7,3},{8,12},{9,13},{10,... | collective-permute-start | bytes 135176 | tf_op jit(solution)/shard_map/ppermute | solution.py:274
  18.5 4.6 %collective-permute-start.6 = (f32[21,8,128]{2,1,0:T(8,128)S(1)}, f32[21,8,128]{2,1,0:T(8,128)S(1)}, u32[]{:S(2)}, u32[]{:S(2)}) collective-permute-start(f32[21,8,128]{2,1,0:T(8,128)S(1)} %pad_maximum_fusion.refs_0_.refs_1_), channel_id=1, source_target_pairs={{0,8},{8,0},{16,24},{24,16},{1,9},{9,1},{17,25},{25,17},{2,10},{10... | collective-permute-start | bytes 258056 | tf_op jit(solution)/shard_map/ppermute | solution.py:274
  20.0 4.5 %collective-permute-start.7 = (f32[21,8,128]{2,1,0:T(8,128)S(1)}, f32[21,8,128]{2,1,0:T(8,128)S(1)}, u32[]{:S(2)}, u32[]{:S(2)}) collective-permute-start(f32[21,8,128]{2,1,0:T(8,128)S(1)} %pad_maximum_fusion.refs_0_.refs_1_), channel_id=1, source_target_pairs={{0,16},{8,24},{16,0},{24,8},{1,17},{9,25},{17,1},{25,9},{2,18},{10... | collective-permute-start | bytes 258056 | tf_op jit(solution)/shard_map/ppermute | solution.py:274
  21.6 5.4 %collective-permute-start.8 = (f32[21,8,128]{2,1,0:T(8,128)S(1)}, f32[21,8,128]{2,1,0:T(8,128)S(1)}, u32[]{:S(2)}, u32[]{:S(2)}) collective-permute-start(f32[21,8,128]{2,1,0:T(8,128)S(1)} %pad_maximum_fusion.refs_0_.refs_1_), channel_id=1, source_target_pairs={{0,24},{8,16},{16,8},{24,0},{1,25},{9,17},{17,9},{25,1},{2,26},{10... | collective-permute-start | bytes 258056 | tf_op jit(solution)/shard_map/ppermute | solution.py:274
  27.8 3.8 %collective-permute-start.10 = (f32[16,256]{1,0:T(8,128)S(1)}, f32[16,256]{1,0:T(8,128)S(1)}, u32[]{:S(2)}, u32[]{:S(2)}) collective-permute-start(f32[16,256]{1,0:T(8,128)S(1)} %share.1), channel_id=1, source_target_pairs={{0,2},{1,3},{2,0},{3,1},{4,6},{5,7},{6,4},{7,5},{8,10},{9,11},{10,... | collective-permute-start | bytes 49160 | tf_op jit(solution)/shard_map/ppermute | solution.py:274
  29.5 2.1 %collective-permute-start.11 = (f32[16,256]{1,0:T(8,128)S(1)}, f32[16,256]{1,0:T(8,128)S(1)}, u32[]{:S(2)}, u32[]{:S(2)}) collective-permute-start(f32[16,256]{1,0:T(8,128)S(1)} %share.1), channel_id=1, source_target_pairs={{0,1},{1,0},{2,3},{3,2},{4,5},{5,4},{6,7},{7,6},{8,9},{9,8},{10,11... | collective-permute-start | bytes 49160 | tf_op jit(solution)/shard_map/ppermute | solution.py:274
  29.5 3.2 %collective-permute-start.9 = (f32[16,256]{1,0:T(8,128)S(1)}, f32[16,256]{1,0:T(8,128)S(1)}, u32[]{:S(2)}, u32[]{:S(2)}) collective-permute-start(f32[16,256]{1,0:T(8,128)S(1)} %share.1), channel_id=1, source_target_pairs={{0,3},{1,2},{2,1},{3,0},{4,7},{5,6},{6,5},{7,4},{8,11},{9,10},{10,... | collective-permute-start | bytes 49160 | tf_op jit(solution)/shard_map/ppermute | solution.py:274
  32.6 4.6 %collective-permute-start.12 = (f32[16,256]{1,0:T(8,128)S(1)}, f32[16,256]{1,0:T(8,128)S(1)}, u32[]{:S(2)}, u32[]{:S(2)}) collective-permute-start(f32[16,256]{1,0:T(8,128)S(1)} %add_add_fusion.refs_0_), channel_id=1, source_target_pairs={{0,4},{1,5},{2,6},{3,7},{4,0},{5,1},{6,2},{7,3},{8,12},{9,13},{10,... | collective-permute-start | bytes 49160 | tf_op jit(solution)/shard_map/ppermute | solution.py:274

commit v5 on v4

--- a/solution.py
+++ b/solution.py
@@ -45,7 +45,7 @@
     return parts
 
 
-def basin_sums(buf, region, spacing, heat_ref, keep_ref, send_ref,
+def basin_sums(buf, mask_ref, spacing, heat_ref, keep_ref, send_ref, wait,
                *, late, half, members_here, layers, columns, groups, tiles):
     feats, _ = split_features(layers, members_here)
     core = lax.axis_index("tile") % 2
@@ -87,10 +87,7 @@
     warm = [[None] * columns for _ in range(blocks)]
     extra = [[] for _ in range(blocks)]
 
-    def label(lb, x):
-        line = region[x : x + 1, lb * LANES : (lb + 1) * LANES]
-        return jnp.broadcast_to(line, (SUB, LANES))
-
+    wait()
     for m in range(members_here):
         for lb in mine:
             scale = spacing[:, lb * LANES : (lb + 1) * LANES]
@@ -104,11 +101,10 @@
                     heat = one * buf[2, at, :]
                     warm[lb][x] = heat if warm[lb][x] is None else warm[lb][x] + heat
                     flux.append(one)
-                here = label(lb, x)
                 for b in range(BASINS):
-                    hit = here == b
+                    hit = mask_ref[lb, b, x]
                     for k in range(halves):
-                        part = jnp.where(hit, flux[k], 0.0)
+                        part = flux[k] * hit
                         acc[b][k] = part if acc[b][k] is None else acc[b][k] + part
             stacked = jnp.concatenate([acc[b][k] for b in range(BASINS) for k in range(halves)], 0)
             stream = select(running, stacked)
@@ -122,7 +118,7 @@
         for b in range(BASINS):
             total = None
             for x in range(columns):
-                part = jnp.where(label(lb, x) == b, warm[lb][x], 0.0)
+                part = warm[lb][x] * mask_ref[lb, b, x]
                 total = part if total is None else total + part
             basin_heat.append(total)
         block = select(gather, jnp.concatenate(basin_heat, 0))
@@ -141,23 +137,35 @@
 
 
 def first_kernel(v_ref, h_ref, w_ref, region_ref, spacing_ref, keep_ref, send_ref, heat_ref,
-                 data_ref, small_ref, sems, small_sem, **sizes):
-    copies = [pltpu.make_async_copy(region_ref, small_ref, small_sem)]
+                 data_ref, mask_ref, small, sems, small_sem, **sizes):
+    labels = pltpu.make_async_copy(region_ref, small, small_sem)
+    labels.start()
+    copies = []
     for a, ref in enumerate((v_ref, h_ref, w_ref)):
         copies.append(pltpu.make_async_copy(ref, data_ref.at[a], sems.at[a]))
-    for copy in copies:
-        copy.start(priority=1)
-    for copy in copies:
-        copy.wait()
+        copies[-1].start()
+    labels.wait()
+    region = small[...]
+    for lb in range(2 * sizes["half"]):
+        for x in range(sizes["columns"]):
+            line = region[x : x + 1, lb * LANES : (lb + 1) * LANES]
+            label = jnp.broadcast_to(line, (SUB, LANES))
+            for b in range(BASINS):
+                mask_ref[lb, b, x] = jnp.where(label == b, 1.0, 0.0)
+
+    def wait():
+        for copy in copies:
+            copy.wait()
+
     basin_sums(
-        data_ref, small_ref[...], spacing_ref[...], heat_ref, keep_ref, send_ref,
+        data_ref, mask_ref, spacing_ref[...], heat_ref, keep_ref, send_ref, wait,
         late=False, **sizes,
     )
 
 
-def second_kernel(data_ref, region_ref, spacing_ref, heat_ref, keep_ref, send_ref, **sizes):
+def second_kernel(data_ref, mask_ref, spacing_ref, heat_ref, keep_ref, send_ref, **sizes):
     basin_sums(
-        data_ref, region_ref[...], spacing_ref[...], heat_ref, keep_ref, send_ref,
+        data_ref, mask_ref, spacing_ref[...], heat_ref, keep_ref, send_ref, lambda: None,
         late=True, **sizes,
     )
 
@@ -337,18 +345,22 @@
     labels = pltpu.with_memory_space_constraint(ocean_region_label, pltpu.MemorySpace.HBM)
     early = pltpu.VMEM((tiles // 2, count * slots, SUB, LANES), jnp.float32)
     late = pltpu.VMEM((tiles // 2, count * slots + 1, SUB, LANES), jnp.float32)
-    keep0, send0, heat, data, labels = pl.pallas_call(
+    keep0, send0, heat, data, mask = pl.pallas_call(
         functools.partial(first_kernel, **sizes),
         out_shape=(
             early,
             early,
             pltpu.VMEM((LANES, LANES), jnp.float32),
             pltpu.VMEM((3, 2 * half * rows, LANES), jnp.float32),
-            pltpu.VMEM((columns, lats), jnp.int32),
+            pltpu.VMEM((2 * half, BASINS, columns, SUB, LANES), jnp.float32),
         ),
         in_specs=[ANY] * 4 + [VMEM],
         out_specs=(VMEM,) * 5,
-        scratch_shapes=[pltpu.SemaphoreType.DMA((3,)), pltpu.SemaphoreType.DMA(())],
+        scratch_shapes=[
+            pltpu.VMEM((columns, lats), jnp.int32),
+            pltpu.SemaphoreType.DMA((3,)),
+            pltpu.SemaphoreType.DMA(()),
+        ],
         compiler_params=PARAMS,
         name="first",
     )(*blocked, labels, spacing)
@@ -360,7 +372,7 @@
         out_specs=(VMEM, VMEM),
         compiler_params=PARAMS,
         name="second",
-    )(data, labels, spacing, heat)
+    )(data, mask, spacing, heat)
     got1 = exchange(send1, "tile", 1)
     bands = pl.pallas_call(
         functools.partial(bands_kernel, members=members, groups=groups, tiles=tiles),

time: 38.2 us -> 38.1 us (level)
  no operation moved by 1% of the time
where the time goes in v5:
time: 38.1 us; the launch traced here: 38 us
  starting transfers between devices  17.1 us (45%)
  waiting for transfers between devices  13.7 us (36%)
  Pallas kernels  6.16 us (16%)
  between operations  0.77 us (2%)
    ppermute x13, starting transfers between devices, exchange(): return lax.ppermute(value, axis, [(i, i ^ bit) for i in range(size)])  17.1 us
    ppermute x13, waiting for transfers between devices, exchange(): return lax.ppermute(value, axis, [(i, i ^ bit) for i in range(size)])  13.7 us
    pallas_call x1, Pallas kernels, local(): pl.pallas_call(functools.partial(first_kernel, **sizes), out_shape=(early...  2.2 us
    pallas_call x1, Pallas kernels, local(): pl.pallas_call(functools.partial(means_kernel, **known), out_shape=(jax.S...  0.87 us
    pallas_call x1, Pallas kernels, local(): pl.pallas_call(functools.partial(share_kernel, **known), out_shape=pltpu....  0.85 us
    pallas_call x1, Pallas kernels, local(): pl.pallas_call(functools.partial(second_kernel, **sizes), out_shape=(late...  0.84 us
  transfers between devices with their start and end apart: 13, of which 9 were waited for; matrix products, arithmetic and copies ran while one was open for 0% of the time, Pallas kernels for 6%

profile of v5, /device:TPU:0, one launch (start us, length us, event | category | flops | bytes accessed | tf_op | source)
XLA Modules:
  0.0 38.0 jit_solution(1268102751459384154)
XLA Ops:
  0.6 0.1 cosine_multiply_fusion.spacing_ref
  0.7 2.2 %first.1 = (f32[4,10,8,128]{3,2,1,0:T(8,128)S(1)}, f32[4,10,8,128]{3,2,1,0:T(8,128)S(1)}, f32[128,128]{1,0:T(8,128)S(1)}, f32[3,1024,128]{2,1,0:T(8,128)S(1)}, f32[2,10,8,8,128]{4,3,2,1,0:T(8,128)S(1)}) custom-call(f32[1024,128]{1,0:T(8,128)} %bitcast.63, f32[1024,128]{1,0:T(8,128)} %bitcast.64, f32[1024,128]{1,0:T(8,128)} %bitcast.65, s32[8,256]{1,0:T(8,128)} %region_ref.1, ...), custom_call_target="tpu_custom_call" | custom-call | tf_op jit(solution)/shard_map/first/pallas_call | solution.py:348
  2.9 0.6 %collective-permute-start = (f32[4,10,8,128]{3,2,1,0:T(8,128)S(1)}, f32[4,10,8,128]{3,2,1,0:T(8,128)S(1)}, u32[]{:S(2)}, u32[]{:S(2)}) collective-permute-start(f32[4,10,8,128]{3,2,1,0:T(8,128)S(1)} %get-tuple-element.13), channel_id=1, source_target_pairs={{0,1},{1,0},{2,3},{3,2},{4,5},{5,4},{6,7},{7,6},{8,9},{9,8},{10,11... | collective-permute-start | bytes 491528 | tf_op jit(solution)/shard_map/ppermute | solution.py:282
  3.5 0.0 copy-start
  3.5 0.8 %second.1 = (f32[4,11,8,128]{3,2,1,0:T(8,128)S(1)}, f32[4,11,8,128]{3,2,1,0:T(8,128)S(1)}) custom-call(f32[3,1024,128]{2,1,0:T(8,128)S(1)} %get-tuple-element.14.data_ref, f32[2,10,8,8,128]{4,3,2,1,0:T(8,128)S(1)} %get-tuple-element.15.mask_ref, f32[1,256]{1,0:T(1,128)S(1)} %cosine_multiply_fusion.spacing_ref, f32[128,128]{1,0:T(8,128)S(1)} %get-tuple-element.16.heat_ref), custom_call_target="tpu_custom_call" | custom-call | tf_op jit(solution)/shard_map/second/pallas_call | solution.py:368
  4.3 0.1 collective-permute-start.3
  4.5 0.0 collective-permute-done.order_ref
  4.5 3.0 %collective-permute-start.1 = (f32[2,10,8,128]{3,2,1,0:T(8,128)S(1)}, f32[2,10,8,128]{3,2,1,0:T(8,128)S(1)}, u32[]{:S(2)}, u32[]{:S(2)}) collective-permute-start(f32[2,10,8,128]{3,2,1,0:T(8,128)S(1)} %fusion.1), channel_id=1, source_target_pairs={{0,2},{1,3},{2,0},{3,1},{4,6},{5,7},{6,4},{7,5},{8,10},{9,11},{10,... | collective-permute-start | bytes 245768 | tf_op jit(solution)/shard_map/ppermute | solution.py:282
  7.5 0.0 collective-permute-done.3
  7.6 1.0 %collective-permute-start.4 = (f32[2,11,8,128]{3,2,1,0:T(8,128)S(1)}, f32[2,11,8,128]{3,2,1,0:T(8,128)S(1)}, u32[]{:S(2)}, u32[]{:S(2)}) collective-permute-start(f32[2,11,8,128]{3,2,1,0:T(8,128)S(1)} %fusion), channel_id=1, source_target_pairs={{0,2},{1,3},{2,0},{3,1},{4,6},{5,7},{6,4},{7,5},{8,10},{9,11},{10,... | collective-permute-start | bytes 270344 | tf_op jit(solution)/shard_map/ppermute | solution.py:282
  8.6 1.8 %collective-permute-done.1 = f32[2,10,8,128]{3,2,1,0:T(8,128)S(1)} collective-permute-done((f32[2,10,8,128]{3,2,1,0:T(8,128)S(1)}, f32[2,10,8,128]{3,2,1,0:T(8,128)S(1)}, u32[]{:S(2)}, u32[]{:S(2)}) %collective-permute-start.1) | collective-permute-done | bytes 81952 | tf_op jit(solution)/shard_map/ppermute | solution.py:282
  10.4 2.9 %collective-permute-start.2 = (f32[1,10,8,128]{3,2,1,0:T(8,128)S(1)}, f32[1,10,8,128]{3,2,1,0:T(8,128)S(1)}, u32[]{:S(2)}, u32[]{:S(2)}) collective-permute-start(f32[1,10,8,128]{3,2,1,0:T(8,128)S(1)} %bitcast_add_fusion.4), channel_id=1, source_target_pairs={{0,4},{1,5},{2,6},{3,7},{4,0},{5,1},{6,2},{7,3},{8,12},{9,13},{10,... | collective-permute-start | bytes 122888 | tf_op jit(solution)/shard_map/ppermute | solution.py:282
  13.3 0.0 collective-permute-done.4
  13.4 1.8 %collective-permute-start.5 = (f32[1,11,8,128]{3,2,1,0:T(8,128)S(1)}, f32[1,11,8,128]{3,2,1,0:T(8,128)S(1)}, u32[]{:S(2)}, u32[]{:S(2)}) collective-permute-start(f32[1,11,8,128]{3,2,1,0:T(8,128)S(1)} %bitcast_add_fusion.2), channel_id=1, source_target_pairs={{0,4},{1,5},{2,6},{3,7},{4,0},{5,1},{6,2},{7,3},{8,12},{9,13},{10,... | collective-permute-start | bytes 135176 | tf_op jit(solution)/shard_map/ppermute | solution.py:282
  15.2 0.1 collective-permute-done.2
  15.3 3.0 %collective-permute-done.5 = f32[1,11,8,128]{3,2,1,0:T(8,128)S(1)} collective-permute-done((f32[1,11,8,128]{3,2,1,0:T(8,128)S(1)}, f32[1,11,8,128]{3,2,1,0:T(8,128)S(1)}, u32[]{:S(2)}, u32[]{:S(2)}) %collective-permute-start.5) | collective-permute-done | bytes 45088 | tf_op jit(solution)/shard_map/ppermute | solution.py:282
  18.4 1.6 %collective-permute-start.6 = (f32[21,8,128]{2,1,0:T(8,128)S(1)}, f32[21,8,128]{2,1,0:T(8,128)S(1)}, u32[]{:S(2)}, u32[]{:S(2)}) collective-permute-start(f32[21,8,128]{2,1,0:T(8,128)S(1)} %pad_maximum_fusion.refs_0_.refs_1_), channel_id=1, source_target_pairs={{0,8},{8,0},{16,24},{24,16},{1,9},{9,1},{17,25},{25,17},{2,10},{10... | collective-permute-start | bytes 258056 | tf_op jit(solution)/shard_map/ppermute | solution.py:282
  20.0 1.5 %collective-permute-start.7 = (f32[21,8,128]{2,1,0:T(8,128)S(1)}, f32[21,8,128]{2,1,0:T(8,128)S(1)}, u32[]{:S(2)}, u32[]{:S(2)}) collective-permute-start(f32[21,8,128]{2,1,0:T(8,128)S(1)} %pad_maximum_fusion.refs_0_.refs_1_), channel_id=1, source_target_pairs={{0,16},{8,24},{16,0},{24,8},{1,17},{9,25},{17,1},{25,9},{2,18},{10... | collective-permute-start | bytes 258056 | tf_op jit(solution)/shard_map/ppermute | solution.py:282
  21.5 0.5 %collective-permute-start.8 = (f32[21,8,128]{2,1,0:T(8,128)S(1)}, f32[21,8,128]{2,1,0:T(8,128)S(1)}, u32[]{:S(2)}, u32[]{:S(2)}) collective-permute-start(f32[21,8,128]{2,1,0:T(8,128)S(1)} %pad_maximum_fusion.refs_0_.refs_1_), channel_id=1, source_target_pairs={{0,24},{8,16},{16,8},{24,0},{1,25},{9,17},{17,9},{25,1},{2,26},{10... | collective-permute-start | bytes 258056 | tf_op jit(solution)/shard_map/ppermute | solution.py:282
  22.0 0.0 copy-done
  22.0 0.7 %bands.1.refs_0_ = bf16[4,256,128]{2,1,0:T(8,128)(2,1)S(1)} custom-call(s32[256]{0:T(256)S(1)} %copy-done, f32[4,10,8,128]{3,2,1,0:T(8,128)S(1)} %collective-permute-done.order_ref), custom_call_target="tpu_custom_call" | custom-call | tf_op jit(solution)/shard_map/bands/pallas_call | solution.py:377
  22.6 0.3 collective-permute-done.6.refs_1_.refs_2_
  22.9 1.5 %collective-permute-done.7.refs_2_.refs_3_ = f32[21,8,128]{2,1,0:T(8,128)S(1)} collective-permute-done((f32[21,8,128]{2,1,0:T(8,128)S(1)}, f32[21,8,128]{2,1,0:T(8,128)S(1)}, u32[]{:S(2)}, u32[]{:S(2)}) %collective-permute-start.7) | collective-permute-done | bytes 86048 | tf_op jit(solution)/shard_map/ppermute | solution.py:282
  24.4 2.4 %collective-permute-done.8.refs_3_.refs_4_ = f32[21,8,128]{2,1,0:T(8,128)S(1)} collective-permute-done((f32[21,8,128]{2,1,0:T(8,128)S(1)}, f32[21,8,128]{2,1,0:T(8,128)S(1)}, u32[]{:S(2)}, u32[]{:S(2)}) %collective-permute-start.8) | collective-permute-done | bytes 86048 | tf_op jit(solution)/shard_map/ppermute | solution.py:282
  26.9 0.8 %share.1 = f32[16,256]{1,0:T(8,128)S(1)} custom-call(bf16[4,256,128]{2,1,0:T(8,128)(2,1)S(1)} %bands.1.refs_0_, f32[21,8,128]{2,1,0:T(8,128)S(1)} %pad_maximum_fusion.refs_0_.refs_1_, f32[21,8,128]{2,1,0:T(8,128)S(1)} %collective-permute-done.6.refs_1_.refs_2_, f32[21,8,128]{2,1,0:T(8,128)S(1)} %collective-permute-done.7.refs_2_.refs_3_, ...), custom_call_target="tpu_custom_call" | custom-call | tf_op jit(solution)/shard_map/share/pallas_call | solution.py:394
  27.7 1.7 %collective-permute-start.10 = (f32[16,256]{1,0:T(8,128)S(1)}, f32[16,256]{1,0:T(8,128)S(1)}, u32[]{:S(2)}, u32[]{:S(2)}) collective-permute-start(f32[16,256]{1,0:T(8,128)S(1)} %share.1), channel_id=1, source_target_pairs={{0,2},{1,3},{2,0},{3,1},{4,6},{5,7},{6,4},{7,5},{8,10},{9,11},{10,... | collective-permute-start | bytes 49160 | tf_op jit(solution)/shard_map/ppermute | solution.py:282
  29.4 0.0 collective-permute-start.11
  29.4 0.5 %collective-permute-start.9 = (f32[16,256]{1,0:T(8,128)S(1)}, f32[16,256]{1,0:T(8,128)S(1)}, u32[]{:S(2)}, u32[]{:S(2)}) collective-permute-start(f32[16,256]{1,0:T(8,128)S(1)} %share.1), channel_id=1, source_target_pairs={{0,3},{1,2},{2,1},{3,0},{4,7},{5,6},{6,5},{7,4},{8,11},{9,10},{10,... | collective-permute-start | bytes 49160 | tf_op jit(solution)/shard_map/ppermute | solution.py:282
  29.9 1.6 %collective-permute-done.10 = f32[16,256]{1,0:T(8,128)S(1)} collective-permute-done((f32[16,256]{1,0:T(8,128)S(1)}, f32[16,256]{1,0:T(8,128)S(1)}, u32[]{:S(2)}, u32[]{:S(2)}) %collective-permute-start.10) | collective-permute-done | bytes 16416 | tf_op jit(solution)/shard_map/ppermute | solution.py:282
  31.5 0.0 collective-permute-done.11
  31.5 1.1 %collective-permute-done.9 = f32[16,256]{1,0:T(8,128)S(1)} collective-permute-done((f32[16,256]{1,0:T(8,128)S(1)}, f32[16,256]{1,0:T(8,128)S(1)}, u32[]{:S(2)}, u32[]{:S(2)}) %collective-permute-start.9) | collective-permute-done | bytes 16416 | tf_op jit(solution)/shard_map/ppermute | solution.py:282
  32.6 2.0 %collective-permute-start.12 = (f32[16,256]{1,0:T(8,128)S(1)}, f32[16,256]{1,0:T(8,128)S(1)}, u32[]{:S(2)}, u32[]{:S(2)}) collective-permute-start(f32[16,256]{1,0:T(8,128)S(1)} %add_add_fusion.refs_0_), channel_id=1, source_target_pairs={{0,4},{1,5},{2,6},{3,7},{4,0},{5,1},{6,2},{7,3},{8,12},{9,13},{10,... | collective-permute-start | bytes 49160 | tf_op jit(solution)/shard_map/ppermute | solution.py:282
  34.6 0.9 %means.1 = (f32[10,8,16]{2,1,0:T(8,128)}, f32[8,10]{1,0:T(8,128)}) custom-call(f32[21,8,128]{2,1,0:T(8,128)S(1)} %pad_maximum_fusion.refs_0_.refs_1_, f32[21,8,128]{2,1,0:T(8,128)S(1)} %collective-permute-done.6.refs_1_.refs_2_, f32[21,8,128]{2,1,0:T(8,128)S(1)} %collective-permute-done.7.refs_2_.refs_3_, ...), custom_call_target="tpu_custom_call" | custom-call | tf_op jit(solution)/shard_map/means/pallas_call | solution.py:403
  35.5 1.8 %collective-permute-done.12.refs_1_ = f32[16,256]{1,0:T(8,128)S(1)} collective-permute-done((f32[16,256]{1,0:T(8,128)S(1)}, f32[16,256]{1,0:T(8,128)S(1)}, u32[]{:S(2)}, u32[]{:S(2)}) %collective-permute-start.12) | collective-permute-done | bytes 16416 | tf_op jit(solution)/shard_map/ppermute | solution.py:282
  37.2 0.8 %unpack.1 = f32[16,16,16]{2,1,0:T(8,128)} custom-call(f32[16,256]{1,0:T(8,128)S(1)} %add_add_fusion.refs_0_, f32[16,256]{1,0:T(8,128)S(1)} %collective-permute-done.12.refs_1_), custom_call_target="tpu_custom_call" | custom-call | tf_op jit(solution)/shard_map/unpack/pallas_call | solution.py:421
  (10 shorter events, 0.1 us)
Async XLA Ops:
  2.9 1.6 %collective-permute-start = (f32[4,10,8,128]{3,2,1,0:T(8,128)S(1)}, f32[4,10,8,128]{3,2,1,0:T(8,128)S(1)}, u32[]{:S(2)}, u32[]{:S(2)}) collective-permute-start(f32[4,10,8,128]{3,2,1,0:T(8,128)S(1)} %get-tuple-element.13), channel_id=1, source_target_pairs={{0,1},{1,0},{2,3},{3,2},{4,5},{5,4},{6,7},{7,6},{8,9},{9,8},{10,11... | collective-permute-start | bytes 491528 | tf_op jit(solution)/shard_map/ppermute | solution.py:282
  3.5 18.5 %copy-start = (s32[256]{0:T(256)S(1)}, s32[256]{0:T(256)}, u32[]{:S(2)}) copy-start(s32[256]{0:T(256)} %zone_ref.1) | copy-start | bytes 3076
  4.3 3.2 %collective-permute-start.3 = (f32[4,11,8,128]{3,2,1,0:T(8,128)S(1)}, f32[4,11,8,128]{3,2,1,0:T(8,128)S(1)}, u32[]{:S(2)}, u32[]{:S(2)}) collective-permute-start(f32[4,11,8,128]{3,2,1,0:T(8,128)S(1)} %get-tuple-element.18), channel_id=1, source_target_pairs={{0,1},{1,0},{2,3},{3,2},{4,5},{5,4},{6,7},{7,6},{8,9},{9,8},{10,11... | collective-permute-start | bytes 540680 | tf_op jit(solution)/shard_map/ppermute | solution.py:282
  4.5 5.9 %collective-permute-start.1 = (f32[2,10,8,128]{3,2,1,0:T(8,128)S(1)}, f32[2,10,8,128]{3,2,1,0:T(8,128)S(1)}, u32[]{:S(2)}, u32[]{:S(2)}) collective-permute-start(f32[2,10,8,128]{3,2,1,0:T(8,128)S(1)} %fusion.1), channel_id=1, source_target_pairs={{0,2},{1,3},{2,0},{3,1},{4,6},{5,7},{6,4},{7,5},{8,10},{9,11},{10,... | collective-permute-start | bytes 245768 | tf_op jit(solution)/shard_map/ppermute | solution.py:282
  7.6 5.8 %collective-permute-start.4 = (f32[2,11,8,128]{3,2,1,0:T(8,128)S(1)}, f32[2,11,8,128]{3,2,1,0:T(8,128)S(1)}, u32[]{:S(2)}, u32[]{:S(2)}) collective-permute-start(f32[2,11,8,128]{3,2,1,0:T(8,128)S(1)} %fusion), channel_id=1, source_target_pairs={{0,2},{1,3},{2,0},{3,1},{4,6},{5,7},{6,4},{7,5},{8,10},{9,11},{10,... | collective-permute-start | bytes 270344 | tf_op jit(solution)/shard_map/ppermute | solution.py:282
  10.4 4.9 %collective-permute-start.2 = (f32[1,10,8,128]{3,2,1,0:T(8,128)S(1)}, f32[1,10,8,128]{3,2,1,0:T(8,128)S(1)}, u32[]{:S(2)}, u32[]{:S(2)}) collective-permute-start(f32[1,10,8,128]{3,2,1,0:T(8,128)S(1)} %bitcast_add_fusion.4), channel_id=1, source_target_pairs={{0,4},{1,5},{2,6},{3,7},{4,0},{5,1},{6,2},{7,3},{8,12},{9,13},{10,... | collective-permute-start | bytes 122888 | tf_op jit(solution)/shard_map/ppermute | solution.py:282
  13.4 5.0 %collective-permute-start.5 = (f32[1,11,8,128]{3,2,1,0:T(8,128)S(1)}, f32[1,11,8,128]{3,2,1,0:T(8,128)S(1)}, u32[]{:S(2)}, u32[]{:S(2)}) collective-permute-start(f32[1,11,8,128]{3,2,1,0:T(8,128)S(1)} %bitcast_add_fusion.2), channel_id=1, source_target_pairs={{0,4},{1,5},{2,6},{3,7},{4,0},{5,1},{6,2},{7,3},{8,12},{9,13},{10,... | collective-permute-start | bytes 135176 | tf_op jit(solution)/shard_map/ppermute | solution.py:282
  18.4 4.6 %collective-permute-start.6 = (f32[21,8,128]{2,1,0:T(8,128)S(1)}, f32[21,8,128]{2,1,0:T(8,128)S(1)}, u32[]{:S(2)}, u32[]{:S(2)}) collective-permute-start(f32[21,8,128]{2,1,0:T(8,128)S(1)} %pad_maximum_fusion.refs_0_.refs_1_), channel_id=1, source_target_pairs={{0,8},{8,0},{16,24},{24,16},{1,9},{9,1},{17,25},{25,17},{2,10},{10... | collective-permute-start | bytes 258056 | tf_op jit(solution)/shard_map/ppermute | solution.py:282
  20.0 4.5 %collective-permute-start.7 = (f32[21,8,128]{2,1,0:T(8,128)S(1)}, f32[21,8,128]{2,1,0:T(8,128)S(1)}, u32[]{:S(2)}, u32[]{:S(2)}) collective-permute-start(f32[21,8,128]{2,1,0:T(8,128)S(1)} %pad_maximum_fusion.refs_0_.refs_1_), channel_id=1, source_target_pairs={{0,16},{8,24},{16,0},{24,8},{1,17},{9,25},{17,1},{25,9},{2,18},{10... | collective-permute-start | bytes 258056 | tf_op jit(solution)/shard_map/ppermute | solution.py:282
  21.5 5.4 %collective-permute-start.8 = (f32[21,8,128]{2,1,0:T(8,128)S(1)}, f32[21,8,128]{2,1,0:T(8,128)S(1)}, u32[]{:S(2)}, u32[]{:S(2)}) collective-permute-start(f32[21,8,128]{2,1,0:T(8,128)S(1)} %pad_maximum_fusion.refs_0_.refs_1_), channel_id=1, source_target_pairs={{0,24},{8,16},{16,8},{24,0},{1,25},{9,17},{17,9},{25,1},{2,26},{10... | collective-permute-start | bytes 258056 | tf_op jit(solution)/shard_map/ppermute | solution.py:282
  27.7 3.8 %collective-permute-start.10 = (f32[16,256]{1,0:T(8,128)S(1)}, f32[16,256]{1,0:T(8,128)S(1)}, u32[]{:S(2)}, u32[]{:S(2)}) collective-permute-start(f32[16,256]{1,0:T(8,128)S(1)} %share.1), channel_id=1, source_target_pairs={{0,2},{1,3},{2,0},{3,1},{4,6},{5,7},{6,4},{7,5},{8,10},{9,11},{10,... | collective-permute-start | bytes 49160 | tf_op jit(solution)/shard_map/ppermute | solution.py:282
  29.4 2.1 %collective-permute-start.11 = (f32[16,256]{1,0:T(8,128)S(1)}, f32[16,256]{1,0:T(8,128)S(1)}, u32[]{:S(2)}, u32[]{:S(2)}) collective-permute-start(f32[16,256]{1,0:T(8,128)S(1)} %share.1), channel_id=1, source_target_pairs={{0,1},{1,0},{2,3},{3,2},{4,5},{5,4},{6,7},{7,6},{8,9},{9,8},{10,11... | collective-permute-start | bytes 49160 | tf_op jit(solution)/shard_map/ppermute | solution.py:282
  29.4 3.2 %collective-permute-start.9 = (f32[16,256]{1,0:T(8,128)S(1)}, f32[16,256]{1,0:T(8,128)S(1)}, u32[]{:S(2)}, u32[]{:S(2)}) collective-permute-start(f32[16,256]{1,0:T(8,128)S(1)} %share.1), channel_id=1, source_target_pairs={{0,3},{1,2},{2,1},{3,0},{4,7},{5,6},{6,5},{7,4},{8,11},{9,10},{10,... | collective-permute-start | bytes 49160 | tf_op jit(solution)/shard_map/ppermute | solution.py:282
  32.6 4.6 %collective-permute-start.12 = (f32[16,256]{1,0:T(8,128)S(1)}, f32[16,256]{1,0:T(8,128)S(1)}, u32[]{:S(2)}, u32[]{:S(2)}) collective-permute-start(f32[16,256]{1,0:T(8,128)S(1)} %add_add_fusion.refs_0_), channel_id=1, source_target_pairs={{0,4},{1,5},{2,6},{3,7},{4,0},{5,1},{6,2},{7,3},{8,12},{9,13},{10,... | collective-permute-start | bytes 49160 | tf_op jit(solution)/shard_map/ppermute | solution.py:282

commit v6 on v5

--- a/solution.py
+++ b/solution.py
@@ -14,11 +14,6 @@
 LANES = 128
 SUB = 8
 HEAT_LANES = 16
-
-
-def metric_factor(lats):
-    index = jnp.arange(lats, dtype=jnp.float32)
-    return jnp.cos((-80.0 + 160.0 * (index + 0.5) / lats) * (math.pi / 180.0))
 
 
 def iota(shape, dim):
@@ -136,14 +131,18 @@
         put(t // 2, slots * (groups // 2), even, heat[(t + 1) * SUB : (t + 2) * SUB])
 
 
-def first_kernel(v_ref, h_ref, w_ref, region_ref, spacing_ref, keep_ref, send_ref, heat_ref,
-                 data_ref, mask_ref, small, sems, small_sem, **sizes):
+def first_kernel(v_ref, h_ref, w_ref, region_ref, keep_ref, send_ref, heat_ref,
+                 data_ref, mask_ref, spacing_ref, small, sems, small_sem, **sizes):
     labels = pltpu.make_async_copy(region_ref, small, small_sem)
     labels.start()
     copies = []
     for a, ref in enumerate((v_ref, h_ref, w_ref)):
         copies.append(pltpu.make_async_copy(ref, data_ref.at[a], sems.at[a]))
         copies[-1].start()
+    lats = spacing_ref.shape[1]
+    index = iota(spacing_ref.shape, 1).astype(jnp.float32)
+    angle = (-80.0 + 160.0 * (index + 0.5) / lats) * (math.pi / 180.0)
+    spacing_ref[...] = jnp.cos(angle) * (1.0 / math.sqrt(sizes["columns"] * sizes["tiles"]))
     labels.wait()
     region = small[...]
     for lb in range(2 * sizes["half"]):
@@ -327,7 +326,6 @@
     slots = members_here + 1
     assert lats == groups * tiles * SUB and groups * HEAT_LANES <= LANES
     assert half >= 1 and half * per_block == count and lats == 2 * half * LANES
-    spacing = (metric_factor(lats) / math.sqrt(columns * tiles)).reshape(1, lats)
     rows = members_here * layers * columns
     sizes = dict(
         half=half, members_here=members_here, layers=layers, columns=columns,
@@ -345,7 +343,7 @@
     labels = pltpu.with_memory_space_constraint(ocean_region_label, pltpu.MemorySpace.HBM)
     early = pltpu.VMEM((tiles // 2, count * slots, SUB, LANES), jnp.float32)
     late = pltpu.VMEM((tiles // 2, count * slots + 1, SUB, LANES), jnp.float32)
-    keep0, send0, heat, data, mask = pl.pallas_call(
+    keep0, send0, heat, data, mask, spacing = pl.pallas_call(
         functools.partial(first_kernel, **sizes),
         out_shape=(
             early,
@@ -353,9 +351,10 @@
             pltpu.VMEM((LANES, LANES), jnp.float32),
             pltpu.VMEM((3, 2 * half * rows, LANES), jnp.float32),
             pltpu.VMEM((2 * half, BASINS, columns, SUB, LANES), jnp.float32),
+            pltpu.VMEM((1, lats), jnp.float32),
         ),
-        in_specs=[ANY] * 4 + [VMEM],
-        out_specs=(VMEM,) * 5,
+        in_specs=[ANY] * 4,
+        out_specs=(VMEM,) * 6,
         scratch_shapes=[
             pltpu.VMEM((columns, lats), jnp.int32),
             pltpu.SemaphoreType.DMA((3,)),
@@ -363,7 +362,7 @@
         ],
         compiler_params=PARAMS,
         name="first",
-    )(*blocked, labels, spacing)
+    )(*blocked, labels)
     got0 = exchange(send0, "tile", 1)
     keep1, send1 = pl.pallas_call(
         functools.partial(second_kernel, **sizes),

time: 38.1 us -> 38.1 us (level)
  no operation moved by 1% of the time
where the time goes in v6:
time: 38.1 us; the launch traced here: 37.9 us
  starting transfers between devices  17.2 us (45%)
  waiting for transfers between devices  13.7 us (36%)
  Pallas kernels  6.17 us (16%)
  between operations  0.77 us (2%)
    ppermute x13, starting transfers between devices, exchange(): return lax.ppermute(value, axis, [(i, i ^ bit) for i in range(size)])  17.2 us
    ppermute x13, waiting for transfers between devices, exchange(): return lax.ppermute(value, axis, [(i, i ^ bit) for i in range(size)])  13.7 us
    pallas_call x1, Pallas kernels, local(): pl.pallas_call(functools.partial(first_kernel, **sizes), out_shape=(early...  2.2 us
    pallas_call x1, Pallas kernels, local(): pl.pallas_call(functools.partial(means_kernel, **known), out_shape=(jax.S...  0.87 us
    pallas_call x1, Pallas kernels, local(): pl.pallas_call(functools.partial(second_kernel, **sizes), out_shape=(late...  0.85 us
    pallas_call x1, Pallas kernels, local(): pl.pallas_call(functools.partial(share_kernel, **known), out_shape=pltpu....  0.85 us
  transfers between devices with their start and end apart: 13, of which 9 were waited for; matrix products, arithmetic and copies ran while one was open for 0% of the time, Pallas kernels for 6%

profile of v6, /device:TPU:0, one launch (start us, length us, event | category | flops | bytes accessed | tf_op | source)
XLA Modules:
  0.0 37.9 jit_solution(16680979528930263409)
XLA Ops:
  0.6 2.2 %first.1 = (f32[4,10,8,128]{3,2,1,0:T(8,128)S(1)}, f32[4,10,8,128]{3,2,1,0:T(8,128)S(1)}, f32[128,128]{1,0:T(8,128)S(1)}, f32[3,1024,128]{2,1,0:T(8,128)S(1)}, f...) custom-call(f32[1024,128]{1,0:T(8,128)} %bitcast.63, f32[1024,128]{1,0:T(8,128)} %bitcast.64, ...), custom_call_target="tpu_custom_call" | custom-call | tf_op jit(solution)/shard_map/first/pallas_call | solution.py:346
  2.8 0.6 %collective-permute-start = (f32[4,10,8,128]{3,2,1,0:T(8,128)S(1)}, f32[4,10,8,128]{3,2,1,0:T(8,128)S(1)}, u32[]{:S(2)}, u32[]{:S(2)}) collective-permute-start(f32[4,10,8,128]{3,2,1,0:T(8,128)S(1)} %get-tuple-element.14), channel_id=1, source_target_pairs={{0,1},{1,0},{2,3},{3,2},{4,5},{5,4},{6,7},{7,6},{8,9},{9,8},{10,11... | collective-permute-start | bytes 491528 | tf_op jit(solution)/shard_map/ppermute | solution.py:281
  3.4 0.0 copy-start
  3.4 0.8 %second.1 = (f32[4,11,8,128]{3,2,1,0:T(8,128)S(1)}, f32[4,11,8,128]{3,2,1,0:T(8,128)S(1)}) custom-call(f32[3,1024,128]{2,1,0:T(8,128)S(1)} %get-tuple-element.15.data_ref, f32[2,10,8,8,128]{4,3,2,1,0:T(8,128)S(1)} %get-tuple-element.16.mask_ref, f32[1,256]{1,0:T(1,128)S(1)} %get-tuple-element.17.spacing_ref, f32[128,128]{1,0:T(8,128)S(1)} %get-tuple-element.18.heat_ref), custom_call_target="tpu_custom_call" | custom-call | tf_op jit(solution)/shard_map/second/pallas_call | solution.py:367
  4.3 0.1 collective-permute-start.3
  4.4 0.0 collective-permute-done.order_ref
  4.4 3.0 %collective-permute-start.1 = (f32[2,10,8,128]{3,2,1,0:T(8,128)S(1)}, f32[2,10,8,128]{3,2,1,0:T(8,128)S(1)}, u32[]{:S(2)}, u32[]{:S(2)}) collective-permute-start(f32[2,10,8,128]{3,2,1,0:T(8,128)S(1)} %fusion.1), channel_id=1, source_target_pairs={{0,2},{1,3},{2,0},{3,1},{4,6},{5,7},{6,4},{7,5},{8,10},{9,11},{10,... | collective-permute-start | bytes 245768 | tf_op jit(solution)/shard_map/ppermute | solution.py:281
  7.5 0.0 collective-permute-done.3
  7.5 1.0 %collective-permute-start.4 = (f32[2,11,8,128]{3,2,1,0:T(8,128)S(1)}, f32[2,11,8,128]{3,2,1,0:T(8,128)S(1)}, u32[]{:S(2)}, u32[]{:S(2)}) collective-permute-start(f32[2,11,8,128]{3,2,1,0:T(8,128)S(1)} %fusion), channel_id=1, source_target_pairs={{0,2},{1,3},{2,0},{3,1},{4,6},{5,7},{6,4},{7,5},{8,10},{9,11},{10,... | collective-permute-start | bytes 270344 | tf_op jit(solution)/shard_map/ppermute | solution.py:281
  8.5 1.8 %collective-permute-done.1 = f32[2,10,8,128]{3,2,1,0:T(8,128)S(1)} collective-permute-done((f32[2,10,8,128]{3,2,1,0:T(8,128)S(1)}, f32[2,10,8,128]{3,2,1,0:T(8,128)S(1)}, u32[]{:S(2)}, u32[]{:S(2)}) %collective-permute-start.1) | collective-permute-done | bytes 81952 | tf_op jit(solution)/shard_map/ppermute | solution.py:281
  10.4 2.9 %collective-permute-start.2 = (f32[1,10,8,128]{3,2,1,0:T(8,128)S(1)}, f32[1,10,8,128]{3,2,1,0:T(8,128)S(1)}, u32[]{:S(2)}, u32[]{:S(2)}) collective-permute-start(f32[1,10,8,128]{3,2,1,0:T(8,128)S(1)} %bitcast_add_fusion.4), channel_id=1, source_target_pairs={{0,4},{1,5},{2,6},{3,7},{4,0},{5,1},{6,2},{7,3},{8,12},{9,13},{10,... | collective-permute-start | bytes 122888 | tf_op jit(solution)/shard_map/ppermute | solution.py:281
  13.3 0.0 collective-permute-done.4
  13.3 1.8 %collective-permute-start.5 = (f32[1,11,8,128]{3,2,1,0:T(8,128)S(1)}, f32[1,11,8,128]{3,2,1,0:T(8,128)S(1)}, u32[]{:S(2)}, u32[]{:S(2)}) collective-permute-start(f32[1,11,8,128]{3,2,1,0:T(8,128)S(1)} %bitcast_add_fusion.2), channel_id=1, source_target_pairs={{0,4},{1,5},{2,6},{3,7},{4,0},{5,1},{6,2},{7,3},{8,12},{9,13},{10,... | collective-permute-start | bytes 135176 | tf_op jit(solution)/shard_map/ppermute | solution.py:281
  15.1 0.1 collective-permute-done.2
  15.3 3.0 %collective-permute-done.5 = f32[1,11,8,128]{3,2,1,0:T(8,128)S(1)} collective-permute-done((f32[1,11,8,128]{3,2,1,0:T(8,128)S(1)}, f32[1,11,8,128]{3,2,1,0:T(8,128)S(1)}, u32[]{:S(2)}, u32[]{:S(2)}) %collective-permute-start.5) | collective-permute-done | bytes 45088 | tf_op jit(solution)/shard_map/ppermute | solution.py:281
  18.3 1.6 %collective-permute-start.6 = (f32[21,8,128]{2,1,0:T(8,128)S(1)}, f32[21,8,128]{2,1,0:T(8,128)S(1)}, u32[]{:S(2)}, u32[]{:S(2)}) collective-permute-start(f32[21,8,128]{2,1,0:T(8,128)S(1)} %pad_maximum_fusion.refs_0_.refs_1_), channel_id=1, source_target_pairs={{0,8},{8,0},{16,24},{24,16},{1,9},{9,1},{17,25},{25,17},{2,10},{10... | collective-permute-start | bytes 258056 | tf_op jit(solution)/shard_map/ppermute | solution.py:281
  19.9 1.5 %collective-permute-start.7 = (f32[21,8,128]{2,1,0:T(8,128)S(1)}, f32[21,8,128]{2,1,0:T(8,128)S(1)}, u32[]{:S(2)}, u32[]{:S(2)}) collective-permute-start(f32[21,8,128]{2,1,0:T(8,128)S(1)} %pad_maximum_fusion.refs_0_.refs_1_), channel_id=1, source_target_pairs={{0,16},{8,24},{16,0},{24,8},{1,17},{9,25},{17,1},{25,9},{2,18},{10... | collective-permute-start | bytes 258056 | tf_op jit(solution)/shard_map/ppermute | solution.py:281
  21.4 0.5 %collective-permute-start.8 = (f32[21,8,128]{2,1,0:T(8,128)S(1)}, f32[21,8,128]{2,1,0:T(8,128)S(1)}, u32[]{:S(2)}, u32[]{:S(2)}) collective-permute-start(f32[21,8,128]{2,1,0:T(8,128)S(1)} %pad_maximum_fusion.refs_0_.refs_1_), channel_id=1, source_target_pairs={{0,24},{8,16},{16,8},{24,0},{1,25},{9,17},{17,9},{25,1},{2,26},{10... | collective-permute-start | bytes 258056 | tf_op jit(solution)/shard_map/ppermute | solution.py:281
  21.9 0.0 copy-done
  21.9 0.7 %bands.1.refs_0_ = bf16[4,256,128]{2,1,0:T(8,128)(2,1)S(1)} custom-call(s32[256]{0:T(256)S(1)} %copy-done, f32[4,10,8,128]{3,2,1,0:T(8,128)S(1)} %collective-permute-done.order_ref), custom_call_target="tpu_custom_call" | custom-call | tf_op jit(solution)/shard_map/bands/pallas_call | solution.py:376
  22.6 0.3 collective-permute-done.6.refs_1_.refs_2_
  22.9 1.5 %collective-permute-done.7.refs_2_.refs_3_ = f32[21,8,128]{2,1,0:T(8,128)S(1)} collective-permute-done((f32[21,8,128]{2,1,0:T(8,128)S(1)}, f32[21,8,128]{2,1,0:T(8,128)S(1)}, u32[]{:S(2)}, u32[]{:S(2)}) %collective-permute-start.7) | collective-permute-done | bytes 86048 | tf_op jit(solution)/shard_map/ppermute | solution.py:281
  24.4 2.4 %collective-permute-done.8.refs_3_.refs_4_ = f32[21,8,128]{2,1,0:T(8,128)S(1)} collective-permute-done((f32[21,8,128]{2,1,0:T(8,128)S(1)}, f32[21,8,128]{2,1,0:T(8,128)S(1)}, u32[]{:S(2)}, u32[]{:S(2)}) %collective-permute-start.8) | collective-permute-done | bytes 86048 | tf_op jit(solution)/shard_map/ppermute | solution.py:281
  26.8 0.8 %share.1 = f32[16,256]{1,0:T(8,128)S(1)} custom-call(bf16[4,256,128]{2,1,0:T(8,128)(2,1)S(1)} %bands.1.refs_0_, f32[21,8,128]{2,1,0:T(8,128)S(1)} %pad_maximum_fusion.refs_0_.refs_1_, f32[21,8,128]{2,1,0:T(8,128)S(1)} %collective-permute-done.6.refs_1_.refs_2_, f32[21,8,128]{2,1,0:T(8,128)S(1)} %collective-permute-done.7.refs_2_.refs_3_, ...), custom_call_target="tpu_custom_call" | custom-call | tf_op jit(solution)/shard_map/share/pallas_call | solution.py:393
  27.6 1.7 %collective-permute-start.10 = (f32[16,256]{1,0:T(8,128)S(1)}, f32[16,256]{1,0:T(8,128)S(1)}, u32[]{:S(2)}, u32[]{:S(2)}) collective-permute-start(f32[16,256]{1,0:T(8,128)S(1)} %share.1), channel_id=1, source_target_pairs={{0,2},{1,3},{2,0},{3,1},{4,6},{5,7},{6,4},{7,5},{8,10},{9,11},{10,... | collective-permute-start | bytes 49160 | tf_op jit(solution)/shard_map/ppermute | solution.py:281
  29.3 0.0 collective-permute-start.11
  29.3 0.5 %collective-permute-start.9 = (f32[16,256]{1,0:T(8,128)S(1)}, f32[16,256]{1,0:T(8,128)S(1)}, u32[]{:S(2)}, u32[]{:S(2)}) collective-permute-start(f32[16,256]{1,0:T(8,128)S(1)} %share.1), channel_id=1, source_target_pairs={{0,3},{1,2},{2,1},{3,0},{4,7},{5,6},{6,5},{7,4},{8,11},{9,10},{10,... | collective-permute-start | bytes 49160 | tf_op jit(solution)/shard_map/ppermute | solution.py:281
  29.8 1.6 %collective-permute-done.10 = f32[16,256]{1,0:T(8,128)S(1)} collective-permute-done((f32[16,256]{1,0:T(8,128)S(1)}, f32[16,256]{1,0:T(8,128)S(1)}, u32[]{:S(2)}, u32[]{:S(2)}) %collective-permute-start.10) | collective-permute-done | bytes 16416 | tf_op jit(solution)/shard_map/ppermute | solution.py:281
  31.4 0.0 collective-permute-done.11
  31.4 1.1 %collective-permute-done.9 = f32[16,256]{1,0:T(8,128)S(1)} collective-permute-done((f32[16,256]{1,0:T(8,128)S(1)}, f32[16,256]{1,0:T(8,128)S(1)}, u32[]{:S(2)}, u32[]{:S(2)}) %collective-permute-start.9) | collective-permute-done | bytes 16416 | tf_op jit(solution)/shard_map/ppermute | solution.py:281
  32.5 2.0 %collective-permute-start.12 = (f32[16,256]{1,0:T(8,128)S(1)}, f32[16,256]{1,0:T(8,128)S(1)}, u32[]{:S(2)}, u32[]{:S(2)}) collective-permute-start(f32[16,256]{1,0:T(8,128)S(1)} %add_add_fusion.refs_0_), channel_id=1, source_target_pairs={{0,4},{1,5},{2,6},{3,7},{4,0},{5,1},{6,2},{7,3},{8,12},{9,13},{10,... | collective-permute-start | bytes 49160 | tf_op jit(solution)/shard_map/ppermute | solution.py:281
  34.5 0.9 %means.1 = (f32[10,8,16]{2,1,0:T(8,128)}, f32[8,10]{1,0:T(8,128)}) custom-call(f32[21,8,128]{2,1,0:T(8,128)S(1)} %pad_maximum_fusion.refs_0_.refs_1_, f32[21,8,128]{2,1,0:T(8,128)S(1)} %collective-permute-done.6.refs_1_.refs_2_, f32[21,8,128]{2,1,0:T(8,128)S(1)} %collective-permute-done.7.refs_2_.refs_3_, ...), custom_call_target="tpu_custom_call" | custom-call | tf_op jit(solution)/shard_map/means/pallas_call | solution.py:402
  35.4 1.8 %collective-permute-done.12.refs_1_ = f32[16,256]{1,0:T(8,128)S(1)} collective-permute-done((f32[16,256]{1,0:T(8,128)S(1)}, f32[16,256]{1,0:T(8,128)S(1)}, u32[]{:S(2)}, u32[]{:S(2)}) %collective-permute-start.12) | collective-permute-done | bytes 16416 | tf_op jit(solution)/shard_map/ppermute | solution.py:281
  37.2 0.8 %unpack.1 = f32[16,16,16]{2,1,0:T(8,128)} custom-call(f32[16,256]{1,0:T(8,128)S(1)} %add_add_fusion.refs_0_, f32[16,256]{1,0:T(8,128)S(1)} %collective-permute-done.12.refs_1_), custom_call_target="tpu_custom_call" | custom-call | tf_op jit(solution)/shard_map/unpack/pallas_call | solution.py:420
  (10 shorter events, 0.1 us)
Async XLA Ops:
  2.8 1.6 %collective-permute-start = (f32[4,10,8,128]{3,2,1,0:T(8,128)S(1)}, f32[4,10,8,128]{3,2,1,0:T(8,128)S(1)}, u32[]{:S(2)}, u32[]{:S(2)}) collective-permute-start(f32[4,10,8,128]{3,2,1,0:T(8,128)S(1)} %get-tuple-element.14), channel_id=1, source_target_pairs={{0,1},{1,0},{2,3},{3,2},{4,5},{5,4},{6,7},{7,6},{8,9},{9,8},{10,11... | collective-permute-start | bytes 491528 | tf_op jit(solution)/shard_map/ppermute | solution.py:281
  3.4 18.5 %copy-start = (s32[256]{0:T(256)S(1)}, s32[256]{0:T(256)}, u32[]{:S(2)}) copy-start(s32[256]{0:T(256)} %zone_ref.1) | copy-start | bytes 3076
  4.3 3.2 %collective-permute-start.3 = (f32[4,11,8,128]{3,2,1,0:T(8,128)S(1)}, f32[4,11,8,128]{3,2,1,0:T(8,128)S(1)}, u32[]{:S(2)}, u32[]{:S(2)}) collective-permute-start(f32[4,11,8,128]{3,2,1,0:T(8,128)S(1)} %get-tuple-element.20), channel_id=1, source_target_pairs={{0,1},{1,0},{2,3},{3,2},{4,5},{5,4},{6,7},{7,6},{8,9},{9,8},{10,11... | collective-permute-start | bytes 540680 | tf_op jit(solution)/shard_map/ppermute | solution.py:281
  4.4 5.9 %collective-permute-start.1 = (f32[2,10,8,128]{3,2,1,0:T(8,128)S(1)}, f32[2,10,8,128]{3,2,1,0:T(8,128)S(1)}, u32[]{:S(2)}, u32[]{:S(2)}) collective-permute-start(f32[2,10,8,128]{3,2,1,0:T(8,128)S(1)} %fusion.1), channel_id=1, source_target_pairs={{0,2},{1,3},{2,0},{3,1},{4,6},{5,7},{6,4},{7,5},{8,10},{9,11},{10,... | collective-permute-start | bytes 245768 | tf_op jit(solution)/shard_map/ppermute | solution.py:281
  7.5 5.8 %collective-permute-start.4 = (f32[2,11,8,128]{3,2,1,0:T(8,128)S(1)}, f32[2,11,8,128]{3,2,1,0:T(8,128)S(1)}, u32[]{:S(2)}, u32[]{:S(2)}) collective-permute-start(f32[2,11,8,128]{3,2,1,0:T(8,128)S(1)} %fusion), channel_id=1, source_target_pairs={{0,2},{1,3},{2,0},{3,1},{4,6},{5,7},{6,4},{7,5},{8,10},{9,11},{10,... | collective-permute-start | bytes 270344 | tf_op jit(solution)/shard_map/ppermute | solution.py:281
  10.4 4.9 %collective-permute-start.2 = (f32[1,10,8,128]{3,2,1,0:T(8,128)S(1)}, f32[1,10,8,128]{3,2,1,0:T(8,128)S(1)}, u32[]{:S(2)}, u32[]{:S(2)}) collective-permute-start(f32[1,10,8,128]{3,2,1,0:T(8,128)S(1)} %bitcast_add_fusion.4), channel_id=1, source_target_pairs={{0,4},{1,5},{2,6},{3,7},{4,0},{5,1},{6,2},{7,3},{8,12},{9,13},{10,... | collective-permute-start | bytes 122888 | tf_op jit(solution)/shard_map/ppermute | solution.py:281
  13.3 5.0 %collective-permute-start.5 = (f32[1,11,8,128]{3,2,1,0:T(8,128)S(1)}, f32[1,11,8,128]{3,2,1,0:T(8,128)S(1)}, u32[]{:S(2)}, u32[]{:S(2)}) collective-permute-start(f32[1,11,8,128]{3,2,1,0:T(8,128)S(1)} %bitcast_add_fusion.2), channel_id=1, source_target_pairs={{0,4},{1,5},{2,6},{3,7},{4,0},{5,1},{6,2},{7,3},{8,12},{9,13},{10,... | collective-permute-start | bytes 135176 | tf_op jit(solution)/shard_map/ppermute | solution.py:281
  18.3 4.6 %collective-permute-start.6 = (f32[21,8,128]{2,1,0:T(8,128)S(1)}, f32[21,8,128]{2,1,0:T(8,128)S(1)}, u32[]{:S(2)}, u32[]{:S(2)}) collective-permute-start(f32[21,8,128]{2,1,0:T(8,128)S(1)} %pad_maximum_fusion.refs_0_.refs_1_), channel_id=1, source_target_pairs={{0,8},{8,0},{16,24},{24,16},{1,9},{9,1},{17,25},{25,17},{2,10},{10... | collective-permute-start | bytes 258056 | tf_op jit(solution)/shard_map/ppermute | solution.py:281
  19.9 4.5 %collective-permute-start.7 = (f32[21,8,128]{2,1,0:T(8,128)S(1)}, f32[21,8,128]{2,1,0:T(8,128)S(1)}, u32[]{:S(2)}, u32[]{:S(2)}) collective-permute-start(f32[21,8,128]{2,1,0:T(8,128)S(1)} %pad_maximum_fusion.refs_0_.refs_1_), channel_id=1, source_target_pairs={{0,16},{8,24},{16,0},{24,8},{1,17},{9,25},{17,1},{25,9},{2,18},{10... | collective-permute-start | bytes 258056 | tf_op jit(solution)/shard_map/ppermute | solution.py:281
  21.4 5.4 %collective-permute-start.8 = (f32[21,8,128]{2,1,0:T(8,128)S(1)}, f32[21,8,128]{2,1,0:T(8,128)S(1)}, u32[]{:S(2)}, u32[]{:S(2)}) collective-permute-start(f32[21,8,128]{2,1,0:T(8,128)S(1)} %pad_maximum_fusion.refs_0_.refs_1_), channel_id=1, source_target_pairs={{0,24},{8,16},{16,8},{24,0},{1,25},{9,17},{17,9},{25,1},{2,26},{10... | collective-permute-start | bytes 258056 | tf_op jit(solution)/shard_map/ppermute | solution.py:281
  27.6 3.8 %collective-permute-start.10 = (f32[16,256]{1,0:T(8,128)S(1)}, f32[16,256]{1,0:T(8,128)S(1)}, u32[]{:S(2)}, u32[]{:S(2)}) collective-permute-start(f32[16,256]{1,0:T(8,128)S(1)} %share.1), channel_id=1, source_target_pairs={{0,2},{1,3},{2,0},{3,1},{4,6},{5,7},{6,4},{7,5},{8,10},{9,11},{10,... | collective-permute-start | bytes 49160 | tf_op jit(solution)/shard_map/ppermute | solution.py:281
  29.3 2.1 %collective-permute-start.11 = (f32[16,256]{1,0:T(8,128)S(1)}, f32[16,256]{1,0:T(8,128)S(1)}, u32[]{:S(2)}, u32[]{:S(2)}) collective-permute-start(f32[16,256]{1,0:T(8,128)S(1)} %share.1), channel_id=1, source_target_pairs={{0,1},{1,0},{2,3},{3,2},{4,5},{5,4},{6,7},{7,6},{8,9},{9,8},{10,11... | collective-permute-start | bytes 49160 | tf_op jit(solution)/shard_map/ppermute | solution.py:281
  29.3 3.2 %collective-permute-start.9 = (f32[16,256]{1,0:T(8,128)S(1)}, f32[16,256]{1,0:T(8,128)S(1)}, u32[]{:S(2)}, u32[]{:S(2)}) collective-permute-start(f32[16,256]{1,0:T(8,128)S(1)} %share.1), channel_id=1, source_target_pairs={{0,3},{1,2},{2,1},{3,0},{4,7},{5,6},{6,5},{7,4},{8,11},{9,10},{10,... | collective-permute-start | bytes 49160 | tf_op jit(solution)/shard_map/ppermute | solution.py:281
  32.5 4.6 %collective-permute-start.12 = (f32[16,256]{1,0:T(8,128)S(1)}, f32[16,256]{1,0:T(8,128)S(1)}, u32[]{:S(2)}, u32[]{:S(2)}) collective-permute-start(f32[16,256]{1,0:T(8,128)S(1)} %add_add_fusion.refs_0_), channel_id=1, source_target_pairs={{0,4},{1,5},{2,6},{3,7},{4,0},{5,1},{6,2},{7,3},{8,12},{9,13},{10,... | collective-permute-start | bytes 49160 | tf_op jit(solution)/shard_map/ppermute | solution.py:281
